TPU v7x, 128 devices: a whole 4x4x4 slice. The times are simulated.
128 devices in a mesh: local: 16 (over z, y), data: 8 (over x, core).
Axes of the slice: x: 4, y: 4, z: 4, core: 2. Of those that a mesh axis runs over, the one named last changes fastest.
Arguments:
- tokens: bfloat16 [2, 16384, 2048], P(None, ('local', 'data'))
- cotangent: bfloat16 [2, 16384, 2048], P(None, ('local', 'data'))
- w_up: bfloat16 [2, 2048, 5632], P(None, ('local', 'data'))
- w_down: bfloat16 [2, 5632, 2048], P(None, ('local', 'data'))
Outputs:
- output 1: bfloat16 [2, 16384, 2048], P(None, ('local', 'data'))
- output 2: bfloat16 [2, 16384, 2048], P(None, ('local', 'data'))
- output 3: float32 [2, 2048, 5632], P(None, ('local', 'data'))
- output 4: float32 [2, 5632, 2048], P(None, ('local', 'data'))
All inputs are finite; a program needn't handle non-finite values.
Results may differ from a plain program's by a relative error of at most 0.0133437.
Values are sent between devices in bfloat16 or wider.
A program may use at most 1 GiB of HBM per device.

v0:
```python
import jax
import jax.numpy as jnp
from jax import lax
from jax.sharding import PartitionSpec as P

NORM_EPS = 1e-6
ALL_AXES = ("local", "data")


def norm_f32(x_f32):
    return x_f32 * lax.rsqrt(jnp.mean(x_f32 * x_f32, axis=-1, keepdims=True) + NORM_EPS)


def gelu_f32(pre_f32):
    return jax.nn.gelu(pre_f32, approximate=True)


def layer_forward(x_in, up_mat, down_mat):
    x_f32 = x_in.astype(jnp.float32)
    normed = norm_f32(x_f32).astype(jnp.bfloat16)
    pre_act = jnp.dot(normed, up_mat, preferred_element_type=jnp.float32).astype(jnp.bfloat16)
    hidden = gelu_f32(pre_act.astype(jnp.float32)).astype(jnp.bfloat16)
    x_out = (x_f32 + jnp.dot(hidden, down_mat, preferred_element_type=jnp.float32)).astype(jnp.bfloat16)
    return x_out, normed, pre_act, hidden


def layer_backward(d_out, x_in, normed, pre_act, hidden, up_mat, down_mat):
    d_hidden = jnp.einsum("tm,fm->tf", d_out, down_mat, preferred_element_type=jnp.float32)
    gelu_pull = jax.vjp(gelu_f32, pre_act.astype(jnp.float32))[1]
    d_pre = gelu_pull(d_hidden)[0].astype(jnp.bfloat16)
    d_normed = jnp.einsum("tf,mf->tm", d_pre, up_mat, preferred_element_type=jnp.float32)
    norm_pull = jax.vjp(norm_f32, x_in.astype(jnp.float32))[1]
    d_in = (d_out.astype(jnp.float32) + norm_pull(d_normed)[0]).astype(jnp.bfloat16)
    grad_up = jnp.einsum("tm,tf->mf", normed, d_pre, preferred_element_type=jnp.float32)
    grad_down = jnp.einsum("tf,tm->fm", hidden, d_out, preferred_element_type=jnp.float32)
    return d_in, grad_up, grad_down


def solution(mesh):
    data_size = mesh.shape["data"]

    def body(tokens, cotangent, w_up, w_down):
        layers = w_up.shape[0]
        local_idx = lax.axis_index("local")
        keep_up = w_up.shape[1] * data_size
        keep_down = w_down.shape[1] * data_size
        total_up = [None] * layers
        total_down = [None] * layers
        outs_x = []
        outs_dx = []
        for micro_idx in range(tokens.shape[0]):
            x_cur = tokens[micro_idx]
            saved_acts = []
            for layer_idx in range(layers):
                full_up = lax.all_gather(w_up[layer_idx], ALL_AXES, axis=0, tiled=True)
                full_down = lax.all_gather(w_down[layer_idx], ALL_AXES, axis=0, tiled=True)
                kept_up = lax.dynamic_slice_in_dim(full_up, local_idx * keep_up, keep_up, axis=0)
                kept_down = lax.dynamic_slice_in_dim(full_down, local_idx * keep_down, keep_down, axis=0)
                x_next, normed, pre_act, hidden = layer_forward(x_cur, full_up, full_down)
                saved_acts.append((x_cur, normed, pre_act, hidden, kept_up, kept_down))
                x_cur = x_next
            outs_x.append(x_cur)
            d_cur = cotangent[micro_idx]
            for layer_idx in reversed(range(layers)):
                x_in, normed, pre_act, hidden, kept_up, kept_down = saved_acts[layer_idx]
                full_up = lax.all_gather(kept_up, "local", axis=0, tiled=True)
                full_down = lax.all_gather(kept_down, "local", axis=0, tiled=True)
                d_cur, grad_up, grad_down = layer_backward(d_cur, x_in, normed, pre_act, hidden, full_up, full_down)
                total_up[layer_idx] = grad_up if total_up[layer_idx] is None else total_up[layer_idx] + grad_up
                total_down[layer_idx] = grad_down if total_down[layer_idx] is None else total_down[layer_idx] + grad_down
            outs_dx.append(d_cur)
        shard_up = [lax.psum_scatter(total, ALL_AXES, scatter_dimension=0, tiled=True) for total in total_up]
        shard_down = [lax.psum_scatter(total, ALL_AXES, scatter_dimension=0, tiled=True) for total in total_down]
        return jnp.stack(outs_x), jnp.stack(outs_dx), jnp.stack(shard_up), jnp.stack(shard_down)

    row_spec = P(None, ALL_AXES, None)
    return jax.shard_map(body, mesh=mesh, in_specs=(row_spec, row_spec, row_spec, row_spec), out_specs=(row_spec, row_spec, row_spec, row_spec), check_vma=False)
```

profile of v0, /device:TPU:1, one launch (start us, length us, event | category | flops | bytes accessed | tf_op | source)
XLA Modules:
  0.0 2667.5 jit_solution(14924940784897350817)
XLA Ops:
  13.0 129.2 %all-gather.23.cloned.1.call-done = bf16[1,5632,2048]{2,0,1:T(2,128)(2,1)} async-done(((bf16[1,44,2048]{2,0,1:T(2,128)(2,1)}), bf16[1,5632,2048]{2,0,1:T(2,128)(2,1)}) %all-gather.23.cloned.1.call-update) | async-done | bytes 23068688 | tf_op jit(solution)/shard_map/all_gather | solution.py:56
  142.2 4.8 constant_dynamic-slice_fusion.3
  149.1 85.5 %all-gather.21.cloned.1.call-done = bf16[1,2048,5632]{2,1,0:T(8,128)(2,1)} async-done(((bf16[1,16,5632]{2,1,0:T(8,128)(2,1)}), bf16[1,2048,5632]{2,1,0:T(8,128)(2,1)}) %all-gather.21.cloned.1.call-update) | async-done | bytes 23068688 | tf_op jit(solution)/shard_map/all_gather | solution.py:55
  237.3 127.4 %all-gather.19.cloned.1.call-done = bf16[1,5632,2048]{2,0,1:T(2,128)(2,1)} async-done(((bf16[1,44,2048]{2,0,1:T(2,128)(2,1)}), bf16[1,5632,2048]{2,0,1:T(2,128)(2,1)}) %all-gather.19.cloned.1.call-update) | async-done | bytes 23068688 | tf_op jit(solution)/shard_map/all_gather | solution.py:56
  364.7 4.8 constant_dynamic-slice_fusion.1
  371.5 85.4 %all-gather.17.cloned.1.call-done = bf16[1,2048,5632]{2,1,0:T(8,128)(2,1)} async-done(((bf16[1,16,5632]{2,1,0:T(8,128)(2,1)}), bf16[1,2048,5632]{2,1,0:T(8,128)(2,1)}) %all-gather.17.cloned.1.call-update) | async-done | bytes 23068688 | tf_op jit(solution)/shard_map/all_gather | solution.py:55
  460.7 12.3 fusion.53
  473.0 20.4 multiply_reduce_fusion.2
  493.9 12.3 fusion.47
  506.3 20.8 multiply_reduce_fusion.3
  527.1 12.8 fusion.65
  539.8 12.4 fusion.59
  552.2 49.0 %all-gather.25.cloned.1.call-done = bf16[1,5632,2048]{2,1,0:T(8,128)(2,1)} async-done(((bf16[1,352,2048]{2,1,0:T(8,128)(2,1)}), bf16[1,5632,2048]{2,1,0:T(8,128)(2,1)}) %all-gather.25.cloned.1.call-update) | async-done | bytes 23068688 | tf_op jit(solution)/shard_map/all_gather | solution.py:67
  601.2 17.5 fusion.81
  618.7 16.8 fusion.95
  635.6 17.9 fusion.174
  653.5 28.8 %convolution_add_fusion.2 = f32[2048,5632]{1,0:T(8,128)} fusion(f32[2048,5632]{1,0:T(8,128)} %fusion.174, bf16[128,5632]{1,0:T(8,128)(2,1)S(1)} %fusion.95, f32[128,2048]{1,0:T(8,128)S(1)} %get-tuple-element.29, f32[128]{0:T(128)S(1)} %fusion.173), kind=kOutput, calls=%fused_computation.2 | convolution fusion | flops 2964848640 | bytes 94765568 | tf_op jit(solution)/shard_map/tm,tf->mf/dot_general | solution.py:34
  682.4 64.0 %all-gather.27.cloned.1.call-done = bf16[1,2048,5632]{2,1,0:T(8,128)(2,1)} async-done(((bf16[1,128,5632]{2,1,0:T(8,128)(2,1)}), bf16[1,2048,5632]{2,1,0:T(8,128)(2,1)}) %all-gather.27.cloned.1.call-update) | async-done | bytes 23068688 | tf_op jit(solution)/shard_map/all_gather | solution.py:66
  746.4 13.3 multiply_reduce_fusion.1
  759.7 13.1 multiply_reduce_fusion
  776.0 115.6 %all-gather.29.cloned.1.call-done = bf16[1,5632,2048]{2,1,0:T(8,128)(2,1)} async-done(((bf16[1,352,2048]{2,1,0:T(8,128)(2,1)}), bf16[1,5632,2048]{2,1,0:T(8,128)(2,1)}) %all-gather.29.cloned.1.call-update) | async-done | bytes 23068688 | tf_op jit(solution)/shard_map/all_gather | solution.py:67
  891.6 14.5 fusion.88
  906.1 14.3 fusion.74
  920.4 19.6 fusion.167
  940.0 28.9 %convolution_add_fusion.3 = f32[2048,5632]{1,0:T(8,128)} fusion(f32[2048,5632]{1,0:T(8,128)} %fusion.167, bf16[128,5632]{1,0:T(8,128)(2,1)S(1)} %copy-done.9, f32[128]{0:T(128)S(1)} %copy-done.32, bf16[2,128,2048]{2,1,0:T(8,128)(2,1)S(1)} %copy-done), kind=kOutput, calls=%fused_computation.3 | convolution fusion | flops 2965110784 | bytes 94241280 | tf_op jit(solution)/shard_map/tm,tf->mf/dot_general | solution.py:34
  969.0 19.4 fusion.158
  988.4 29.3 %convolution_add_fusion = f32[5632,2048]{1,0:T(8,128)} fusion(f32[5632,2048]{1,0:T(8,128)} %fusion.158, bf16[2,128,2048]{2,1,0:T(8,128)(2,1)} %param.5, f32[128,5632]{1,0:T(8,128)S(1)} %copy-done.7), kind=kOutput, calls=%fused_computation | convolution fusion | flops 2970812416 | bytes 95682560 | tf_op jit(solution)/shard_map/tf,tm->fm/dot_general | solution.py:35
  1017.7 454.1 %fusion.1 = f32[48,2048]{1,0:T(8,128)} fusion(f32[5632,2048]{1,0:T(8,128)} %convolution_add_fusion), kind=kCustom, calls=%all-reduce-scatter.1 | all-reduce-scatter fusion | flops 12582913 | bytes 46530560
  1483.4 32.5 %fusion.137 = bf16[1,128,2048]{2,1,0:T(8,128)(2,1)S(1)} fusion(f32[128,2048]{1,0:T(8,128)S(1)} %get-tuple-element.29, bf16[1,5632,2048]{2,0,1:T(2,128)(2,1)} %all-gather.23.cloned.1.call-done, f32[128,5632]{1,0:T(8,128)} %fusion.65), kind=kOutput, calls=%fused_computation.101 | convolution fusion | flops 2959802368 | bytes 27525120 | tf_op jit(solution)/shard_map/dot_general | solution.py:23
  1516.0 5.1 collective-permute-start.15
  1521.0 10.5 collective-permute-start.14
  1533.6 16.4 collective-permute-done.17
  1554.0 32.2 %fusion.134 = bf16[1,128,2048]{2,1,0:T(8,128)(2,1)S(1)} fusion(f32[128,2048]{1,0:T(8,128)S(1)} %copy-done.3, bf16[1,5632,2048]{2,0,1:T(2,128)(2,1)} %all-gather.23.cloned.1.call-done, f32[128,5632]{1,0:T(8,128)S(1)} %copy-done.4), kind=kOutput, calls=%fused_computation.100 | convolution fusion | flops 2959802368 | bytes 27525120 | tf_op jit(solution)/shard_map/dot_general | solution.py:23
  1587.4 31.1 %concatenate.1 = f32[556,2048]{1,0:T(8,128)} concatenate(f32[28,2048]{1,0:T(8,128)} %copy-done.27, f32[48,2048]{1,0:T(8,128)} %copy-done.22, f32[48,2048]{1,0:T(8,128)} %copy-done.23, f32[48,2048]{1,0:T(8,128)} %copy-done.24, f32[48,2048]{1,0:T(8,128)} %copy-done.25, f32[48,2048]{1,0:T(8,128)} %copy-done.26, f32[48,2048]{1,0:T(8,128)} %collective-permute-done.15, ...), dimensions={0} | concatenate | bytes 9109504
  1620.3 18.1 fusion.175
  1638.4 29.3 %convolution_add_fusion.1 = f32[5632,2048]{1,0:T(8,128)} fusion(f32[5632,2048]{1,0:T(8,128)} %fusion.175, bf16[128,2048]{1,0:T(8,128)(2,1)} %get-tuple-element.23, f32[128,5632]{1,0:T(8,128)S(1)} %copy-done.8), kind=kOutput, calls=%fused_computation.1 | convolution fusion | flops 2970812416 | bytes 95682560 | tf_op jit(solution)/shard_map/tf,tm->fm/dot_general | solution.py:35
  1667.7 500.6 %fusion = f32[48,2048]{1,0:T(8,128)} fusion(f32[5632,2048]{1,0:T(8,128)} %convolution_add_fusion.1), kind=kCustom, calls=%all-reduce-scatter | all-reduce-scatter fusion | flops 12582913 | bytes 46530560
  2178.3 12.6 collective-permute-start.10
  2190.9 11.9 fusion.10
  2202.9 6.9 collective-permute-start.5
  2209.8 13.2 fusion.150
  2227.6 5.5 collective-permute-start.3
  2238.5 10.4 collective-permute-start
  2251.8 5.0 collective-permute-done.2
  2256.8 11.8 collective-permute-done.1
  2268.6 8.9 collective-permute-done
  2277.5 30.8 %concatenate = f32[556,2048]{1,0:T(8,128)} concatenate(f32[28,2048]{1,0:T(8,128)} %collective-permute-done.10, f32[48,2048]{1,0:T(8,128)} %collective-permute-done.9, f32[48,2048]{1,0:T(8,128)} %collective-permute-done.8, f32[48,2048]{1,0:T(8,128)} %collective-permute-done.7, f32[48,2048]{1,0:T(8,128)} %collective-permute-done.6, f32[48,2048]{1,0:T(8,128)S(1)} %collective-permute-done.5, ...), dimensions={0} | concatenate | bytes 9109504
  2310.9 347.3 %reduce-scatter.7.cloned.1.call-done = f32[16,5632]{1,0:T(8,128)} async-done(((f32[2048,5632]{1,0:T(8,128)}), f32[16,5632]{1,0:T(8,128)}) %reduce-scatter.7.cloned.1.call-update) | async-done | bytes 360464 | tf_op jit(solution)/shard_map/reduce_scatter | solution.py:72
  (161 shorter events, 67.7 us)
Async XLA Ops:
  7.2 135.1 %all-gather.23.cloned.1.call-start = ((), (), s32[]{:S(2)}) async-start(), calls=%async_computation.7 | async-start | bytes 46497792 | tf_op jit(solution)/shard_map/all_gather | solution.py:56
  9.8 224.8 %all-gather.21.cloned.1.call-start = ((), (), s32[]{:S(2)}) async-start(), calls=%async_computation.6 | async-start | bytes 23248896 | tf_op jit(solution)/shard_map/all_gather | solution.py:55
  11.6 353.1 %all-gather.19.cloned.1.call-start = ((), (), s32[]{:S(2)}) async-start(), calls=%async_computation.5 | async-start | bytes 46497792 | tf_op jit(solution)/shard_map/all_gather | solution.py:56
  12.4 444.6 %all-gather.17.cloned.1.call-start = ((), (), s32[]{:S(2)}) async-start(), calls=%async_computation.4 | async-start | bytes 23248896 | tf_op jit(solution)/shard_map/all_gather | solution.py:55
  13.0 588.3 %all-gather.25.cloned.1.call-start = ((), (), s32[]{:S(2)}) async-start(), calls=%async_computation.8 | async-start | bytes 24510464 | tf_op jit(solution)/shard_map/all_gather | solution.py:67
  149.0 597.3 %all-gather.27.cloned.1.call-start = ((), (), s32[]{:S(2)}) async-start(), calls=%async_computation.9 | async-start | bytes 24510464 | tf_op jit(solution)/shard_map/all_gather | solution.py:66
  237.2 654.3 %all-gather.29.cloned.1.call-start = ((), (), s32[]{:S(2)}) async-start(), calls=%async_computation.10 | async-start | bytes 24510464 | tf_op jit(solution)/shard_map/all_gather | solution.py:67
  371.5 88.3 %copy-start = (bf16[2,128,2048]{2,1,0:T(8,128)(2,1)S(1)}, bf16[2,128,2048]{2,1,0:T(8,128)(2,1)}, u32[]{:S(2)}) copy-start(bf16[2,128,2048]{2,1,0:T(8,128)(2,1)} %param.4) | copy-start | bytes 3145732
  371.5 1819.4 %all-gather.31.cloned.1.call-start = ((), (), s32[]{:S(2)}) async-start(), calls=%async_computation.11 | async-start | bytes 24510464 | tf_op jit(solution)/shard_map/all_gather | solution.py:66
  459.5 1851.3 %reduce-scatter.9.cloned.1.call-start = ((), (), s32[]{:S(2)}) async-start(), calls=%async_computation.3 | async-start | bytes 46497792 | tf_op jit(solution)/shard_map/reduce_scatter | solution.py:72
  527.0 245.8 %copy-start.2 = (f32[128,2048]{1,0:T(8,128)}, f32[128,2048]{1,0:T(8,128)S(1)}, u32[]{:S(2)}) copy-start(f32[128,2048]{1,0:T(8,128)S(1)} %get-tuple-element.31) | copy-start | bytes 3145732
  682.3 1975.9 %reduce-scatter.7.cloned.1.call-start = ((), (), s32[]{:S(2)}) async-start(), calls=%async_computation.2 | async-start | bytes 46497792 | tf_op jit(solution)/shard_map/reduce_scatter | solution.py:72
  1472.8 6.9 collective-permute-start.21
  1474.1 79.8 %copy-start.3 = (f32[128,2048]{1,0:T(8,128)S(1)}, f32[128,2048]{1,0:T(8,128)}, u32[]{:S(2)}) copy-start(f32[128,2048]{1,0:T(8,128)} %copy-done.2) | copy-start | bytes 3145732
  1474.2 79.8 %copy-start.4 = (f32[128,5632]{1,0:T(8,128)S(1)}, f32[128,5632]{1,0:T(8,128)}, u32[]{:S(2)}) copy-start(f32[128,5632]{1,0:T(8,128)} %fusion.59) | copy-start | bytes 8650756
  1474.2 41.8 %collective-permute-start.20 = (f32[48,2048]{1,0:T(8,128)}, f32[48,2048]{1,0:T(8,128)S(1)}, u32[]{:S(2)}, u32[]{:S(2)}) collective-permute-start(f32[48,2048]{1,0:T(8,128)} %fusion.1), channel_id=1, source_target_pairs={{0,10},{1,11},{2,12},{3,13},{4,14},{5,15},{6,16},{7,17},{8,18},{9,... | collective-permute-start | bytes 1179656
  1475.7 45.3 %collective-permute-start.19 = (f32[48,2048]{1,0:T(8,128)}, f32[48,2048]{1,0:T(8,128)S(1)}, u32[]{:S(2)}, u32[]{:S(2)}) collective-permute-start(f32[48,2048]{1,0:T(8,128)} %fusion.1), channel_id=1, source_target_pairs={{0,9},{1,10},{2,11},{3,12},{4,13},{5,14},{6,15},{7,16},{8,17},{9,1... | collective-permute-start | bytes 1179656
  1477.1 54.4 %collective-permute-start.18 = (f32[48,2048]{1,0:T(8,128)}, f32[48,2048]{1,0:T(8,128)S(1)}, u32[]{:S(2)}, u32[]{:S(2)}) collective-permute-start(f32[48,2048]{1,0:T(8,128)} %fusion.1), channel_id=1, source_target_pairs={{0,8},{1,9},{2,10},{3,11},{4,12},{5,13},{6,14},{7,15},{8,16},{9,17... | collective-permute-start | bytes 1179656
  1478.4 71.6 %collective-permute-start.17 = (f32[48,2048]{1,0:T(8,128)}, f32[48,2048]{1,0:T(8,128)S(1)}, u32[]{:S(2)}, u32[]{:S(2)}) collective-permute-start(f32[48,2048]{1,0:T(8,128)} %fusion.1), channel_id=1, source_target_pairs={{0,7},{1,8},{2,9},{3,10},{4,11},{5,12},{6,13},{7,14},{8,15},{9,16}... | collective-permute-start | bytes 1179656
  1479.7 36.2 %copy-start.27 = (f32[28,2048]{1,0:T(8,128)}, f32[28,2048]{1,0:T(8,128)S(1)}, u32[]{:S(2)}) copy-start(f32[28,2048]{1,0:T(8,128)S(1)} %collective-permute-done.21) | copy-start | bytes 688132
  1479.7 72.3 %collective-permute-start.16 = (f32[48,2048]{1,0:T(8,128)}, f32[48,2048]{1,0:T(8,128)S(1)}, u32[]{:S(2)}, u32[]{:S(2)}) collective-permute-start(f32[48,2048]{1,0:T(8,128)} %fusion.1), channel_id=1, source_target_pairs={{0,6},{1,7},{2,8},{3,9},{4,10},{5,11},{6,12},{7,13},{8,14},{9,15},... | collective-permute-start | bytes 1179656
  1515.9 36.1 %copy-start.22 = (f32[48,2048]{1,0:T(8,128)}, f32[48,2048]{1,0:T(8,128)S(1)}, u32[]{:S(2)}) copy-start(f32[48,2048]{1,0:T(8,128)S(1)} %collective-permute-done.20) | copy-start | bytes 1179652
  1516.0 71.4 %collective-permute-start.15 = (f32[48,2048]{1,0:T(8,128)}, f32[48,2048]{1,0:T(8,128)}, u32[]{:S(2)}, u32[]{:S(2)}) collective-permute-start(f32[48,2048]{1,0:T(8,128)} %fusion.1), channel_id=1, source_target_pairs={{0,5},{1,6},{2,7},{3,8},{4,9},{5,10},{6,11},{7,12},{8,13},{9,14},{... | collective-permute-start | bytes 1179656
  1521.0 66.3 %collective-permute-start.14 = (f32[48,2048]{1,0:T(8,128)}, f32[48,2048]{1,0:T(8,128)}, u32[]{:S(2)}, u32[]{:S(2)}) collective-permute-start(f32[48,2048]{1,0:T(8,128)} %fusion.1), channel_id=1, source_target_pairs={{0,4},{1,5},{2,6},{3,7},{4,8},{5,9},{6,10},{7,11},{8,12},{9,13},{1... | collective-permute-start | bytes 1179656
  1531.5 54.8 %copy-start.24 = (f32[48,2048]{1,0:T(8,128)}, f32[48,2048]{1,0:T(8,128)S(1)}, u32[]{:S(2)}) copy-start(f32[48,2048]{1,0:T(8,128)S(1)} %collective-permute-done.18) | copy-start | bytes 1179652
  1531.5 55.9 %collective-permute-start.13 = (f32[48,2048]{1,0:T(8,128)}, f32[48,2048]{1,0:T(8,128)}, u32[]{:S(2)}, u32[]{:S(2)}) collective-permute-start(f32[48,2048]{1,0:T(8,128)} %fusion.1), channel_id=1, source_target_pairs={{0,3},{1,4},{2,5},{3,6},{4,7},{5,8},{6,9},{7,10},{8,11},{9,12},{10... | collective-permute-start | bytes 1179656
  1550.0 36.3 %copy-start.25 = (f32[48,2048]{1,0:T(8,128)}, f32[48,2048]{1,0:T(8,128)S(1)}, u32[]{:S(2)}) copy-start(f32[48,2048]{1,0:T(8,128)S(1)} %collective-permute-done.17) | copy-start | bytes 1179652
  1550.0 37.4 %collective-permute-start.12 = (f32[48,2048]{1,0:T(8,128)}, f32[48,2048]{1,0:T(8,128)}, u32[]{:S(2)}, u32[]{:S(2)}) collective-permute-start(f32[48,2048]{1,0:T(8,128)} %fusion.1), channel_id=1, source_target_pairs={{0,2},{1,3},{2,4},{3,5},{4,6},{5,7},{6,8},{7,9},{8,10},{9,11},{10,... | collective-permute-start | bytes 1179656
  1552.0 34.2 %copy-start.26 = (f32[48,2048]{1,0:T(8,128)}, f32[48,2048]{1,0:T(8,128)S(1)}, u32[]{:S(2)}) copy-start(f32[48,2048]{1,0:T(8,128)S(1)} %collective-permute-done.16) | copy-start | bytes 1179652
  1552.0 35.3 %collective-permute-start.11 = (f32[48,2048]{1,0:T(8,128)}, f32[48,2048]{1,0:T(8,128)}, u32[]{:S(2)}, u32[]{:S(2)}) collective-permute-start(f32[48,2048]{1,0:T(8,128)} %fusion.1), channel_id=1, source_target_pairs={{0,1},{1,2},{2,3},{3,4},{4,5},{5,6},{6,7},{7,8},{8,9},{9,10},{10,1... | collective-permute-start | bytes 1179656
  1667.7 523.2 %copy-start.10 = (bf16[128,5632]{1,0:T(8,128)(2,1)S(1)}, bf16[128,5632]{1,0:T(8,128)(2,1)}, u32[]{:S(2)}) copy-start(bf16[128,5632]{1,0:T(8,128)(2,1)} %fusion.88) | copy-start | bytes 4325380
  2169.9 39.9 %copy-start.1 = (bf16[2,128,2048]{2,1,0:T(8,128)(2,1)S(1)}, bf16[2,128,2048]{2,1,0:T(8,128)(2,1)}, u32[]{:S(2)}) copy-start(bf16[2,128,2048]{2,1,0:T(8,128)(2,1)} %param.4) | copy-start | bytes 3145732
  2169.9 53.2 %collective-permute-start.9 = (f32[48,2048]{1,0:T(8,128)}, f32[48,2048]{1,0:T(8,128)}, u32[]{:S(2)}, u32[]{:S(2)}) collective-permute-start(f32[48,2048]{1,0:T(8,128)} %fusion), channel_id=1, source_target_pairs={{0,10},{1,11},{2,12},{3,13},{4,14},{5,15},{6,16},{7,17},{8,18},{9,... | collective-permute-start | bytes 1179656
  2172.1 55.5 %collective-permute-start.8 = (f32[48,2048]{1,0:T(8,128)}, f32[48,2048]{1,0:T(8,128)}, u32[]{:S(2)}, u32[]{:S(2)}) collective-permute-start(f32[48,2048]{1,0:T(8,128)} %fusion), channel_id=1, source_target_pairs={{0,9},{1,10},{2,11},{3,12},{4,13},{5,14},{6,15},{7,16},{8,17},{9,1... | collective-permute-start | bytes 1179656
  2174.2 58.9 %collective-permute-start.7 = (f32[48,2048]{1,0:T(8,128)}, f32[48,2048]{1,0:T(8,128)}, u32[]{:S(2)}, u32[]{:S(2)}) collective-permute-start(f32[48,2048]{1,0:T(8,128)} %fusion), channel_id=1, source_target_pairs={{0,8},{1,9},{2,10},{3,11},{4,12},{5,13},{6,14},{7,15},{8,16},{9,17... | collective-permute-start | bytes 1179656
  2176.3 58.9 %collective-permute-start.6 = (f32[48,2048]{1,0:T(8,128)}, f32[48,2048]{1,0:T(8,128)}, u32[]{:S(2)}, u32[]{:S(2)}) collective-permute-start(f32[48,2048]{1,0:T(8,128)} %fusion), channel_id=1, source_target_pairs={{0,7},{1,8},{2,9},{3,10},{4,11},{5,12},{6,13},{7,14},{8,15},{9,16}... | collective-permute-start | bytes 1179656
  2178.3 24.6 collective-permute-start.10
  2202.8 46.1 %copy-start.17 = (bf16[128,2048]{1,0:T(8,128)(2,1)S(1)}, bf16[128,2048]{1,0:T(8,128)(2,1)}, u32[]{:S(2)}) copy-start(bf16[128,2048]{1,0:T(8,128)(2,1)} %get-tuple-element.22) | copy-start | bytes 1572868
  2202.8 46.1 %copy-start.18 = (bf16[128,2048]{1,0:T(8,128)(2,1)S(1)}, bf16[128,2048]{1,0:T(8,128)(2,1)}, u32[]{:S(2)}) copy-start(bf16[128,2048]{1,0:T(8,128)(2,1)} %get-tuple-element.23) | copy-start | bytes 1572868
  2202.8 46.1 %copy-start.30 = (f32[128]{0:T(128)S(1)}, f32[128]{0:T(128)}, u32[]{:S(2)}) copy-start(f32[128]{0:T(128)} %copy-done.28) | copy-start | bytes 1540
  2202.9 46.1 %copy-start.33 = (f32[128]{0:T(128)S(1)}, f32[128]{0:T(128)}, u32[]{:S(2)}) copy-start(f32[128]{0:T(128)} %copy-done.31) | copy-start | bytes 1540
  2202.9 35.6 %collective-permute-start.5 = (f32[48,2048]{1,0:T(8,128)}, f32[48,2048]{1,0:T(8,128)S(1)}, u32[]{:S(2)}, u32[]{:S(2)}) collective-permute-start(f32[48,2048]{1,0:T(8,128)} %fusion), channel_id=1, source_target_pairs={{0,6},{1,7},{2,8},{3,9},{4,10},{5,11},{6,12},{7,13},{8,14},{9,15},... | collective-permute-start | bytes 1179656
  2223.1 28.7 %collective-permute-start.4 = (f32[48,2048]{1,0:T(8,128)}, f32[48,2048]{1,0:T(8,128)}, u32[]{:S(2)}, u32[]{:S(2)}) collective-permute-start(f32[48,2048]{1,0:T(8,128)} %fusion), channel_id=1, source_target_pairs={{0,5},{1,6},{2,7},{3,8},{4,9},{5,10},{6,11},{7,12},{8,13},{9,14},{... | collective-permute-start | bytes 1179656
  2227.6 24.2 collective-permute-start.3
  2233.1 23.7 collective-permute-start.2
  2235.2 33.4 %collective-permute-start.1 = (f32[48,2048]{1,0:T(8,128)}, f32[48,2048]{1,0:T(8,128)}, u32[]{:S(2)}, u32[]{:S(2)}) collective-permute-start(f32[48,2048]{1,0:T(8,128)} %fusion), channel_id=1, source_target_pairs={{0,2},{1,3},{2,4},{3,5},{4,6},{5,7},{6,8},{7,9},{8,10},{9,11},{10,... | collective-permute-start | bytes 1179656
  2238.5 39.0 %collective-permute-start = (f32[48,2048]{1,0:T(8,128)}, f32[48,2048]{1,0:T(8,128)}, u32[]{:S(2)}, u32[]{:S(2)}) collective-permute-start(f32[48,2048]{1,0:T(8,128)} %fusion), channel_id=1, source_target_pairs={{0,1},{1,2},{2,3},{3,4},{4,5},{5,6},{6,7},{7,8},{8,9},{9,10},{10,1... | collective-permute-start | bytes 1179656
  2251.8 57.6 %copy-start.21 = (f32[1,44,2048]{2,1,0:T(8,128)S(1)}, f32[1,44,2048]{2,1,0:T(8,128)}, u32[]{:S(2)}) copy-start(f32[1,44,2048]{2,1,0:T(8,128)} %dynamic-slice_bitcast_fusion) | copy-start | bytes 1081348
  (24 other events, 406.4 us)
Sparse Core Ops, SparseCore 0:
  11.5 130.6 all-gather.22
  145.8 88.8 all-gather.20
  238.2 126.4 all-gather.18
  368.1 88.8 all-gather.16
  459.0 142.2 all-gather.24
  603.2 143.1 all-gather.26
  748.5 143.0 all-gather.28
  893.7 206.4 all-gather.30
  1102.6 809.4 reduce-scatter.8
  1914.4 743.7 reduce-scatter.6
where the time goes:
time: 2680 us; the launch traced here: 2670 us
  waiting for transfers between devices  1050 us (39%)
  blocking collectives  955 us (36%)
  matrix products  462 us (17%)
  local copies, waits for them, and re-layouts  93.1 us (3%)
  starting transfers between devices  86.4 us (3%)
    unnamed x2, blocking collectives  955 us
    reduce_scatter x2, waiting for transfers between devices, body(): lax.psum_scatter(total, ALL_AXES, scatter_dimension=0, tiled=True)  347 us
    all_gather x2, waiting for transfers between devices, body(): full_down = lax.all_gather(w_down[layer_idx], ALL_AXES, axis=0, tiled=True)  257 us
    all_gather x2, waiting for transfers between devices, body(): full_up = lax.all_gather(w_up[layer_idx], ALL_AXES, axis=0, tiled=True)  171 us
    all_gather x2, waiting for transfers between devices, body(): full_down = lax.all_gather(kept_down, 'local', axis=0, tiled=True)  165 us
    dot_general x4, matrix products, layer_forward(): jnp.dot(hidden, down_mat, preferred_element_type=jnp.float32)  106 us
    dot_general x4, matrix products, layer_backward(): jnp.einsum('tf,tm->fm', hidden, d_out, preferred_element_type=jnp.float32)  96.1 us
    dot_general x4, matrix products, layer_backward(): jnp.einsum('tm,tf->mf', normed, d_pre, preferred_element_type=jnp.float32)  95.2 us
  transfers between devices with their start and end apart: 32, of which 12 were waited for; matrix products, arithmetic and copies ran while one was open for 57% of the time, Pallas kernels for 0%

commit v1 on v0

v1 whole, which is shorter than its diff:
```python
import jax
import jax.numpy as jnp
from jax import lax
from jax.sharding import PartitionSpec as P

NORM_EPS = 1e-6
ALL_AXES = ("local", "data")
PAD = 48


def norm_f32(x_f32):
    return x_f32 * lax.rsqrt(jnp.mean(x_f32 * x_f32, axis=-1, keepdims=True) + NORM_EPS)


def gelu_f32(pre_f32):
    return jax.nn.gelu(pre_f32, approximate=True)


def solution(mesh):
    n_data = mesh.shape["data"]
    n_local = mesh.shape["local"]

    def body(tokens, cotangent, w_up, w_down):
        micro, rows, hidden = tokens.shape
        layers, up_rows, ffn = w_up.shape
        down_rows = w_down.shape[1]
        pad = PAD - down_rows
        width = n_local * PAD

        up = w_up.reshape(layers, up_rows, n_local, n_data, down_rows)
        up = jnp.pad(up, ((0, 0),) * 4 + ((0, pad),))
        up = up.transpose(3, 0, 1, 2, 4).reshape(n_data, layers, up_rows, width)
        up = lax.all_to_all(up, "data", 0, 0)
        up = up.transpose(1, 0, 2, 3).reshape(layers, n_data * up_rows, width)
        down = jnp.pad(w_down, ((0, 0), (0, pad), (0, 0)))

        def gather_weights(layer, after=None):
            u, d = up[layer], down[layer]
            if after is not None:
                u, d, _ = lax.optimization_barrier((u, d, after))
            return (lax.all_gather(u, "local", axis=0, tiled=True),
                    lax.all_gather(d, "local", axis=0, tiled=True))

        x_cur = tokens.reshape(micro * rows, hidden)
        saved = []
        for layer in range(layers):
            w1, w2 = gather_weights(layer)
            x_f32 = x_cur.astype(jnp.float32)
            normed = norm_f32(x_f32).astype(jnp.bfloat16)
            u_all = lax.all_gather(normed, "data", axis=0, tiled=True)
            pre = jnp.dot(u_all, w1, preferred_element_type=jnp.float32).astype(jnp.bfloat16)
            act = gelu_f32(pre.astype(jnp.float32)).astype(jnp.bfloat16)
            part = jnp.dot(act, w2, preferred_element_type=jnp.float32)
            y = lax.psum_scatter(part, "data", scatter_dimension=0, tiled=True)
            saved.append((x_cur, u_all, pre, act))
            x_cur = (x_f32 + y).astype(jnp.bfloat16)
        x_final = x_cur

        d_cur = cotangent.reshape(micro * rows, hidden)
        grads_up = [None] * layers
        grads_down = [None] * layers
        after = part
        for layer in reversed(range(layers)):
            x_in, u_all, pre, act = saved[layer]
            w1, w2 = gather_weights(layer, after)
            c_all = lax.all_gather(d_cur, "data", axis=0, tiled=True)
            e = jnp.einsum("tm,fm->tf", c_all, w2, preferred_element_type=jnp.float32)
            z = jax.vjp(gelu_f32, pre.astype(jnp.float32))[1](e)[0].astype(jnp.bfloat16)
            part = jnp.einsum("tf,mf->tm", z, w1, preferred_element_type=jnp.float32)
            v = lax.psum_scatter(part, "data", scatter_dimension=0, tiled=True)
            d_w1 = jnp.einsum("tm,tf->mf", u_all, z, preferred_element_type=jnp.float32)
            d_w2 = jnp.einsum("tf,tm->fm", act, c_all, preferred_element_type=jnp.float32)
            grads_up[layer] = lax.psum_scatter(d_w1, "local", scatter_dimension=0, tiled=True)
            grads_down[layer] = lax.psum_scatter(d_w2, "local", scatter_dimension=0, tiled=True)[:down_rows]
            norm_pull = jax.vjp(norm_f32, x_in.astype(jnp.float32))[1]
            d_cur = (d_cur.astype(jnp.float32) + norm_pull(v)[0]).astype(jnp.bfloat16)
            after = z
        g_up = jnp.stack(grads_up).reshape(layers, n_data, up_rows, width).transpose(1, 0, 2, 3)
        g_up = lax.all_to_all(g_up, "data", 0, 0)
        g_up = g_up.reshape(n_data, layers, up_rows, n_local, PAD)[..., :down_rows]
        g_up = g_up.transpose(1, 2, 3, 0, 4).reshape(layers, up_rows, ffn)
        shape = (micro, rows, hidden)
        return x_final.reshape(shape), d_cur.reshape(shape), g_up, jnp.stack(grads_down)

    spec = P(None, ALL_AXES, None)
    return jax.shard_map(body, mesh=mesh, in_specs=(spec,) * 4, out_specs=(spec,) * 4, check_vma=False)
```

time: 2680 us -> 1380 us (0.51)
  blocking collectives: 955 us -> 13.6 us
  matrix products: 462 us -> 148 us
  waiting for transfers between devices: 1050 us -> 1140 us
  starting transfers between devices: 86.4 us -> 8.8 us
  local copies, waits for them, and re-layouts: 93.1 us -> 24.8 us
    unnamed x2 -> x0, blocking collectives: 955 us -> none
    reduce_scatter x2 -> x8, waiting for transfers between devices: 347 us -> 670 us  [the longest x2 183 us: body(): y = lax.psum_scatter(part, 'data', scatter_dimension=0, tiled=True)]
    dot_general x24 -> x12, matrix products: 462 us -> 148 us  [the longest x2 28 us: body(): e = jnp.einsum('tm,fm->tf', c_all, w2, preferred_element_type=jnp.float32)]
    all_gather x8 -> x12, waiting for transfers between devices: 656 us -> 468 us  [the longest x4 142 us: gather_weights(): lax.all_gather(d, 'local', axis=0, tiled=True)]
    unnamed x22 -> x0, starting transfers between devices: 85.8 us -> none
    unnamed x87 -> x28, local copies, waits for them, and re-layouts: 71.2 us -> 5.02 us
    unnamed x32 -> x20, waiting for transfers between devices: 43.5 us -> 4.42 us
  transfers between devices with their start and end apart: 32 -> 21, of which waited for: 12 -> 20; matrix products, arithmetic and copies ran while one was open for 57% -> 11% of each run, Pallas kernels for 0% -> 0%
where the time goes in v1:
time: 1380 us; the launch traced here: 1370 us
  waiting for transfers between devices  1140 us (83%)
  matrix products  148 us (11%)
  local copies, waits for them, and re-layouts  24.8 us (2%)
  other arithmetic  18 us (1%)
  between operations  15 us (1%)
    reduce_scatter x2, waiting for transfers between devices, body(): y = lax.psum_scatter(part, 'data', scatter_dimension=0, tiled=True)  183 us
    reduce_scatter x2, waiting for transfers between devices, body(): v = lax.psum_scatter(part, 'data', scatter_dimension=0, tiled=True)  172 us
    reduce_scatter x2, waiting for transfers between devices, body(): lax.psum_scatter(d_w1, 'local', scatter_dimension=0, tiled=True)  168 us
    reduce_scatter x2, waiting for transfers between devices, body(): lax.psum_scatter(d_w2, 'local', scatter_dimension=0, tiled=True)[:down_rows]  147 us
    all_gather x4, waiting for transfers between devices, gather_weights(): lax.all_gather(d, 'local', axis=0, tiled=True)  142 us
    all_gather x4, waiting for transfers between devices, gather_weights(): lax.all_gather(u, 'local', axis=0, tiled=True)  132 us
    all_gather x2, waiting for transfers between devices, body(): u_all = lax.all_gather(normed, 'data', axis=0, tiled=True)  105 us
    all_gather x2, waiting for transfers between devices, body(): c_all = lax.all_gather(d_cur, 'data', axis=0, tiled=True)  90.3 us
  transfers between devices with their start and end apart: 21, of which 20 were waited for; matrix products, arithmetic and copies ran while one was open for 11% of the time, Pallas kernels for 0%

profile of v1, /device:TPU:1, one launch (start us, length us, event | category | flops | bytes accessed | tf_op | source)
XLA Modules:
  0.0 1370.5 jit_solution(15294624619523538752)
XLA Ops:
  7.2 4.1 reshape.82
  13.0 13.6 all_to_all.10
  30.2 44.4 %all-gather.17.cloned.1.call-done = bf16[2048,768]{1,0:T(8,128)(2,1)} async-done(((bf16[128,768]{1,0:T(8,128)(2,1)}), bf16[2048,768]{1,0:T(8,128)(2,1)}) %all-gather.17.cloned.1.call-update) | async-done | bytes 3145744 | tf_op jit(solution)/shard_map/all_gather | solution.py:41
  74.6 52.4 %all-gather.15.cloned.1.call-done = bf16[2048,2048]{1,0:T(8,128)(2,1)} async-done(((bf16[256,2048]{1,0:T(8,128)(2,1)}), bf16[2048,2048]{1,0:T(8,128)(2,1)}) %all-gather.15.cloned.1.call-update) | async-done | bytes 8388624 | tf_op jit(solution)/shard_map/all_gather | solution.py:50
  127.0 11.1 convolution_convert_fusion.1
  138.2 37.2 %all-gather.35.cloned.1.call-done = bf16[1,768,2048]{2,1,0:T(8,128)(2,1)} async-done(((bf16[1,48,2048]{2,1,0:T(8,128)(2,1)}), bf16[1,768,2048]{2,1,0:T(8,128)(2,1)}) %all-gather.35.cloned.1.call-update) | async-done | bytes 3145744 | tf_op jit(solution)/shard_map/all_gather | solution.py:42
  175.4 13.1 fusion.23
  189.1 91.0 %reduce-scatter.9.cloned.1.call-done = f32[256,2048]{1,0:T(8,128)} async-done(((f32[2048,2048]{1,0:T(8,128)}), f32[256,2048]{1,0:T(8,128)}) %reduce-scatter.9.cloned.1.call-update) | async-done | bytes 2097168 | tf_op jit(solution)/shard_map/reduce_scatter | solution.py:54
  280.2 2.0 fusion.29
  285.4 43.3 %all-gather.21.cloned.1.call-done = bf16[2048,768]{1,0:T(8,128)(2,1)} async-done(((bf16[128,768]{1,0:T(8,128)(2,1)}), bf16[2048,768]{1,0:T(8,128)(2,1)}) %all-gather.21.cloned.1.call-update) | async-done | bytes 3145744 | tf_op jit(solution)/shard_map/all_gather | solution.py:41
  328.7 52.2 %all-gather.19.cloned.1.call-done = bf16[2048,2048]{1,0:T(8,128)(2,1)} async-done(((bf16[256,2048]{1,0:T(8,128)(2,1)}), bf16[2048,2048]{1,0:T(8,128)(2,1)}) %all-gather.19.cloned.1.call-update) | async-done | bytes 8388624 | tf_op jit(solution)/shard_map/all_gather | solution.py:50
  380.9 11.2 convolution_convert_fusion
  392.1 37.8 %all-gather.37.cloned.1.call-done = bf16[1,768,2048]{2,1,0:T(8,128)(2,1)} async-done(((bf16[1,48,2048]{2,1,0:T(8,128)(2,1)}), bf16[1,768,2048]{2,1,0:T(8,128)(2,1)}) %all-gather.37.cloned.1.call-update) | async-done | bytes 3145744 | tf_op jit(solution)/shard_map/all_gather | solution.py:42
  429.8 13.1 fusion.21
  443.6 38.1 %all-gather.25.cloned.1.call-done = bf16[2048,2048]{1,0:T(8,128)(2,1)} async-done(((bf16[256,2048]{1,0:T(8,128)(2,1)}), bf16[2048,2048]{1,0:T(8,128)(2,1)}) %all-gather.25.cloned.1.call-update) | async-done | bytes 8388624 | tf_op jit(solution)/shard_map/all_gather | solution.py:66
  481.6 48.9 %all-gather.23.cloned.1.call-done = bf16[768,2048]{1,0:T(8,128)(2,1)} async-done(((bf16[48,2048]{1,0:T(8,128)(2,1)}), bf16[768,2048]{1,0:T(8,128)(2,1)}) %all-gather.23.cloned.1.call-update) | async-done | bytes 3145744 | tf_op jit(solution)/shard_map/all_gather | solution.py:42
  530.6 14.8 %fusion.4 = bf16[2048,768]{1,0:T(8,128)(2,1)} fusion(bf16[2048,768]{1,0:T(8,128)(2,1)} %convolution_convert_fusion, bf16[768,2048]{1,0:T(8,128)(2,1)} %all-gather.23.cloned.1.call-done, bf16[2048,2048]{1,0:T(8,128)(2,1)} %all-gather.25.cloned.1.call-done), kind=kOutput, calls=%fused_computation.14 | convolution fusion | flops 6475481088 | bytes 17825792 | tf_op jit(solution)/shard_map/tm,fm->tf/dot_general | solution.py:67
  545.4 33.7 %all-gather.27.cloned.1.call-done = bf16[2048,768]{1,0:T(8,128)(2,1)} async-done(((bf16[128,768]{1,0:T(8,128)(2,1)}), bf16[2048,768]{1,0:T(8,128)(2,1)}) %all-gather.27.cloned.1.call-update) | async-done | bytes 3145744 | tf_op jit(solution)/shard_map/all_gather | solution.py:41
  579.1 12.5 fusion.48
  593.1 90.3 %reduce-scatter.13.cloned.1.call-done = f32[256,2048]{1,0:T(8,128)} async-done(((f32[2048,2048]{1,0:T(8,128)}), f32[256,2048]{1,0:T(8,128)}) %reduce-scatter.13.cloned.1.call-update) | async-done | bytes 2097168 | tf_op jit(solution)/shard_map/reduce_scatter | solution.py:70
  683.3 1.9 fusion.32
  685.2 92.0 %reduce-scatter.11.cloned.1.call-done = f32[256,2048]{1,0:T(8,128)} async-done(((f32[2048,2048]{1,0:T(8,128)}), f32[256,2048]{1,0:T(8,128)}) %reduce-scatter.11.cloned.1.call-update) | async-done | bytes 2097168 | tf_op jit(solution)/shard_map/reduce_scatter | solution.py:54
  777.2 4.2 fusion.26
  782.3 13.2 fusion.40
  795.5 1.8 copy-done.10
  797.3 10.9 fusion.51
  808.5 17.9 %all-gather.31.cloned.1.call-done = bf16[768,2048]{1,0:T(8,128)(2,1)} async-done(((bf16[48,2048]{1,0:T(8,128)(2,1)}), bf16[768,2048]{1,0:T(8,128)(2,1)}) %all-gather.31.cloned.1.call-update) | async-done | bytes 3145744 | tf_op jit(solution)/shard_map/all_gather | solution.py:42
  826.4 52.2 %all-gather.29.cloned.1.call-done = bf16[2048,2048]{1,0:T(8,128)(2,1)} async-done(((bf16[256,2048]{1,0:T(8,128)(2,1)}), bf16[2048,2048]{1,0:T(8,128)(2,1)}) %all-gather.29.cloned.1.call-update) | async-done | bytes 8388624 | tf_op jit(solution)/shard_map/all_gather | solution.py:66
  878.7 13.2 fusion.7
  891.8 1.6 copy-done.11
  893.5 11.0 fusion.50
  904.5 12.2 fusion.43
  917.1 10.1 all-gather.33.cloned.1.call-done
  927.2 11.4 fusion.49
  938.6 71.5 %reduce-scatter.23.cloned.1.call-done = f32[48,2048]{1,0:T(8,128)} async-done(((f32[768,2048]{1,0:T(8,128)}), f32[48,2048]{1,0:T(8,128)}) %reduce-scatter.23.cloned.1.call-update) | async-done | bytes 393232 | tf_op jit(solution)/shard_map/reduce_scatter | solution.py:74
  1011.1 83.3 %reduce-scatter.19.cloned.1.call-done = f32[128,768]{1,0:T(8,128)} async-done(((f32[2048,768]{1,0:T(8,128)}), f32[128,768]{1,0:T(8,128)}) %reduce-scatter.19.cloned.1.call-update) | async-done | bytes 393232 | tf_op jit(solution)/shard_map/reduce_scatter | solution.py:73
  1094.4 84.3 %reduce-scatter.17.cloned.1.call-done = f32[128,768]{1,0:T(8,128)} async-done(((f32[2048,768]{1,0:T(8,128)}), f32[128,768]{1,0:T(8,128)}) %reduce-scatter.17.cloned.1.call-update) | async-done | bytes 393232 | tf_op jit(solution)/shard_map/reduce_scatter | solution.py:73
  1178.7 2.1 maximum_bitcast_fusion
  1180.8 6.9 all-to-all-start.1
  1187.7 75.6 %reduce-scatter.21.cloned.1.call-done = f32[48,2048]{1,0:T(8,128)} async-done(((f32[768,2048]{1,0:T(8,128)}), f32[48,2048]{1,0:T(8,128)}) %reduce-scatter.21.cloned.1.call-update) | async-done | bytes 393232 | tf_op jit(solution)/shard_map/reduce_scatter | solution.py:74
  1264.3 1.4 copy.22
  1265.7 2.4 reshape.87
  1268.1 1.9 slice_bitcast_fusion
  1270.0 2.6 copy.21
  1272.6 3.5 reshape.88
  1276.1 82.1 %reduce-scatter.15.cloned.1.call-done = f32[256,2048]{1,0:T(8,128)} async-done(((f32[2048,2048]{1,0:T(8,128)}), f32[256,2048]{1,0:T(8,128)}) %reduce-scatter.15.cloned.1.call-update) | async-done | bytes 2097168 | tf_op jit(solution)/shard_map/reduce_scatter | solution.py:70
  1358.2 1.9 fusion.36
  1360.1 3.1 fusion.28
  (81 shorter events, 14.7 us)
Async XLA Ops:
  7.2 20.4 %copy-start = (bf16[2,128,2048]{2,1,0:T(8,128)(2,1)S(1)}, bf16[2,128,2048]{2,1,0:T(8,128)(2,1)}, u32[]{:S(2)}) copy-start(bf16[2,128,2048]{2,1,0:T(8,128)(2,1)} %param.4) | copy-start | bytes 3145732
  7.2 21.9 %copy-start.4 = (bf16[2,44,2048]{2,0,1:T(2,128)(2,1)S(1)}, bf16[2,44,2048]{2,0,1:T(2,128)(2,1)}, u32[]{:S(2)}) copy-start(bf16[2,44,2048]{2,0,1:T(2,128)(2,1)} %param.7) | copy-start | bytes 1081348
  7.2 67.5 %all-gather.17.cloned.1.call-start = ((), (), s32[]{:S(2)}) async-start(), calls=%async_computation.11 | async-start | bytes 3342336 | tf_op jit(solution)/shard_map/all_gather | solution.py:41
  27.5 99.6 %all-gather.15.cloned.1.call-start = ((), (), s32[]{:S(2)}) async-start(), calls=%async_computation.10 | async-start | bytes 9437184 | tf_op jit(solution)/shard_map/all_gather | solution.py:50
  27.8 110.3 %copy-start.7 = (f32[2,128]{1,0:T(2,128)}, f32[2,128]{1,0:T(2,128)S(1)}, u32[]{:S(2)}) copy-start(f32[2,128]{1,0:T(2,128)S(1)} %fusion.33) | copy-start | bytes 3076
  27.8 110.3 %copy-start.5 = (f32[256]{0:T(256)}, f32[256]{0:T(256)S(1)}, u32[]{:S(2)}) copy-start(f32[256]{0:T(256)S(1)} %bitcast_rsqrt_fusion) | copy-start | bytes 3076
  29.1 146.3 %all-gather.35.cloned.1.call-start = ((), (), s32[]{:S(2)}) async-start(), calls=%async_computation.28 | async-start | bytes 3342336 | tf_op jit(solution)/shard_map/all_gather | solution.py:42
  30.2 250.0 %reduce-scatter.9.cloned.1.call-start = ((), (), s32[]{:S(2)}) async-start(), calls=%async_computation.12 | async-start | bytes 18874368 | tf_op jit(solution)/shard_map/reduce_scatter | solution.py:54
  188.5 140.2 %all-gather.21.cloned.1.call-start = ((), (), s32[]{:S(2)}) async-start(), calls=%async_computation.14 | async-start | bytes 3342336 | tf_op jit(solution)/shard_map/all_gather | solution.py:41
  189.1 191.8 %all-gather.19.cloned.1.call-start = ((), (), s32[]{:S(2)}) async-start(), calls=%async_computation.13 | async-start | bytes 9437184 | tf_op jit(solution)/shard_map/all_gather | solution.py:50
  283.4 146.4 %all-gather.37.cloned.1.call-start = ((), (), s32[]{:S(2)}) async-start(), calls=%async_computation.29 | async-start | bytes 3342336 | tf_op jit(solution)/shard_map/all_gather | solution.py:42
  284.1 197.5 %all-gather.25.cloned.1.call-start = ((), (), s32[]{:S(2)}) async-start(), calls=%async_computation.17 | async-start | bytes 9437184 | tf_op jit(solution)/shard_map/all_gather | solution.py:66
  284.9 245.7 %all-gather.23.cloned.1.call-start = ((), (), s32[]{:S(2)}) async-start(), calls=%async_computation.16 | async-start | bytes 3342336 | tf_op jit(solution)/shard_map/all_gather | solution.py:42
  442.9 136.2 %all-gather.27.cloned.1.call-start = ((), (), s32[]{:S(2)}) async-start(), calls=%async_computation.18 | async-start | bytes 3342336 | tf_op jit(solution)/shard_map/all_gather | solution.py:41
  443.5 239.8 %reduce-scatter.13.cloned.1.call-start = ((), (), s32[]{:S(2)}) async-start(), calls=%async_computation.19 | async-start | bytes 18874368 | tf_op jit(solution)/shard_map/reduce_scatter | solution.py:70
  591.7 185.5 %copy-start.3 = (bf16[2,128,2048]{2,1,0:T(8,128)(2,1)S(1)}, bf16[2,128,2048]{2,1,0:T(8,128)(2,1)}, u32[]{:S(2)}) copy-start(bf16[2,128,2048]{2,1,0:T(8,128)(2,1)} %param.5) | copy-start | bytes 3145732
  591.7 185.5 %reduce-scatter.11.cloned.1.call-start = ((), (), s32[]{:S(2)}) async-start(), calls=%async_computation.15 | async-start | bytes 18874368 | tf_op jit(solution)/shard_map/reduce_scatter | solution.py:54
  592.3 234.2 %all-gather.31.cloned.1.call-start = ((), (), s32[]{:S(2)}) async-start(), calls=%async_computation.21 | async-start | bytes 3342336 | tf_op jit(solution)/shard_map/all_gather | solution.py:42
  593.0 285.6 %all-gather.29.cloned.1.call-start = ((), (), s32[]{:S(2)}) async-start(), calls=%async_computation.20 | async-start | bytes 9437184 | tf_op jit(solution)/shard_map/all_gather | solution.py:66
  781.5 145.7 %all-gather.33.cloned.1.call-start = ((), (), s32[]{:S(2)}) async-start(), calls=%async_computation.22 | async-start | bytes 3342336 | tf_op jit(solution)/shard_map/all_gather | solution.py:41
  782.0 228.0 %reduce-scatter.23.cloned.1.call-start = ((), (), s32[]{:S(2)}) async-start(), calls=%async_computation.27 | async-start | bytes 6684672 | tf_op jit(solution)/shard_map/reduce_scatter | solution.py:74
  795.4 1.9 copy-start.10
  795.5 298.9 %reduce-scatter.19.cloned.1.call-start = ((), (), s32[]{:S(2)}) async-start(), calls=%async_computation.25 | async-start | bytes 6684672 | tf_op jit(solution)/shard_map/reduce_scatter | solution.py:73
  808.2 70.4 %copy-start.9 = (bf16[2048,768]{1,0:T(8,128)(2,1)S(1)}, bf16[2048,768]{1,0:T(8,128)(2,1)}, u32[]{:S(2)}) copy-start(bf16[2048,768]{1,0:T(8,128)(2,1)} %convolution_convert_fusion.1) | copy-start | bytes 9437188
  808.3 370.4 %reduce-scatter.17.cloned.1.call-start = ((), (), s32[]{:S(2)}) async-start(), calls=%async_computation.24 | async-start | bytes 6684672 | tf_op jit(solution)/shard_map/reduce_scatter | solution.py:73
  891.8 1.6 copy-start.11
  904.5 358.8 %reduce-scatter.21.cloned.1.call-start = ((), (), s32[]{:S(2)}) async-start(), calls=%async_computation.26 | async-start | bytes 6684672 | tf_op jit(solution)/shard_map/reduce_scatter | solution.py:74
  916.7 10.4 copy-start.12
  916.8 441.4 %reduce-scatter.15.cloned.1.call-start = ((), (), s32[]{:S(2)}) async-start(), calls=%async_computation.23 | async-start | bytes 18874368 | tf_op jit(solution)/shard_map/reduce_scatter | solution.py:70
  1180.8 85.0 %all-to-all-start.1 = ((f32[8,2,16,768]{3,2,1,0:T(8,128)}), f32[8,2,16,768]{3,2,1,0:T(8,128)S(1)}, u32[]{:S(2)}, u32[]{:S(2)}) async-start(f32[8,2,16,768]{3,2,1,0:T(8,128)} %maximum_bitcast_fusion), calls=%async_computation.7 | async-start | bytes 1572864 | tf_op jit(solution)/shard_map/all_to_all | solution.py:79
  1268.1 90.0 %copy-start.1 = (bf16[2,128,2048]{2,1,0:T(8,128)(2,1)S(1)}, bf16[2,128,2048]{2,1,0:T(8,128)(2,1)}, u32[]{:S(2)}) copy-start(bf16[2,128,2048]{2,1,0:T(8,128)(2,1)} %param.4) | copy-start | bytes 3145732
  1268.1 91.9 %copy-start.8 = (f32[2,128]{1,0:T(2,128)S(1)}, f32[2,128]{1,0:T(2,128)}, u32[]{:S(2)}) copy-start(f32[2,128]{1,0:T(2,128)} %copy-done.7) | copy-start | bytes 3076
  1268.1 91.9 %copy-start.2 = (bf16[256,2048]{1,0:T(8,128)(2,1)S(1)}, bf16[256,2048]{1,0:T(8,128)(2,1)}, u32[]{:S(2)}) copy-start(bf16[256,2048]{1,0:T(8,128)(2,1)} %get-tuple-element.26) | copy-start | bytes 3145732
  1268.1 91.9 %copy-start.6 = (f32[256]{0:T(256)S(1)}, f32[256]{0:T(256)}, u32[]{:S(2)}) copy-start(f32[256]{0:T(256)} %copy-done.5) | copy-start | bytes 3076
Sparse Core Ops, SparseCore 0:
  27.6 47.0 all-gather.16
  76.9 50.0 all-gather.14
  129.2 46.1 all-gather.34
  188.6 91.5 reduce-scatter.8
  282.1 46.4 all-gather.20
  330.8 50.0 all-gather.18
  383.6 46.1 all-gather.36
  431.5 50.0 all-gather.24
  484.3 46.1 all-gather.22
  532.5 46.4 all-gather.26
  591.8 91.5 reduce-scatter.12
  685.7 91.4 reduce-scatter.10
  779.9 46.4 all-gather.30
  828.6 50.0 all-gather.28
  880.6 46.4 all-gather.32
  930.4 79.5 reduce-scatter.22
  1013.4 80.9 reduce-scatter.18
  1097.7 80.9 reduce-scatter.16
  1182.1 81.0 reduce-scatter.20
  1265.5 92.5 reduce-scatter.14

commit v2 on v1

v2 whole, which is shorter than its diff:
```python
import functools

import jax
import jax.numpy as jnp
from jax import lax
from jax.experimental import pallas as pl
from jax.experimental.pallas import tpu as pltpu
from jax.sharding import PartitionSpec as P

NORM_EPS = 1e-6
ALL_AXES = ("local", "data")
PAD = 48
RING = 4
CORES = 2
MESH = pl.DeviceIdType.MESH


def norm_f32(x_f32):
    return x_f32 * lax.rsqrt(jnp.mean(x_f32 * x_f32, axis=-1, keepdims=True) + NORM_EPS)


def gelu_f32(pre_f32):
    return jax.nn.gelu(pre_f32, approximate=True)


class Place:
    def __init__(self):
        local, data = lax.axis_index("local"), lax.axis_index("data")
        self.z, self.y = local // RING, local % RING
        self.x, self.core = data // CORES, data % CORES

    def dev(self, z=None, y=None, x=None, core=None):
        z, y = self.z if z is None else z, self.y if y is None else y
        x, core = self.x if x is None else x, self.core if core is None else core
        return (z * RING + y, x * CORES + core)

    def along(self, axis):
        me = getattr(self, axis)
        right, left = lax.rem(me + 1, RING), lax.rem(me + RING - 1, RING)
        return me, self.dev(**{axis: right}), self.dev(**{axis: left})

    def sibling(self):
        return self.dev(core=1 - self.core)


def greet(devices):
    barrier = pltpu.get_barrier_semaphore()
    for device in devices:
        pl.semaphore_signal(barrier, inc=1, device_id=device, device_id_type=MESH)
    pl.semaphore_wait(barrier, len(devices))


class Sender:
    def __init__(self, send_sems, recv_sems):
        self.send_sems, self.recv_sems, self.started = send_sems, recv_sems, []

    def copy(self, slot, src, dst, device):
        c = pltpu.make_async_remote_copy(src_ref=src, dst_ref=dst, send_sem=self.send_sems.at[slot],
                                         recv_sem=self.recv_sems.at[slot], device_id=device, device_id_type=MESH)
        return c

    def start(self, slot, src, dst, device):
        c = self.copy(slot, src, dst, device)
        c.start()
        self.started.append(c)

    def arrived(self, slot, dst, device):
        self.copy(slot, dst, dst, device).wait_recv()

    def drain(self):
        for c in self.started:
            c.wait_send()


class RingGather:
    def __init__(self, sender, base, ring, own, block):
        self.s, self.base, self.own, self.block = sender, base, own, block
        self.me, self.right, self.left = ring
        self.prev, self.next = lax.rem(self.me + 3, RING), lax.rem(self.me + 1, RING)
        self.far = lax.rem(self.me + 2, RING)

    def start(self):
        for h in (0, 1):
            self.s.start(self.base + h, self.own(h), self.block(self.me, h), self.right)
            self.s.start(self.base + 3 - h, self.own(1 - h), self.block(self.me, 1 - h), self.left)

    def relay(self):
        self.s.arrived(self.base, self.block(self.prev, 0), self.left)
        self.s.start(self.base + 4, self.block(self.prev, 0), self.block(self.prev, 0), self.right)
        self.s.arrived(self.base + 3, self.block(self.next, 1), self.right)
        self.s.start(self.base + 5, self.block(self.next, 1), self.block(self.next, 1), self.left)

    def near(self):
        self.s.arrived(self.base + 1, self.block(self.prev, 1), self.left)
        self.s.arrived(self.base + 2, self.block(self.next, 0), self.right)

    def finish(self):
        self.s.arrived(self.base + 4, self.block(self.far, 0), self.left)
        self.s.arrived(self.base + 5, self.block(self.far, 1), self.right)


def gather_kernel(x_ref, up_ref, down_ref, xs_ref, w1_ref, w2_ref, send_sems, recv_sems, local_sems):
    p = Place()
    ring_x, ring_y, ring_z = p.along("x"), p.along("y"), p.along("z")
    sib, c, o = p.sibling(), p.core, 1 - p.core
    keep = [pltpu.make_async_copy(x_ref, xs_ref.at[p.x, c], local_sems.at[0]),
            pltpu.make_async_copy(up_ref, w1_ref.at[p.z, p.y], local_sems.at[1]),
            pltpu.make_async_copy(down_ref, w2_ref.at[p.z, p.y], local_sems.at[2])]
    for copy in keep:
        copy.start()
    greet([ring_x[1], ring_x[2], ring_y[1], ring_y[2], ring_z[1], ring_z[2], sib])
    s = Sender(send_sems, recv_sems)
    rows, cols = up_ref.shape[0] // 2, down_ref.shape[1] // 2
    gx = RingGather(s, 0, ring_x, lambda h: x_ref.at[h], lambda i, h: xs_ref.at[i, c, h])
    up1 = RingGather(s, 6, ring_y, lambda h: up_ref.at[pl.ds(h * rows, rows)],
                     lambda i, h: w1_ref.at[p.z, i, pl.ds(h * rows, rows)])
    down1 = RingGather(s, 12, ring_z, lambda h: down_ref.at[:, pl.ds(h * cols, cols)],
                       lambda i, h: w2_ref.at[i, p.y, :, pl.ds(h * cols, cols)])
    up2 = RingGather(s, 18, ring_z, lambda h: w1_ref.at[p.z, pl.ds(2 * h, 2)],
                     lambda i, h: w1_ref.at[i, pl.ds(2 * h, 2)])
    down2 = RingGather(s, 24, ring_y, lambda h: w2_ref.at[pl.ds(2 * h, 2), p.y],
                       lambda i, h: w2_ref.at[pl.ds(2 * h, 2), i])

    def to_sibling(k, i, h, src=None):
        s.start(30 + k, xs_ref.at[i, c, h] if src is None else src, xs_ref.at[i, c, h], sib)

    up1.start()
    down1.start()
    gx.start()
    for h in (0, 1):
        to_sibling(h, p.x, h, x_ref.at[h])
    up1.relay()
    down1.relay()
    up1.near()
    down1.near()
    up1.finish()
    down1.finish()
    for copy in keep:
        copy.wait()
    up2.start()
    down2.start()
    gx.relay()
    to_sibling(2, gx.prev, 0)
    to_sibling(3, gx.next, 1)
    up2.relay()
    down2.relay()
    gx.near()
    to_sibling(4, gx.prev, 1)
    to_sibling(5, gx.next, 0)
    up2.near()
    down2.near()
    up2.finish()
    down2.finish()
    gx.finish()
    to_sibling(6, gx.far, 0)
    to_sibling(7, gx.far, 1)
    for k, (i, h) in enumerate(((p.x, 0), (p.x, 1), (gx.prev, 0), (gx.next, 1), (gx.prev, 1), (gx.next, 0), (gx.far, 0), (gx.far, 1))):
        s.arrived(30 + k, xs_ref.at[i, o, h], sib)
    s.drain()


def gather(x, up, down):
    vmem, anywhere = pl.BlockSpec(memory_space=pltpu.VMEM), pl.BlockSpec(memory_space=pl.ANY)
    return pl.pallas_call(
        gather_kernel,
        out_shape=[jax.ShapeDtypeStruct((RING, CORES) + x.shape, x.dtype),
                   jax.ShapeDtypeStruct((RING, RING) + up.shape, up.dtype),
                   jax.ShapeDtypeStruct((RING, RING) + down.shape, down.dtype)],
        in_specs=[vmem] * 3,
        out_specs=[anywhere] * 3,
        scratch_shapes=[pltpu.SemaphoreType.DMA((38,)), pltpu.SemaphoreType.DMA((38,)), pltpu.SemaphoreType.DMA((3,))],
        compiler_params=pltpu.CompilerParams(collective_id=0, has_side_effects=True),
        cost_estimate=pl.CostEstimate(flops=0, bytes_accessed=120_000_000, transcendentals=0),
        name="gather",
    )(x, up, down)


def add_into(dst, *terms):
    rows = dst.shape[0]

    @pl.loop(0, rows // 8)
    def _(i):
        at = pl.ds(pl.multiple_of(i * 8, 8), 8)
        total = dst[at, :]
        for term in terms:
            total = total + term[at, :]
        dst[at, :] = total


def scatter_kernel(transposed, h_ref, w_ref, y_ref, to_sib, from_sib, acc, relayed, arriving, send_sems, recv_sems):
    p = Place()
    me, right, left = p.along("x")
    sib, c, o = p.sibling(), p.core, 1 - p.core
    greet([right, left, sib])
    s = Sender(send_sems, recv_sems)
    hidden = y_ref.shape[1]
    rows = y_ref.shape[0] // 2
    step = 512
    first, second = pl.ds(0, rows), pl.ds(rows, rows)

    def product(dx, core, dst):
        block = lax.rem(me + dx, RING)

        @pl.loop(0, hidden // step)
        def _(n):
            at = pl.ds(pl.multiple_of(n * step, step), step)
            if transposed:
                dst[:, at] = lax.dot_general(h_ref[block, core], w_ref[at, :], (((1,), (1,)), ((), ())),
                                             preferred_element_type=jnp.float32)
            else:
                dst[:, at] = jnp.dot(h_ref[block, core], w_ref[:, at], preferred_element_type=jnp.float32)

    def both(k, dx, dst):
        product(dx, o, to_sib.at[k])
        s.start(k, to_sib.at[k], from_sib.at[k], sib)
        product(dx, c, dst)

    def joined(k, dst):
        s.arrived(k, from_sib.at[k], sib)
        add_into(dst, from_sib.at[k])

    both(0, 2, acc.at[0])
    both(1, 1, acc.at[1])
    joined(0, acc.at[0])
    s.start(4, acc.at[0, first], relayed.at[0], right)
    s.start(5, acc.at[0, second], relayed.at[1], left)
    both(2, 3, acc.at[2])
    joined(1, acc.at[1])
    s.start(6, acc.at[1, second], arriving.at[0, second], right)
    both(3, 0, y_ref)
    joined(2, acc.at[2])
    s.start(7, acc.at[2, first], arriving.at[1, first], left)
    joined(3, y_ref)
    s.arrived(4, relayed.at[0], left)
    add_into(acc.at[1, first], relayed.at[0])
    s.start(8, acc.at[1, first], arriving.at[0, first], right)
    s.arrived(5, relayed.at[1], right)
    add_into(acc.at[2, second], relayed.at[1])
    s.start(9, acc.at[2, second], arriving.at[1, second], left)
    s.arrived(6, arriving.at[0, second], left)
    s.arrived(7, arriving.at[1, first], right)
    s.arrived(8, arriving.at[0, first], left)
    s.arrived(9, arriving.at[1, second], right)
    add_into(y_ref, arriving.at[0], arriving.at[1])
    s.drain()


def scatter(h, w, transposed):
    rows, width = h.shape[2:]
    hidden = w.shape[0] if transposed else w.shape[1]
    vmem = pl.BlockSpec(memory_space=pltpu.VMEM)
    f32 = jnp.float32
    return pl.pallas_call(
        functools.partial(scatter_kernel, transposed),
        out_shape=jax.ShapeDtypeStruct((rows, hidden), f32),
        in_specs=[vmem] * 2,
        out_specs=vmem,
        scratch_shapes=[pltpu.VMEM((RING, rows, hidden), f32), pltpu.VMEM((RING, rows, hidden), f32),
                        pltpu.VMEM((3, rows, hidden), f32), pltpu.VMEM((2, rows // 2, hidden), f32),
                        pltpu.VMEM((2, rows, hidden), f32),
                        pltpu.SemaphoreType.DMA((10,)), pltpu.SemaphoreType.DMA((10,))],
        compiler_params=pltpu.CompilerParams(collective_id=2 if transposed else 1, has_side_effects=True,
                                             vmem_limit_bytes=48 * 1024 * 1024),
        cost_estimate=pl.CostEstimate(flops=0, bytes_accessed=240_000_000, transcendentals=0),
        name="scatter_t" if transposed else "scatter",
    )(h, w)


def solution(mesh):
    n_data = mesh.shape["data"]
    n_local = mesh.shape["local"]

    def body(tokens, cotangent, w_up, w_down):
        micro, rows, hidden = tokens.shape
        layers, up_rows, ffn = w_up.shape
        down_rows = w_down.shape[1]
        pad = PAD - down_rows
        width = n_local * PAD
        own = micro * rows
        count = n_data * own

        up = w_up.reshape(layers, up_rows, n_local, n_data, down_rows)
        up = jnp.pad(up, ((0, 0),) * 4 + ((0, pad),))
        up = up.transpose(3, 0, 1, 2, 4).reshape(n_data, layers, up_rows, width)
        up = lax.all_to_all(up, "data", 0, 0)
        up = up.transpose(1, 0, 2, 3).reshape(layers, n_data * up_rows, width)
        down = jnp.pad(w_down, ((0, 0), (0, pad), (0, 0)))

        def gathered(x, layer):
            xs, w1, w2 = gather(x.reshape(micro, rows, hidden), up[layer], down[layer])
            return xs.reshape(count, hidden), w1.reshape(hidden, width), w2.reshape(width, hidden)

        def scattered(h, w, transposed):
            return scatter(h.reshape(RING, CORES, own, width), w, transposed)

        x_cur = tokens.reshape(own, hidden)
        saved = []
        for layer in range(layers):
            x_f32 = x_cur.astype(jnp.float32)
            u_all, w1, w2 = gathered(norm_f32(x_f32).astype(jnp.bfloat16), layer)
            pre = jnp.dot(u_all, w1, preferred_element_type=jnp.float32).astype(jnp.bfloat16)
            act = gelu_f32(pre.astype(jnp.float32)).astype(jnp.bfloat16)
            y = scattered(act, w2, False)
            saved.append((x_cur, u_all, pre, act))
            x_cur = (x_f32 + y).astype(jnp.bfloat16)
        x_final = x_cur

        d_cur = cotangent.reshape(own, hidden)
        d_cur, x_final = lax.optimization_barrier((d_cur, x_final))
        grads_up = [None] * layers
        grads_down = [None] * layers
        for layer in reversed(range(layers)):
            x_in, u_all, pre, act = saved[layer]
            c_all, w1, w2 = gathered(d_cur, layer)
            e = jnp.einsum("tm,fm->tf", c_all, w2, preferred_element_type=jnp.float32)
            z = jax.vjp(gelu_f32, pre.astype(jnp.float32))[1](e)[0].astype(jnp.bfloat16)
            d_w2 = jnp.einsum("tf,tm->fm", act, c_all, preferred_element_type=jnp.float32)
            d_w1 = jnp.einsum("tm,tf->mf", u_all, z, preferred_element_type=jnp.float32)
            v = scattered(z, w1, True)
            grads_up[layer] = lax.psum_scatter(d_w1, "local", scatter_dimension=0, tiled=True)
            grads_down[layer] = lax.psum_scatter(d_w2, "local", scatter_dimension=0, tiled=True)[:down_rows]
            norm_pull = jax.vjp(norm_f32, x_in.astype(jnp.float32))[1]
            d_cur = (d_cur.astype(jnp.float32) + norm_pull(v)[0]).astype(jnp.bfloat16)
        g_up = jnp.stack(grads_up).reshape(layers, n_data, up_rows, width).transpose(1, 0, 2, 3)
        g_up = lax.all_to_all(g_up, "data", 0, 0)
        g_up = g_up.reshape(n_data, layers, up_rows, n_local, PAD)[..., :down_rows]
        g_up = g_up.transpose(1, 2, 3, 0, 4).reshape(layers, up_rows, ffn)
        shape = (micro, rows, hidden)
        return x_final.reshape(shape), d_cur.reshape(shape), g_up, jnp.stack(grads_down)

    spec = P(None, ALL_AXES, None)
    return jax.shard_map(body, mesh=mesh, in_specs=(spec,) * 4, out_specs=(spec,) * 4, check_vma=False)
```

time: 1380 us -> 785 us (0.57)
  waiting for transfers between devices: 1140 us -> 134 us
  Pallas kernels: 0 us -> 493 us
  matrix products: 148 us -> 101 us
    pallas_call x0 -> x8, Pallas kernels: none -> 493 us  [the longest x4 320 us: scatter(): pl.pallas_call(functools.partial(scatter_kernel, transposed), out_shape=j...]
    all_gather x12 -> x0, waiting for transfers between devices: 468 us -> none  [the longest x4 142 us: gather_weights(): lax.all_gather(d, 'local', axis=0, tiled=True)]
    reduce_scatter x4 -> x0, waiting for transfers between devices: 355 us -> none  [the longest x2 183 us: body(): y = lax.psum_scatter(part, 'data', scatter_dimension=0, tiled=True)]
    reduce_scatter x2, waiting for transfers between devices: 168 us -> 0.01 us  [body(): lax.psum_scatter(d_w1, 'local', scatter_dimension=0, tiled=True)]
    dot_general x4 -> x0, matrix products: 50.1 us -> none  [the longest x2 26.2 us: body(): part = jnp.dot(act, w2, preferred_element_type=jnp.float32)]
    reduce_scatter x2, waiting for transfers between devices: 147 us -> 129 us  [body(): lax.psum_scatter(d_w2, 'local', scatter_dimension=0, tiled=True)[:down_rows]]
  transfers between devices with their start and end apart: 21 -> 6, of which waited for: 20 -> 3; matrix products, arithmetic and copies ran while one was open for 11% -> 8% of each run, Pallas kernels for 0% -> 26%
where the time goes in v2:
time: 785 us; the launch traced here: 780 us
  Pallas kernels  493 us (63%)
  waiting for transfers between devices  134 us (17%)
  matrix products  101 us (13%)
  local copies, waits for them, and re-layouts  16.6 us (2%)
  between operations  14.2 us (2%)
  starting transfers between devices  10.6 us (1%)
  other arithmetic  10.4 us (1%)
    pallas_call x4, Pallas kernels, scatter(): pl.pallas_call(functools.partial(scatter_kernel, transposed), out_shape=j...  320 us
    pallas_call x4, Pallas kernels, gather(): pl.pallas_call(gather_kernel, out_shape=[jax.ShapeDtypeStruct((RING, CORE...  173 us
    reduce_scatter x2, waiting for transfers between devices, body(): lax.psum_scatter(d_w2, 'local', scatter_dimension=0, tiled=True)[:down_rows]  129 us
    dot_general x2, matrix products, body(): e = jnp.einsum('tm,fm->tf', c_all, w2, preferred_element_type=jnp.float32)  27.6 us
    dot_general x2, matrix products, body(): jnp.einsum('tf,tm->fm', act, c_all, preferred_element_type=jnp.float32)  26.5 us
    dot_general x2, matrix products, body(): jnp.dot(u_all, w1, preferred_element_type=jnp.float32).astype(jnp.bfloat16)  24.6 us
    dot_general x2, matrix products, body(): d_w1 = jnp.einsum('tm,tf->mf', u_all, z, preferred_element_type=jnp.float32)  22.1 us
  transfers between devices with their start and end apart: 6, of which 3 were waited for; matrix products, arithmetic and copies ran while one was open for 8% of the time, Pallas kernels for 26%

profile of v2, /device:TPU:1, one launch (start us, length us, event | category | flops | bytes accessed | tf_op | source)
XLA Modules:
  0.0 779.6 jit_solution(14085289341762387922)
XLA Ops:
  7.2 4.1 reshape.146
  11.3 0.2 copy.12
  11.5 0.3 pad_bitcast_fusion
  11.8 2.0 reshape.147
  13.8 5.8 all-to-all-start
  19.6 0.3 fusion.28
  19.9 1.2 fusion.29.x_ref
  21.1 0.1 copy.13
  21.2 0.8 fusion.33
  22.0 5.1 all-to-all-done
  27.1 0.8 fusion.41
  27.9 45.6 %gather.4 = (bf16[4,2,2,128,2048]{4,3,2,1,0:T(8,128)(2,1)}, bf16[4,4,128,768]{3,2,1,0:T(8,128)(2,1)}, bf16[4,4,48,2048]{3,2,1,0:T(8,128)(2,1)}) custom-call(bf16[2,128,2048]{2,1,0:T(8,128)(2,1)} %fusion.29.x_ref, bf16[128,768]{1,0:T(8,128)(2,1)} %bitcast.94, bf16[48,2048]{1,0:T(8,128)(2,1)} %get-tuple-element.43.down_ref), custom_call_target="tpu_custom_call" | custom-call | bytes 120000000 | tf_op jit(solution)/shard_map/gather/pallas_call | solution.py:164
  73.5 12.4 %fusion.11 = (bf16[2048,768]{1,0:T(8,128)(2,1)S(1)}, bf16[2048,768]{1,0:T(8,128)(2,1)}) fusion(bf16[2048,2048]{1,0:T(8,128)(2,1)} %bitcast.103, bf16[2048,768]{1,0:T(8,128)(2,1)} %bitcast.111), kind=kOutput, calls=%fused_computation.21 | convolution fusion | flops 6459752448 | bytes 17825792 | tf_op jit(solution)/shard_map/dot_general | solution.py:301
  85.9 79.6 %scatter.2 = f32[256,2048]{1,0:T(8,128)S(1)} custom-call(bf16[4,2,256,768]{3,2,1,0:T(8,128)(2,1)S(1)} %bitcast.85, bf16[768,2048]{1,0:T(8,128)(2,1)} %bitcast.92), custom_call_target="tpu_custom_call" | custom-call | bytes 240000000 | tf_op jit(solution)/shard_map/scatter/pallas_call | solution.py:253
  165.5 0.4 fusion.24
  165.9 1.3 fusion.25
  167.2 42.6 %gather.5 = (bf16[4,2,2,128,2048]{4,3,2,1,0:T(8,128)(2,1)}, bf16[4,4,128,768]{3,2,1,0:T(8,128)(2,1)}, bf16[4,4,48,2048]{3,2,1,0:T(8,128)(2,1)}) custom-call(bf16[2,128,2048]{2,1,0:T(8,128)(2,1)} %bitcast.89, bf16[128,768]{1,0:T(8,128)(2,1)} %bitcast.96, bf16[48,2048]{1,0:T(8,128)(2,1)} %get-tuple-element.42.down_ref), custom_call_target="tpu_custom_call" | custom-call | bytes 120000000 | tf_op jit(solution)/shard_map/gather/pallas_call | solution.py:164
  209.9 12.2 %fusion.17 = (bf16[2048,768]{1,0:T(8,128)(2,1)S(1)}, bf16[2048,768]{1,0:T(8,128)(2,1)}) fusion(bf16[2048,2048]{1,0:T(8,128)(2,1)} %bitcast.109, bf16[2048,768]{1,0:T(8,128)(2,1)} %bitcast.112), kind=kOutput, calls=%fused_computation.27 | convolution fusion | flops 6459752448 | bytes 17825792 | tf_op jit(solution)/shard_map/dot_general | solution.py:301
  222.1 79.6 %scatter.3 = f32[256,2048]{1,0:T(8,128)S(1)} custom-call(bf16[4,2,256,768]{3,2,1,0:T(8,128)(2,1)S(1)} %bitcast.86, bf16[768,2048]{1,0:T(8,128)(2,1)} %bitcast.93), custom_call_target="tpu_custom_call" | custom-call | bytes 240000000 | tf_op jit(solution)/shard_map/scatter/pallas_call | solution.py:253
  301.7 1.3 fusion.26
  303.0 42.2 %gather.6 = (bf16[4,2,2,128,2048]{4,3,2,1,0:T(8,128)(2,1)}, bf16[4,4,128,768]{3,2,1,0:T(8,128)(2,1)}, bf16[4,4,48,2048]{3,2,1,0:T(8,128)(2,1)}) custom-call(bf16[2,128,2048]{2,1,0:T(8,128)(2,1)} %param.5, bf16[128,768]{1,0:T(8,128)(2,1)} %bitcast.97, bf16[48,2048]{1,0:T(8,128)(2,1)} %get-tuple-element.42.down_ref), custom_call_target="tpu_custom_call" | custom-call | bytes 120000000 | tf_op jit(solution)/shard_map/gather/pallas_call | solution.py:164
  345.2 13.9 %fusion.4 = bf16[2048,768]{1,0:T(8,128)(2,1)S(1)} fusion(bf16[2048,768]{1,0:T(8,128)(2,1)} %get-tuple-element.51, bf16[2048,2048]{1,0:T(8,128)(2,1)} %bitcast.105, bf16[768,2048]{1,0:T(8,128)(2,1)} %bitcast.113), kind=kOutput, calls=%fused_computation.14 | convolution fusion | flops 6475481088 | bytes 17825792 | tf_op jit(solution)/shard_map/tm,fm->tf/dot_general | solution.py:315
  359.1 11.0 %fusion.43 = f32[2048,768]{1,0:T(8,128)} fusion(bf16[2048,2048]{1,0:T(8,128)(2,1)} %bitcast.110, bf16[2048,768]{1,0:T(8,128)(2,1)S(1)} %fusion.4), kind=kOutput, calls=%fused_computation.78 | convolution fusion | flops 6442450944 | bytes 17825792 | tf_op jit(solution)/shard_map/tm,tf->mf/dot_general | solution.py:318
  370.2 80.6 %scatter_t.2 = f32[256,2048]{1,0:T(8,128)S(1)} custom-call(bf16[4,2,256,768]{3,2,1,0:T(8,128)(2,1)S(1)} %bitcast.84, bf16[2048,768]{1,0:T(8,128)(2,1)} %bitcast.91), custom_call_target="tpu_custom_call" | custom-call | bytes 240000000 | tf_op jit(solution)/shard_map/scatter_t/pallas_call | solution.py:253
  450.8 0.3 fusion.27
  451.2 1.6 fusion.21
  452.8 42.2 %gather.7 = (bf16[4,2,2,128,2048]{4,3,2,1,0:T(8,128)(2,1)}, bf16[4,4,128,768]{3,2,1,0:T(8,128)(2,1)}, bf16[4,4,48,2048]{3,2,1,0:T(8,128)(2,1)}) custom-call(bf16[2,128,2048]{2,1,0:T(8,128)(2,1)} %bitcast.87, bf16[128,768]{1,0:T(8,128)(2,1)} %bitcast.95, bf16[48,2048]{1,0:T(8,128)(2,1)} %get-tuple-element.43.down_ref), custom_call_target="tpu_custom_call" | custom-call | bytes 120000000 | tf_op jit(solution)/shard_map/gather/pallas_call | solution.py:164
  495.0 13.7 %fusion.7 = bf16[2048,768]{1,0:T(8,128)(2,1)S(1)} fusion(bf16[2048,768]{1,0:T(8,128)(2,1)} %get-tuple-element.49, bf16[2048,2048]{1,0:T(8,128)(2,1)} %bitcast.107, bf16[768,2048]{1,0:T(8,128)(2,1)} %bitcast.114), kind=kOutput, calls=%fused_computation.17 | convolution fusion | flops 6475481088 | bytes 17825792 | tf_op jit(solution)/shard_map/tm,fm->tf/dot_general | solution.py:315
  508.7 11.1 %fusion.42 = f32[2048,768]{1,0:T(8,128)} fusion(bf16[2048,2048]{1,0:T(8,128)(2,1)} %bitcast.104, bf16[2048,768]{1,0:T(8,128)(2,1)S(1)} %fusion.7), kind=kOutput, calls=%fused_computation.77 | convolution fusion | flops 6442450944 | bytes 17825792 | tf_op jit(solution)/shard_map/tm,tf->mf/dot_general | solution.py:318
  519.8 0.0 reduce-scatter.11.cloned.1.call-start
  519.8 13.3 %fusion.36 = f32[768,2048]{1,0:T(8,128)} fusion(bf16[2048,2048]{1,0:T(8,128)(2,1)} %bitcast.106, bf16[2048,768]{1,0:T(8,128)(2,1)} %get-tuple-element.51), kind=kOutput, calls=%fused_computation.74 | convolution fusion | flops 6458179584 | bytes 17825792 | tf_op jit(solution)/shard_map/tf,tm->fm/dot_general | solution.py:317
  533.2 0.0 reduce-scatter.9.cloned.1.call-start
  533.2 13.1 %fusion.38 = f32[768,2048]{1,0:T(8,128)} fusion(bf16[2048,2048]{1,0:T(8,128)(2,1)} %bitcast.108, bf16[2048,768]{1,0:T(8,128)(2,1)} %get-tuple-element.49), kind=kOutput, calls=%fused_computation.75 | convolution fusion | flops 6458179584 | bytes 17825792 | tf_op jit(solution)/shard_map/tf,tm->fm/dot_general | solution.py:317
  546.4 80.2 %scatter_t.3 = f32[256,2048]{1,0:T(8,128)S(1)} custom-call(bf16[4,2,256,768]{3,2,1,0:T(8,128)(2,1)S(1)} %bitcast.83, bf16[2048,768]{1,0:T(8,128)(2,1)} %bitcast.90), custom_call_target="tpu_custom_call" | custom-call | bytes 240000000 | tf_op jit(solution)/shard_map/scatter_t/pallas_call | solution.py:253
  626.6 0.3 fusion.31
  626.9 1.6 fusion.23
  628.5 2.1 maximum_bitcast_fusion
  630.6 4.7 all-to-all-start.1
  635.2 45.8 %reduce-scatter.11.cloned.1.call-done = f32[48,2048]{1,0:T(8,128)} async-done(((f32[768,2048]{1,0:T(8,128)}), f32[48,2048]{1,0:T(8,128)}) %reduce-scatter.11.cloned.1.call-update) | async-done | bytes 393232 | tf_op jit(solution)/shard_map/reduce_scatter | solution.py:321
  681.0 1.0 slice_bitcast_fusion.1
  682.0 83.3 %reduce-scatter.9.cloned.1.call-done = f32[48,2048]{1,0:T(8,128)} async-done(((f32[768,2048]{1,0:T(8,128)}), f32[48,2048]{1,0:T(8,128)}) %reduce-scatter.9.cloned.1.call-update) | async-done | bytes 393232 | tf_op jit(solution)/shard_map/reduce_scatter | solution.py:321
  765.3 1.0 slice_bitcast_fusion.2
  766.4 0.1 pad_maximum_fusion
  766.4 1.4 copy.17
  767.9 1.0 reshape.169
  768.9 0.1 slice_bitcast_fusion
  769.0 1.2 copy.16
  770.3 2.6 reshape.170
  (27 shorter events, 0.2 us)
Async XLA Ops:
  7.2 12.4 %copy-start = (bf16[2,128,2048]{2,1,0:T(8,128)(2,1)S(1)}, bf16[2,128,2048]{2,1,0:T(8,128)(2,1)}, u32[]{:S(2)}) copy-start(bf16[2,128,2048]{2,1,0:T(8,128)(2,1)} %param.4) | copy-start | bytes 3145732
  7.2 13.9 %copy-start.6 = (bf16[2,44,2048]{2,0,1:T(2,128)(2,1)S(1)}, bf16[2,44,2048]{2,0,1:T(2,128)(2,1)}, u32[]{:S(2)}) copy-start(bf16[2,44,2048]{2,0,1:T(2,128)(2,1)} %param.7) | copy-start | bytes 1081348
  13.8 13.3 %all-to-all-start = ((bf16[8,2,16,768]{3,2,1,0:T(8,128)(2,1)}), bf16[8,2,16,768]{3,2,1,0:T(8,128)(2,1)S(1)}, u32[]{:S(2)}, u32[]{:S(2)}) async-start(bf16[8,2,16,768]{3,2,1,0:T(8,128)(2,1)} %reshape.147), calls=%async_computation | async-start | bytes 786432 | tf_op jit(solution)/shard_map/all_to_all | solution.py:285
  19.6 609.0 %reduce-scatter.7.cloned.1.call-start = ((), (), s32[]{:S(2)}) async-start(), calls=%async_computation.7 | async-start | bytes 6684672 | tf_op jit(solution)/shard_map/reduce_scatter | solution.py:320
  165.9 135.7 %copy-start.2 = (bf16[256,2048]{1,0:T(8,128)(2,1)}, bf16[256,2048]{1,0:T(8,128)(2,1)S(1)}, u32[]{:S(2)}) copy-start(bf16[256,2048]{1,0:T(8,128)(2,1)S(1)} %get-tuple-element.41) | copy-start | bytes 3145732
  370.1 258.4 %reduce-scatter.5.cloned.1.call-start = ((), (), s32[]{:S(2)}) async-start(), calls=%async_computation.6 | async-start | bytes 6684672 | tf_op jit(solution)/shard_map/reduce_scatter | solution.py:320
  370.2 80.7 %copy-start.3 = (bf16[256,2048]{1,0:T(8,128)(2,1)S(1)}, bf16[256,2048]{1,0:T(8,128)(2,1)}, u32[]{:S(2)}) copy-start(bf16[256,2048]{1,0:T(8,128)(2,1)} %copy-done.2) | copy-start | bytes 3145732
  370.2 81.0 %copy-start.5 = (bf16[2,128,2048]{2,1,0:T(8,128)(2,1)S(1)}, bf16[2,128,2048]{2,1,0:T(8,128)(2,1)}, u32[]{:S(2)}) copy-start(bf16[2,128,2048]{2,1,0:T(8,128)(2,1)} %param.5) | copy-start | bytes 3145732
  519.8 161.2 %reduce-scatter.11.cloned.1.call-start = ((), (), s32[]{:S(2)}) async-start(), calls=%async_computation.9 | async-start | bytes 6684672 | tf_op jit(solution)/shard_map/reduce_scatter | solution.py:321
  533.2 232.2 %reduce-scatter.9.cloned.1.call-start = ((), (), s32[]{:S(2)}) async-start(), calls=%async_computation.8 | async-start | bytes 6684672 | tf_op jit(solution)/shard_map/reduce_scatter | solution.py:321
  546.4 80.2 %copy-start.1 = (bf16[2,128,2048]{2,1,0:T(8,128)(2,1)S(1)}, bf16[2,128,2048]{2,1,0:T(8,128)(2,1)}, u32[]{:S(2)}) copy-start(bf16[2,128,2048]{2,1,0:T(8,128)(2,1)} %param.4) | copy-start | bytes 3145732
  546.4 80.5 %copy-start.4 = (bf16[256,2048]{1,0:T(8,128)(2,1)S(1)}, bf16[256,2048]{1,0:T(8,128)(2,1)}, u32[]{:S(2)}) copy-start(bf16[256,2048]{1,0:T(8,128)(2,1)} %fusion.21) | copy-start | bytes 3145732
  630.6 137.3 %all-to-all-start.1 = ((f32[8,2,16,768]{3,2,1,0:T(8,128)}), f32[8,2,16,768]{3,2,1,0:T(8,128)S(1)}, u32[]{:S(2)}, u32[]{:S(2)}) async-start(f32[8,2,16,768]{3,2,1,0:T(8,128)} %maximum_bitcast_fusion), calls=%async_computation.3 | async-start | bytes 1572864 | tf_op jit(solution)/shard_map/all_to_all | solution.py:325
Sparse Core Ops, SparseCore 0:
  370.2 76.5 reduce-scatter.6
  519.9 76.8 reduce-scatter.4
  600.2 80.7 reduce-scatter.10
  684.3 80.9 reduce-scatter.8

commit v3 on v2

--- a/solution.py
+++ b/solution.py
@@ -176,9 +176,12 @@
 
 
 def add_into(dst, *terms):
-    rows = dst.shape[0]
-
-    @pl.loop(0, rows // 8)
+    if len(dst.shape) > 2:
+        for i in range(dst.shape[0]):
+            add_into(dst.at[i], *(term.at[i] for term in terms))
+        return
+
+    @pl.loop(0, dst.shape[0] // 8)
     def _(i):
         at = pl.ds(pl.multiple_of(i * 8, 8), 8)
         total = dst[at, :]
@@ -187,12 +190,120 @@
         dst[at, :] = total
 
 
-def scatter_kernel(transposed, h_ref, w_ref, y_ref, to_sib, from_sib, acc, relayed, arriving, send_sems, recv_sems):
+class RingScatter:
+    def __init__(self, sender, base, ring, block, relayed, arriving):
+        self.s, self.base, self.block, self.relayed, self.arriving = sender, base, block, relayed, arriving
+        self.me, self.right, self.left = ring
+        self.prev, self.next = lax.rem(self.me + 3, RING), lax.rem(self.me + 1, RING)
+        self.far = lax.rem(self.me + 2, RING)
+
+    def start(self):
+        self.s.start(self.base, self.block(self.far, 0), self.relayed(0), self.right)
+        self.s.start(self.base + 1, self.block(self.far, 1), self.relayed(1), self.left)
+        self.s.start(self.base + 2, self.block(self.next, 1), self.arriving(0, 1), self.right)
+        self.s.start(self.base + 3, self.block(self.prev, 0), self.arriving(1, 0), self.left)
+
+    def relay(self, to_next, to_prev):
+        self.s.arrived(self.base, self.relayed(0), self.left)
+        add_into(self.relayed(0), to_next)
+        self.s.start(self.base + 4, self.relayed(0), self.arriving(0, 0), self.right)
+        self.s.arrived(self.base + 1, self.relayed(1), self.right)
+        add_into(self.relayed(1), to_prev)
+        self.s.start(self.base + 5, self.relayed(1), self.arriving(1, 1), self.left)
+
+    def finish(self):
+        self.s.arrived(self.base + 2, self.arriving(0, 1), self.left)
+        self.s.arrived(self.base + 3, self.arriving(1, 0), self.right)
+        self.s.arrived(self.base + 4, self.arriving(0, 0), self.left)
+        self.s.arrived(self.base + 5, self.arriving(1, 1), self.right)
+
+
+class GradScatter:
+    SLOTS = 24
+
+    def __init__(self, p, sender, base, up, down, bufs, sems):
+        self.p, self.sems, self.up, self.down = p, sems, up, down
+        (self.u_rel, self.u_arr, self.u_loc, self.u_own, self.u_rel2, self.u_arr2,
+         self.d_rel, self.d_arr, self.d_loc, self.d_own, self.d_rel2, self.d_arr2) = bufs
+        ring_y, ring_z = p.along("y"), p.along("z")
+        half = lambda h: pl.ds(2 * h, 2)
+        u_rows, d_rows = up.shape[2] // 2, down.shape[2] // 2
+        u_part, d_part = (lambda h: pl.ds(h * u_rows, u_rows)), (lambda h: pl.ds(h * d_rows, d_rows))
+        self.up1 = RingScatter(sender, base, ring_y, lambda i, h: up.at[half(h), i], lambda h: self.u_rel.at[h],
+                               lambda side, h: self.u_arr.at[side, half(h)])
+        self.down1 = RingScatter(sender, base + 6, ring_z, lambda i, h: down.at[i, half(h)], lambda h: self.d_rel.at[h],
+                                 lambda side, h: self.d_arr.at[side, half(h)])
+        self.up2 = RingScatter(sender, base + 12, ring_z, lambda i, h: self.u_own.at[i, u_part(h)], lambda h: self.u_rel2.at[h],
+                               lambda side, h: self.u_arr2.at[side, u_part(h)])
+        self.down2 = RingScatter(sender, base + 18, ring_y, lambda i, h: self.d_own.at[i, d_part(h)], lambda h: self.d_rel2.at[h],
+                                 lambda side, h: self.d_arr2.at[side, d_part(h)])
+        self.u_part, self.d_part = u_part, d_part
+        u, d = self.up1, self.down1
+        pairs = [(up.at[half(0), u.next], self.u_loc.at[0]), (up.at[half(1), u.prev], self.u_loc.at[1]),
+                 (up.at[:, u.me], self.u_own), (down.at[d.next, half(0)], self.d_loc.at[0]),
+                 (down.at[d.prev, half(1)], self.d_loc.at[1]), (down.at[d.me], self.d_own)]
+        self.loads = [pltpu.make_async_copy(src, dst, sems.at[k]) for k, (src, dst) in enumerate(pairs)]
+
+    def load(self):
+        for copy in self.loads:
+            copy.start()
+
+    def start(self):
+        self.up1.start()
+        self.down1.start()
+
+    def relay(self):
+        for copy in self.loads:
+            copy.wait()
+        self.up1.relay(self.u_loc.at[0], self.u_loc.at[1])
+        self.down1.relay(self.d_loc.at[0], self.d_loc.at[1])
+
+    def second(self):
+        self.up1.finish()
+        add_into(self.u_own, self.u_arr.at[0], self.u_arr.at[1])
+        self.up2.start()
+        self.down1.finish()
+        add_into(self.d_own, self.d_arr.at[0], self.d_arr.at[1])
+        self.down2.start()
+        u, d = self.up2, self.down2
+        u.relay(self.u_own.at[u.next, self.u_part(0)], self.u_own.at[u.prev, self.u_part(1)])
+        d.relay(self.d_own.at[d.next, self.d_part(0)], self.d_own.at[d.prev, self.d_part(1)])
+
+    def finish(self, up_out, down_out):
+        self.up2.finish()
+        self.down2.finish()
+        up_out[...] = self.u_own[self.up2.me] + self.u_arr2[0] + self.u_arr2[1]
+        down_out[...] = self.d_own[self.down2.me] + self.d_arr2[0] + self.d_arr2[1]
+
+    @staticmethod
+    def buffers(up, down):
+        f32 = jnp.float32
+        out = []
+        for rows, cols in (up.shape[2:], down.shape[2:]):
+            out += [(2, 2, rows, cols), (2, RING, rows, cols), (2, 2, rows, cols), (RING, rows, cols),
+                    (2, rows // 2, cols), (2, rows, cols)]
+        return [pltpu.VMEM(shape, f32) for shape in out]
+
+
+def scatter_kernel(h_ref, w_ref, *refs):
+    backward = len(refs) > 8
     p = Place()
     me, right, left = p.along("x")
     sib, c, o = p.sibling(), p.core, 1 - p.core
-    greet([right, left, sib])
-    s = Sender(send_sems, recv_sems)
+    if backward:
+        (g_up, g_down, y_ref, up_out, down_out, to_sib, from_sib, acc, relayed, arriving, send_sems, recv_sems,
+         up_sum, local_sems, *bufs) = refs
+        ring_y, ring_z = p.along("y"), p.along("z")
+        others = [p.dev(x=lax.rem(me + dx, RING), core=lax.rem(c + dc, CORES)) for dx in range(RING) for dc in range(CORES)][1:]
+        greet(others + [ring_y[1], ring_y[2], ring_z[1], ring_z[2]])
+        s = Sender(send_sems, recv_sems)
+        grads = GradScatter(p, s, 10, g_up, g_down, bufs, local_sems)
+        grads.start()
+        grads.load()
+    else:
+        y_ref, to_sib, from_sib, acc, relayed, arriving, send_sems, recv_sems = refs
+        greet([right, left, sib])
+        s = Sender(send_sems, recv_sems)
     hidden = y_ref.shape[1]
     rows = y_ref.shape[0] // 2
     step = 512
@@ -204,7 +315,7 @@
         @pl.loop(0, hidden // step)
         def _(n):
             at = pl.ds(pl.multiple_of(n * step, step), step)
-            if transposed:
+            if backward:
                 dst[:, at] = lax.dot_general(h_ref[block, core], w_ref[at, :], (((1,), (1,)), ((), ())),
                                              preferred_element_type=jnp.float32)
             else:
@@ -220,50 +331,78 @@
         add_into(dst, from_sib.at[k])
 
     both(0, 2, acc.at[0])
-    both(1, 1, acc.at[1])
     joined(0, acc.at[0])
     s.start(4, acc.at[0, first], relayed.at[0], right)
     s.start(5, acc.at[0, second], relayed.at[1], left)
+    both(1, 1, acc.at[1])
     both(2, 3, acc.at[2])
     joined(1, acc.at[1])
     s.start(6, acc.at[1, second], arriving.at[0, second], right)
-    both(3, 0, y_ref)
     joined(2, acc.at[2])
     s.start(7, acc.at[2, first], arriving.at[1, first], left)
+    both(3, 0, y_ref)
     joined(3, y_ref)
+    if backward:
+        grads.relay()
     s.arrived(4, relayed.at[0], left)
     add_into(acc.at[1, first], relayed.at[0])
     s.start(8, acc.at[1, first], arriving.at[0, first], right)
     s.arrived(5, relayed.at[1], right)
     add_into(acc.at[2, second], relayed.at[1])
     s.start(9, acc.at[2, second], arriving.at[1, second], left)
+    if backward:
+        grads.second()
+        grads.finish(up_sum, down_out)
+        mine = me * CORES + c
+        piece = up_out.shape[1]
+        keep = pltpu.make_async_copy(up_sum.at[pl.ds(pl.multiple_of(mine * piece, piece), piece)], up_out.at[mine], local_sems.at[6])
+        keep.start()
+        turns = [(lax.rem(me + dx, RING), lax.rem(c + dc, CORES)) for dx in range(RING) for dc in range(CORES)][1:]
+        for k, (x, core) in enumerate(turns):
+            to = x * CORES + core
+            s.start(34 + k, up_sum.at[pl.ds(pl.multiple_of(to * piece, piece), piece)], up_out.at[mine], p.dev(x=x, core=core))
     s.arrived(6, arriving.at[0, second], left)
     s.arrived(7, arriving.at[1, first], right)
     s.arrived(8, arriving.at[0, first], left)
     s.arrived(9, arriving.at[1, second], right)
     add_into(y_ref, arriving.at[0], arriving.at[1])
+    if backward:
+        for k in range(len(turns)):
+            dx, dc = divmod(k + 1, CORES)
+            x, core = lax.rem(me + RING - dx, RING), lax.rem(c + dc, CORES)
+            s.arrived(34 + k, up_out.at[x * CORES + core], p.dev(x=x, core=core))
+        keep.wait()
     s.drain()
 
 
-def scatter(h, w, transposed):
+def scatter(h, w, grads=None):
     rows, width = h.shape[2:]
-    hidden = w.shape[0] if transposed else w.shape[1]
-    vmem = pl.BlockSpec(memory_space=pltpu.VMEM)
+    hidden = w.shape[1] if grads is None else w.shape[0]
+    vmem, anywhere = pl.BlockSpec(memory_space=pltpu.VMEM), pl.BlockSpec(memory_space=pl.ANY)
     f32 = jnp.float32
+    outs = [jax.ShapeDtypeStruct((rows, hidden), f32)]
+    slots = 10
+    extra = []
+    if grads is not None:
+        up_rows, down_rows = grads[0].shape[2], grads[1].shape[2]
+        n_data = RING * CORES
+        outs += [jax.ShapeDtypeStruct((n_data, up_rows // n_data, width), f32), jax.ShapeDtypeStruct((down_rows, hidden), f32)]
+        slots = 10 + GradScatter.SLOTS + n_data - 1
+        extra = [pltpu.VMEM((up_rows, width), f32), pltpu.SemaphoreType.DMA((7,))] + GradScatter.buffers(*grads)
     return pl.pallas_call(
-        functools.partial(scatter_kernel, transposed),
-        out_shape=jax.ShapeDtypeStruct((rows, hidden), f32),
-        in_specs=[vmem] * 2,
-        out_specs=vmem,
+        scatter_kernel,
+        out_shape=outs,
+        in_specs=[vmem] * 2 + [anywhere] * (0 if grads is None else 2),
+        out_specs=[vmem] * len(outs),
         scratch_shapes=[pltpu.VMEM((RING, rows, hidden), f32), pltpu.VMEM((RING, rows, hidden), f32),
                         pltpu.VMEM((3, rows, hidden), f32), pltpu.VMEM((2, rows // 2, hidden), f32),
                         pltpu.VMEM((2, rows, hidden), f32),
-                        pltpu.SemaphoreType.DMA((10,)), pltpu.SemaphoreType.DMA((10,))],
-        compiler_params=pltpu.CompilerParams(collective_id=2 if transposed else 1, has_side_effects=True,
-                                             vmem_limit_bytes=48 * 1024 * 1024),
+                        pltpu.SemaphoreType.DMA((slots,)), pltpu.SemaphoreType.DMA((slots,))] + extra,
+        compiler_params=pltpu.CompilerParams(collective_id=1 if grads is None else 2, has_side_effects=True,
+                                             vmem_limit_bytes=(44 if grads is None else 62) * 1024 * 1024),
         cost_estimate=pl.CostEstimate(flops=0, bytes_accessed=240_000_000, transcendentals=0),
-        name="scatter_t" if transposed else "scatter",
-    )(h, w)
+        name="scatter" if grads is None else "scatter_grads",
+    )(h, w, *(grads or ()))
 
 
 def solution(mesh):
@@ -290,8 +429,8 @@
             xs, w1, w2 = gather(x.reshape(micro, rows, hidden), up[layer], down[layer])
             return xs.reshape(count, hidden), w1.reshape(hidden, width), w2.reshape(width, hidden)
 
-        def scattered(h, w, transposed):
-            return scatter(h.reshape(RING, CORES, own, width), w, transposed)
+        def blocks(h):
+            return h.reshape(RING, CORES, own, width)
 
         x_cur = tokens.reshape(own, hidden)
         saved = []
@@ -300,7 +439,7 @@
             u_all, w1, w2 = gathered(norm_f32(x_f32).astype(jnp.bfloat16), layer)
             pre = jnp.dot(u_all, w1, preferred_element_type=jnp.float32).astype(jnp.bfloat16)
             act = gelu_f32(pre.astype(jnp.float32)).astype(jnp.bfloat16)
-            y = scattered(act, w2, False)
+            y, = scatter(blocks(act), w2)
             saved.append((x_cur, u_all, pre, act))
             x_cur = (x_f32 + y).astype(jnp.bfloat16)
         x_final = x_cur
@@ -316,14 +455,12 @@
             z = jax.vjp(gelu_f32, pre.astype(jnp.float32))[1](e)[0].astype(jnp.bfloat16)
             d_w2 = jnp.einsum("tf,tm->fm", act, c_all, preferred_element_type=jnp.float32)
             d_w1 = jnp.einsum("tm,tf->mf", u_all, z, preferred_element_type=jnp.float32)
-            v = scattered(z, w1, True)
-            grads_up[layer] = lax.psum_scatter(d_w1, "local", scatter_dimension=0, tiled=True)
-            grads_down[layer] = lax.psum_scatter(d_w2, "local", scatter_dimension=0, tiled=True)[:down_rows]
+            g_up, g_down = (g.reshape((RING, RING, -1) + g.shape[1:]) for g in (d_w1, d_w2))
+            v, grads_up[layer], g_down = scatter(blocks(z), w1, (g_up, g_down))
+            grads_down[layer] = g_down[:down_rows]
             norm_pull = jax.vjp(norm_f32, x_in.astype(jnp.float32))[1]
             d_cur = (d_cur.astype(jnp.float32) + norm_pull(v)[0]).astype(jnp.bfloat16)
-        g_up = jnp.stack(grads_up).reshape(layers, n_data, up_rows, width).transpose(1, 0, 2, 3)
-        g_up = lax.all_to_all(g_up, "data", 0, 0)
-        g_up = g_up.reshape(n_data, layers, up_rows, n_local, PAD)[..., :down_rows]
+        g_up = jnp.stack(grads_up, 1).reshape(n_data, layers, up_rows, n_local, PAD)[..., :down_rows]
         g_up = g_up.transpose(1, 2, 3, 0, 4).reshape(layers, up_rows, ffn)
         shape = (micro, rows, hidden)
         return x_final.reshape(shape), d_cur.reshape(shape), g_up, jnp.stack(grads_down)

time: 785 us -> 694 us (0.88)
  waiting for transfers between devices: 134 us -> 5.07 us
  local copies, waits for them, and re-layouts: 16.6 us -> 52 us
  other arithmetic: 10.4 us -> 25.1 us
  between operations: 14.2 us -> 1.18 us
  Pallas kernels: 493 us -> 502 us
    reduce_scatter x4 -> x0, waiting for transfers between devices: 129 us -> none  [the longest x2 129 us: body(): lax.psum_scatter(d_w2, 'local', scatter_dimension=0, tiled=True)[:down_rows]]
    dot_general x0 -> x2, local copies, waits for them, and re-layouts: none -> 24.7 us  [body(): d_w1 = jnp.einsum('tm,tf->mf', u_all, z, preferred_element_type=jnp.float32)]
    pallas_call x4, Pallas kernels: 320 us -> 330 us  [scatter(): pl.pallas_call(scatter_kernel, out_shape=outs, in_specs=[vmem] * 2 + [any...]
    convert_element_type x0 -> x2, local copies, waits for them, and re-layouts: none -> 9.49 us  [body(): act = gelu_f32(pre.astype(jnp.float32)).astype(jnp.bfloat16)]
    convert_element_type x0 -> x2, other arithmetic: none -> 9.48 us  [body(): act = gelu_f32(pre.astype(jnp.float32)).astype(jnp.bfloat16)]
  transfers between devices with their start and end apart: 6 -> 1, of which waited for: 3 -> 1; matrix products, arithmetic and copies ran while one was open for 8% -> 0% of each run, Pallas kernels for 26% -> 0%
where the time goes in v3:
time: 694 us; the launch traced here: 690 us
  Pallas kernels  502 us (72%)
  matrix products  97.8 us (14%)
  local copies, waits for them, and re-layouts  52 us (7%)
  other arithmetic  25.1 us (4%)
    pallas_call x4, Pallas kernels, scatter(): pl.pallas_call(scatter_kernel, out_shape=outs, in_specs=[vmem] * 2 + [any...  330 us
    pallas_call x4, Pallas kernels, gather(): pl.pallas_call(gather_kernel, out_shape=[jax.ShapeDtypeStruct((RING, CORE...  173 us
    dot_general x2, matrix products, body(): e = jnp.einsum('tm,fm->tf', c_all, w2, preferred_element_type=jnp.float32)  27.4 us
    dot_general x2, local copies, waits for them, and re-layouts, body(): d_w1 = jnp.einsum('tm,tf->mf', u_all, z, preferred_element_type=jnp.float32)  24.7 us
    dot_general x2, matrix products, body(): jnp.dot(u_all, w1, preferred_element_type=jnp.float32).astype(jnp.bfloat16)  24.6 us
    dot_general x2, matrix products, body(): d_w1 = jnp.einsum('tm,tf->mf', u_all, z, preferred_element_type=jnp.float32)  23.8 us
    dot_general x2, matrix products, body(): jnp.einsum('tf,tm->fm', act, c_all, preferred_element_type=jnp.float32)  22 us
  transfers between devices with their start and end apart: 1, of which 1 were waited for; matrix products, arithmetic and copies ran while one was open for 0% of the time, Pallas kernels for 0%

profile of v3, /device:TPU:1, one launch (start us, length us, event | category | flops | bytes accessed | tf_op | source)
XLA Modules:
  0.0 689.6 jit_solution(11191912720908128956)
XLA Ops:
  0.7 4.1 reshape.151
  4.8 0.2 copy.24
  5.0 0.2 pad_bitcast_fusion
  5.2 2.0 reshape.152
  7.2 6.0 all-to-all-start
  13.2 0.3 fusion.53
  13.5 1.2 fusion.54.x_ref
  14.8 0.1 copy.25
  14.9 0.8 fusion.58
  15.7 5.1 all-to-all-done
  20.7 0.8 fusion.62
  21.5 45.6 %gather.4 = (bf16[4,2,2,128,2048]{4,3,2,1,0:T(8,128)(2,1)}, bf16[4,4,128,768]{3,2,1,0:T(8,128)(2,1)}, bf16[4,4,48,2048]{3,2,1,0:T(8,128)(2,1)}) custom-call(bf16[2,128,2048]{2,1,0:T(8,128)(2,1)} %fusion.54.x_ref, bf16[128,768]{1,0:T(8,128)(2,1)} %bitcast.174, bf16[48,2048]{1,0:T(8,128)(2,1)} %get-tuple-element.59.down_ref), custom_call_target="tpu_custom_call" | custom-call | bytes 120000000 | tf_op jit(solution)/shard_map/gather/pallas_call | solution.py:164
  67.2 12.3 %fusion.31 = (bf16[2048,768]{1,0:T(8,128)(2,1)S(1)}, bf16[2048,768]{1,0:T(8,128)(2,1)}) fusion(bf16[2048,2048]{1,0:T(8,128)(2,1)} %bitcast.160, bf16[2048,768]{1,0:T(8,128)(2,1)} %bitcast.187), kind=kOutput, calls=%fused_computation.43 | convolution fusion | flops 6459752448 | bytes 17825792 | tf_op jit(solution)/shard_map/dot_general | solution.py:440
  79.4 77.6 %scatter.2 = f32[256,2048]{1,0:T(8,128)S(1)} custom-call(bf16[4,2,256,768]{3,2,1,0:T(8,128)(2,1)S(1)} %bitcast.157, bf16[768,2048]{1,0:T(8,128)(2,1)S(1)} %bitcast.155), custom_call_target="tpu_custom_call" | custom-call | bytes 240000000 | tf_op jit(solution)/shard_map/scatter/pallas_call | solution.py:392
  157.0 0.4 fusion.48
  157.4 1.3 fusion.49
  158.7 42.7 %gather.5 = (bf16[4,2,2,128,2048]{4,3,2,1,0:T(8,128)(2,1)}, bf16[4,4,128,768]{3,2,1,0:T(8,128)(2,1)}, bf16[4,4,48,2048]{3,2,1,0:T(8,128)(2,1)}) custom-call(bf16[2,128,2048]{2,1,0:T(8,128)(2,1)} %bitcast.167, bf16[128,768]{1,0:T(8,128)(2,1)} %bitcast.176, bf16[48,2048]{1,0:T(8,128)(2,1)} %get-tuple-element.58.down_ref), custom_call_target="tpu_custom_call" | custom-call | bytes 120000000 | tf_op jit(solution)/shard_map/gather/pallas_call | solution.py:164
  201.4 12.3 %fusion.37 = (bf16[2048,768]{1,0:T(8,128)(2,1)S(1)}, bf16[2048,768]{1,0:T(8,128)(2,1)}) fusion(bf16[2048,2048]{1,0:T(8,128)(2,1)} %bitcast.162, bf16[2048,768]{1,0:T(8,128)(2,1)} %bitcast.188), kind=kOutput, calls=%fused_computation.49 | convolution fusion | flops 6459752448 | bytes 17825792 | tf_op jit(solution)/shard_map/dot_general | solution.py:440
  213.7 77.8 %scatter.3 = f32[256,2048]{1,0:T(8,128)S(1)} custom-call(bf16[4,2,256,768]{3,2,1,0:T(8,128)(2,1)S(1)} %bitcast.158, bf16[768,2048]{1,0:T(8,128)(2,1)S(1)} %bitcast.156), custom_call_target="tpu_custom_call" | custom-call | bytes 240000000 | tf_op jit(solution)/shard_map/scatter/pallas_call | solution.py:392
  291.6 1.3 fusion.50
  292.8 42.2 %gather.6 = (bf16[4,2,2,128,2048]{4,3,2,1,0:T(8,128)(2,1)}, bf16[4,4,128,768]{3,2,1,0:T(8,128)(2,1)}, bf16[4,4,48,2048]{3,2,1,0:T(8,128)(2,1)}) custom-call(bf16[2,128,2048]{2,1,0:T(8,128)(2,1)} %param.5, bf16[128,768]{1,0:T(8,128)(2,1)} %bitcast.177, bf16[48,2048]{1,0:T(8,128)(2,1)} %get-tuple-element.58.down_ref), custom_call_target="tpu_custom_call" | custom-call | bytes 120000000 | tf_op jit(solution)/shard_map/gather/pallas_call | solution.py:164
  335.1 12.3 %copy.26 = bf16[2048,2048]{1,0:T(8,128)(2,1)} copy(bf16[2048,2048]{0,1:T(8,128)(2,1)} %bitcast.163) | data formatting | bytes 16777216 | tf_op jit(solution)/shard_map/tm,tf->mf/dot_general | solution.py:457
  347.4 4.7 fusion.21
  352.1 4.8 copy.27
  356.9 13.6 %fusion.12 = bf16[2048,768]{1,0:T(8,128)(2,1)S(1)} fusion(bf16[2048,768]{1,0:T(8,128)(2,1)} %get-tuple-element.67, bf16[2048,2048]{1,0:T(8,128)(2,1)} %bitcast.181, bf16[768,2048]{1,0:T(8,128)(2,1)} %bitcast.185), kind=kOutput, calls=%fused_computation.24 | convolution fusion | flops 6475481088 | bytes 17825792 | tf_op jit(solution)/shard_map/tm,fm->tf/dot_general | solution.py:454
  370.6 11.9 %fusion.42.refs_0_ = f32[4,4,128,768]{3,2,1,0:T(8,128)} fusion(bf16[4,4,128,2048]{3,2,1,0:T(8,128)(2,1)} %bitcast.164, bf16[2048,768]{1,0:T(8,128)(2,1)S(1)} %fusion.12), kind=kOutput, calls=%fused_computation.61 | convolution fusion | flops 6442450944 | bytes 17825792 | tf_op jit(solution)/shard_map/tm,tf->mf/dot_general | solution.py:457
  382.5 11.2 %fusion.63.refs_1_ = f32[4,4,48,2048]{3,2,1,0:T(8,128)} fusion(bf16[4,4,48,2048]{3,2,1,0:T(8,128)(2,1)S(1)} %bitcast.172, bf16[2048,2048,1,1]{1,0,3,2:T(8,128)(2,1)} %bitcast.182), kind=kOutput, calls=%fused_computation.101 | convolution fusion | flops 6442450944 | bytes 17825792 | tf_op jit(solution)/shard_map/tf,tm->fm/dot_general | solution.py:456
  393.7 87.1 %scatter_grads.2 = (f32[256,2048]{1,0:T(8,128)}, f32[8,16,768]{2,1,0:T(8,128)}, f32[48,2048]{1,0:T(8,128)}) custom-call(bf16[4,2,256,768]{3,2,1,0:T(8,128)(2,1)} %bitcast.170, bf16[2048,768]{1,0:T(8,128)(2,1)} %bitcast.168, f32[4,4,128,768]{3,2,1,0:T(8,128)} %fusion.42.refs_0_, f32[4,4,48,2048]{3,2,1,0:T(8,128)} %fusion.63.refs_1_), custom_call_target="tpu_custom_call" | custom-call | bytes 240000000 | tf_op jit(solution)/shard_map/scatter_grads/pallas_call | solution.py:392
  480.8 2.1 fusion.51
  482.9 3.7 fusion.45
  486.7 42.2 %gather.7 = (bf16[4,2,2,128,2048]{4,3,2,1,0:T(8,128)(2,1)}, bf16[4,4,128,768]{3,2,1,0:T(8,128)(2,1)}, bf16[4,4,48,2048]{3,2,1,0:T(8,128)(2,1)}) custom-call(bf16[2,128,2048]{2,1,0:T(8,128)(2,1)} %bitcast.159, bf16[128,768]{1,0:T(8,128)(2,1)} %bitcast.175, bf16[48,2048]{1,0:T(8,128)(2,1)} %get-tuple-element.59.down_ref), custom_call_target="tpu_custom_call" | custom-call | bytes 120000000 | tf_op jit(solution)/shard_map/gather/pallas_call | solution.py:164
  528.9 12.3 %copy.28 = bf16[2048,2048]{1,0:T(8,128)(2,1)} copy(bf16[2048,2048]{0,1:T(8,128)(2,1)} %bitcast.161) | data formatting | bytes 16777216 | tf_op jit(solution)/shard_map/tm,tf->mf/dot_general | solution.py:457
  541.2 4.8 fusion.27
  546.0 4.7 copy.29
  550.7 13.8 %fusion.15 = bf16[2048,768]{1,0:T(8,128)(2,1)S(1)} fusion(bf16[2048,768]{1,0:T(8,128)(2,1)} %get-tuple-element.65, bf16[2048,2048]{1,0:T(8,128)(2,1)} %bitcast.183, bf16[768,2048]{1,0:T(8,128)(2,1)} %bitcast.186), kind=kOutput, calls=%fused_computation.27 | convolution fusion | flops 6475481088 | bytes 17825792 | tf_op jit(solution)/shard_map/tm,fm->tf/dot_general | solution.py:454
  564.5 11.9 %fusion.40.refs_0_ = f32[4,4,128,768]{3,2,1,0:T(8,128)} fusion(bf16[4,4,128,2048]{3,2,1,0:T(8,128)(2,1)} %bitcast.165, bf16[2048,768]{1,0:T(8,128)(2,1)S(1)} %fusion.15), kind=kOutput, calls=%fused_computation.59 | convolution fusion | flops 6442450944 | bytes 17825792 | tf_op jit(solution)/shard_map/tm,tf->mf/dot_general | solution.py:457
  576.5 10.8 %fusion.64.refs_1_ = f32[4,4,48,2048]{3,2,1,0:T(8,128)} fusion(bf16[4,4,48,2048]{3,2,1,0:T(8,128)(2,1)S(1)} %bitcast.173, bf16[2048,2048,1,1]{1,0,3,2:T(8,128)(2,1)} %bitcast.184), kind=kOutput, calls=%fused_computation.102 | convolution fusion | flops 6442450944 | bytes 17825792 | tf_op jit(solution)/shard_map/tf,tm->fm/dot_general | solution.py:456
  587.2 87.1 %scatter_grads.3 = (f32[256,2048]{1,0:T(8,128)}, f32[8,16,768]{2,1,0:T(8,128)}, f32[48,2048]{1,0:T(8,128)}) custom-call(bf16[4,2,256,768]{3,2,1,0:T(8,128)(2,1)} %bitcast.171, bf16[2048,768]{1,0:T(8,128)(2,1)} %bitcast.169, f32[4,4,128,768]{3,2,1,0:T(8,128)} %fusion.40.refs_0_, f32[4,4,48,2048]{3,2,1,0:T(8,128)} %fusion.64.refs_1_), custom_call_target="tpu_custom_call" | custom-call | bytes 240000000 | tf_op jit(solution)/shard_map/scatter_grads/pallas_call | solution.py:392
  674.4 1.9 fusion.56
  676.3 0.5 stack.19
  676.8 1.6 stack.18
  678.4 0.2 fusion.52
  678.6 2.5 copy.30
  681.2 3.5 reshape.174
  684.7 0.1 slice_bitcast_fusion
  684.7 0.1 pad_maximum_fusion.1
  684.8 1.4 copy.31
  686.2 3.1 fusion.47
  (34 shorter events, 0.1 us)
Async XLA Ops:
  0.6 12.6 %copy-start.2 = (bf16[2,128,2048]{2,1,0:T(8,128)(2,1)S(1)}, bf16[2,128,2048]{2,1,0:T(8,128)(2,1)}, u32[]{:S(2)}) copy-start(bf16[2,128,2048]{2,1,0:T(8,128)(2,1)} %param.4) | copy-start | bytes 3145732
  0.6 14.1 %copy-start.12 = (bf16[2,44,2048]{2,0,1:T(2,128)(2,1)S(1)}, bf16[2,44,2048]{2,0,1:T(2,128)(2,1)}, u32[]{:S(2)}) copy-start(bf16[2,44,2048]{2,0,1:T(2,128)(2,1)} %param.7) | copy-start | bytes 1081348
  7.2 13.5 %all-to-all-start = ((bf16[8,2,16,768]{3,2,1,0:T(8,128)(2,1)}), bf16[8,2,16,768]{3,2,1,0:T(8,128)(2,1)S(1)}, u32[]{:S(2)}, u32[]{:S(2)}) async-start(bf16[8,2,16,768]{3,2,1,0:T(8,128)(2,1)} %reshape.152), calls=%async_computation | async-start | bytes 786432 | tf_op jit(solution)/shard_map/all_to_all | solution.py:424
  13.5 65.9 %copy-start.13 = (f32[2,128]{1,0:T(2,128)}, f32[2,128]{1,0:T(2,128)S(1)}, u32[]{:S(2)}) copy-start(f32[2,128]{1,0:T(2,128)S(1)} %fusion.53) | copy-start | bytes 3076
  67.1 12.3 %copy-start = (bf16[4,4,48,2048]{3,2,1,0:T(8,128)(2,1)S(1)}, bf16[4,4,48,2048]{3,2,1,0:T(8,128)(2,1)}, u32[]{:S(2)}) copy-start(bf16[4,4,48,2048]{3,2,1,0:T(8,128)(2,1)} %get-tuple-element.26) | copy-start | bytes 9437188
  157.4 134.1 %copy-start.3 = (bf16[256,2048]{1,0:T(8,128)(2,1)}, bf16[256,2048]{1,0:T(8,128)(2,1)S(1)}, u32[]{:S(2)}) copy-start(bf16[256,2048]{1,0:T(8,128)(2,1)S(1)} %get-tuple-element.57) | copy-start | bytes 3145732
  201.4 12.3 %copy-start.1 = (bf16[4,4,48,2048]{3,2,1,0:T(8,128)(2,1)S(1)}, bf16[4,4,48,2048]{3,2,1,0:T(8,128)(2,1)}, u32[]{:S(2)}) copy-start(bf16[4,4,48,2048]{3,2,1,0:T(8,128)(2,1)} %get-tuple-element.29) | copy-start | bytes 9437188
  370.5 11.9 %copy-start.5 = (bf16[2048,768]{1,0:T(8,128)(2,1)}, bf16[2048,768]{1,0:T(8,128)(2,1)S(1)}, u32[]{:S(2)}) copy-start(bf16[2048,768]{1,0:T(8,128)(2,1)S(1)} %fusion.12) | copy-start | bytes 9437188
  370.5 11.9 %copy-start.7 = (bf16[768,2048]{1,0:T(8,128)(2,1)S(1)}, bf16[768,2048]{1,0:T(8,128)(2,1)}, u32[]{:S(2)}) copy-start(bf16[768,2048]{1,0:T(8,128)(2,1)} %copy.27) | copy-start | bytes 9437188
  564.5 11.9 %copy-start.6 = (bf16[2048,768]{1,0:T(8,128)(2,1)}, bf16[2048,768]{1,0:T(8,128)(2,1)S(1)}, u32[]{:S(2)}) copy-start(bf16[2048,768]{1,0:T(8,128)(2,1)S(1)} %fusion.15) | copy-start | bytes 9437188
  564.5 11.9 %copy-start.8 = (bf16[768,2048]{1,0:T(8,128)(2,1)S(1)}, bf16[768,2048]{1,0:T(8,128)(2,1)}, u32[]{:S(2)}) copy-start(bf16[768,2048]{1,0:T(8,128)(2,1)} %copy.29) | copy-start | bytes 9437188
  587.2 89.0 %copy-start.14 = (f32[2,128]{1,0:T(2,128)S(1)}, f32[2,128]{1,0:T(2,128)}, u32[]{:S(2)}) copy-start(f32[2,128]{1,0:T(2,128)} %copy-done.13) | copy-start | bytes 3076
  587.2 89.0 %copy-start.10 = (f32[8,16,768]{2,1,0:T(8,128)S(1)}, f32[8,16,768]{2,1,0:T(8,128)}, u32[]{:S(2)}) copy-start(f32[8,16,768]{2,1,0:T(8,128)} %get-tuple-element.41) | copy-start | bytes 1179652
  676.8 7.9 %copy-start.9 = (f32[48,2048]{1,0:T(8,128)S(1)}, f32[48,2048]{1,0:T(8,128)}, u32[]{:S(2)}) copy-start(f32[48,2048]{1,0:T(8,128)} %get-tuple-element.43) | copy-start | bytes 1179652
  678.6 6.1 copy-start.11
  678.6 7.6 %copy-start.4 = (bf16[256,2048]{1,0:T(8,128)(2,1)S(1)}, bf16[256,2048]{1,0:T(8,128)(2,1)}, u32[]{:S(2)}) copy-start(bf16[256,2048]{1,0:T(8,128)(2,1)} %fusion.45) | copy-start | bytes 3145732

commit v4 on v3

--- a/solution.py
+++ b/solution.py
@@ -99,80 +99,227 @@
         self.s.arrived(self.base + 5, self.block(self.far, 1), self.right)
 
 
-def gather_kernel(x_ref, up_ref, down_ref, xs_ref, w1_ref, w2_ref, send_sems, recv_sems, local_sems):
-    p = Place()
-    ring_x, ring_y, ring_z = p.along("x"), p.along("y"), p.along("z")
-    sib, c, o = p.sibling(), p.core, 1 - p.core
-    keep = [pltpu.make_async_copy(x_ref, xs_ref.at[p.x, c], local_sems.at[0]),
-            pltpu.make_async_copy(up_ref, w1_ref.at[p.z, p.y], local_sems.at[1]),
-            pltpu.make_async_copy(down_ref, w2_ref.at[p.z, p.y], local_sems.at[2])]
-    for copy in keep:
+class WeightGather:
+    def __init__(self, p, sender, base, src, dst):
+        ring_y, ring_z = p.along("y"), p.along("z")
+        rows, cols = src.shape
+        if rows >= 64:
+            quarter = rows // 4
+            sub = lambda part, h: (pl.ds((2 * part + h) * quarter, quarter), slice(None))
+        else:
+            quarter = cols // 4
+            sub = lambda part, h: (slice(None), pl.ds((2 * part + h) * quarter, quarter))
+        block2 = (lambda i, h: dst.at[(i, slice(None)) + sub(0, h)], lambda i, h: dst.at[(slice(None), i) + sub(1, h)])
+        self.stage1 = (RingGather(sender, base, ring_y, lambda h: src.at[sub(0, h)], lambda i, h: dst.at[(p.z, i) + sub(0, h)]),
+                       RingGather(sender, base + 6, ring_z, lambda h: src.at[sub(1, h)], lambda i, h: dst.at[(i, p.y) + sub(1, h)]))
+        self.stage2 = (RingGather(sender, base + 12, ring_z, lambda h: block2[0](p.z, h), block2[0]),
+                       RingGather(sender, base + 18, ring_y, lambda h: block2[1](p.y, h), block2[1]))
+
+    def start(self):
+        for g in self.stage1:
+            g.start()
+
+    def second(self, keep=None):
+        for g in self.stage1:
+            g.relay()
+        for g in self.stage1:
+            g.near()
+            g.finish()
+        if keep is not None:
+            keep.wait()
+        for g in self.stage2:
+            g.start()
+
+    def relay(self):
+        for g in self.stage2:
+            g.relay()
+
+    def finish(self):
+        for g in self.stage2:
+            g.near()
+            g.finish()
+
+
+class Exchange:
+    SLOTS = 62
+
+    def __init__(self, x_ref, xs, first, first_dst, second, second_dst, send_sems, recv_sems, keep_sem):
+        p = Place()
+        ring_x, ring_y, ring_z = p.along("x"), p.along("y"), p.along("z")
+        self.p, self.sib, self.xs, self.x_ref = p, p.sibling(), xs, x_ref
+        c = p.core
+        self.keep = pltpu.make_async_copy(second, second_dst.at[p.z, p.y], keep_sem)
+        self.keep.start()
+        first_dst[p.z, p.y] = first[...]
+        xs[p.x, c] = x_ref[...]
+        greet([ring_x[1], ring_x[2], ring_y[1], ring_y[2], ring_z[1], ring_z[2], self.sib])
+        self.s = Sender(send_sems, recv_sems)
+        self.gx = RingGather(self.s, 0, ring_x, lambda h: x_ref.at[h], lambda i, h: xs.at[i, c, h])
+        self.first = WeightGather(p, self.s, 14, first, first_dst)
+        self.second = WeightGather(p, self.s, 38, second, second_dst)
+
+    def give(self, k, i, h, src=None):
+        at = self.xs.at[i, self.p.core, h]
+        self.s.start(6 + k, at if src is None else src, at, self.sib)
+
+    def take(self, k, i, h):
+        self.s.arrived(6 + k, self.xs.at[i, 1 - self.p.core, h], self.sib)
+
+    def run(self, compute):
+        gx, me = self.gx, self.p.x
+        self.first.start()
+        gx.start()
+        for h in (0, 1):
+            self.give(h, me, h, self.x_ref.at[h])
+        self.second.start()
+        self.first.second()
+        self.second.second(self.keep)
+        gx.relay()
+        self.give(2, gx.prev, 0)
+        self.give(3, gx.next, 1)
+        self.first.relay()
+        self.first.finish()
+        self.second.relay()
+        self.take(0, me, 0)
+        self.take(1, me, 1)
+        compute(me, True)
+        gx.near()
+        self.give(4, gx.prev, 1)
+        self.give(5, gx.next, 0)
+        self.take(2, gx.prev, 0)
+        self.take(4, gx.prev, 1)
+        compute(gx.prev, False)
+        self.take(3, gx.next, 1)
+        self.take(5, gx.next, 0)
+        gx.finish()
+        self.give(6, gx.far, 0)
+        self.give(7, gx.far, 1)
+        compute(gx.next, False)
+        self.take(6, gx.far, 0)
+        self.take(7, gx.far, 1)
+        compute(gx.far, False)
+        self.second.finish()
+        self.s.drain()
+
+
+def up_kernel(x_ref, up_ref, down_ref, u_ref, pre_ref, act_ref, w2_ref, xs, w1, wide, send_sems, recv_sems, sems):
+    saves = []
+    hidden, width = xs.shape[-1], w1.shape[-1]
+    ex = Exchange(x_ref, xs, up_ref, w1, down_ref, w2_ref, send_sems, recv_sems, sems.at[0])
+
+    def compute(i, _):
+        save = pltpu.make_async_copy(xs.at[i], u_ref.at[i], sems.at[1 + len(saves)])
+        save.start()
+        saves.append(save)
+        wide[...] = jnp.dot(xs[i].reshape(wide.shape[0], hidden), w1[...].reshape(hidden, width),
+                            preferred_element_type=jnp.float32)
+
+        @pl.loop(0, wide.shape[0] // 32)
+        def _(r):
+            at = pl.ds(pl.multiple_of(r * 32, 32), 32)
+            pre = wide[at, :].astype(jnp.bfloat16)
+            pre_ref[i, at, :] = pre
+            act_ref[i, at, :] = gelu_f32(pre.astype(jnp.float32)).astype(jnp.bfloat16)
+
+    ex.run(compute)
+    for save in saves:
+        save.wait()
+
+
+def gather_up(x, up, down):
+    vmem, anywhere = pl.BlockSpec(memory_space=pltpu.VMEM), pl.BlockSpec(memory_space=pl.ANY)
+    micro, rows, hidden = x.shape
+    block = CORES * micro * rows
+    bf16, dma = jnp.bfloat16, pltpu.SemaphoreType.DMA
+    return pl.pallas_call(
+        up_kernel,
+        out_shape=[jax.ShapeDtypeStruct((RING, CORES) + x.shape, bf16),
+                   jax.ShapeDtypeStruct((RING, block, up.shape[1]), bf16),
+                   jax.ShapeDtypeStruct((RING, block, up.shape[1]), bf16),
+                   jax.ShapeDtypeStruct((RING, RING) + down.shape, bf16)],
+        in_specs=[vmem] * 3,
+        out_specs=[anywhere, vmem, vmem, anywhere],
+        scratch_shapes=[pltpu.VMEM((RING, CORES) + x.shape, bf16), pltpu.VMEM((RING, RING) + up.shape, bf16),
+                        pltpu.VMEM((block, up.shape[1]), jnp.float32),
+                        dma((Exchange.SLOTS,)), dma((Exchange.SLOTS,)), dma((5,))],
+        compiler_params=pltpu.CompilerParams(collective_id=0, has_side_effects=True, vmem_limit_bytes=40 * 1024 * 1024),
+        cost_estimate=pl.CostEstimate(flops=0, bytes_accessed=120_000_000, transcendentals=0),
+        name="gather_up",
+    )(x, up, down)
+
+
+def back_kernel(x_ref, up_ref, down_ref, u_hbm, pre_hbm, act_hbm, z_ref, w1_ref, g_up, g_down,
+                xs, w2, wide, us, pres, acts, acc_up, acc_down, send_sems, recv_sems, sems):
+    loads = [pltpu.make_async_copy(src, dst, sems.at[1 + k])
+             for k, (src, dst) in enumerate(((pre_hbm, pres), (act_hbm, acts), (u_hbm, us)))]
+    for load in loads:
+        load.start()
+    hidden, width = xs.shape[-1], z_ref.shape[-1]
+    block = wide.shape[0]
+    ex = Exchange(x_ref, xs, down_ref, w2, up_ref, w1_ref, send_sems, recv_sems, sems.at[0])
+    over_rows = (((0,), (0,)), ((), ()))
+
+    def compute(i, initial):
+        if initial:
+            for load in loads:
+                load.wait()
+        wide[...] = lax.dot_general(xs[i].reshape(block, hidden), w2[...].reshape(width, hidden), (((1,), (1,)), ((), ())),
+                                    preferred_element_type=jnp.float32)
+
+        @pl.loop(0, block // 32)
+        def _(r):
+            at = pl.ds(pl.multiple_of(r * 32, 32), 32)
+            pull = jax.vjp(gelu_f32, pres[i, at, :].astype(jnp.float32))[1]
+            z_ref[i, at, :] = pull(wide[at, :])[0].astype(jnp.bfloat16)
+
+        step = 512
+
+        @pl.loop(0, hidden // step)
+        def _(n):
+            at = pl.ds(pl.multiple_of(n * step, step), step)
+            d_down = lax.dot_general(acts[i], xs.at[i, :, :, :, at][...].reshape(block, step), over_rows,
+                                     preferred_element_type=jnp.float32)
+            d_up = lax.dot_general(z_ref[i], us.at[i, :, :, :, at][...].reshape(block, step), over_rows,
+                                   preferred_element_type=jnp.float32)
+            if initial:
+                acc_down[:, at] = d_down
+                acc_up[:, at] = d_up
+            else:
+                acc_down[:, at] += d_down
+                acc_up[:, at] += d_up
+
+    ex.run(compute)
+    cols, rows = g_up.shape[3], g_down.shape[2]
+    copies = []
+    for k in range(RING * RING):
+        copies.append(pltpu.make_async_copy(acc_up.at[:, pl.ds(k * cols, cols)], g_up.at[k // RING, k % RING], sems.at[4 + k]))
+        copies.append(pltpu.make_async_copy(acc_down.at[pl.ds(k * rows, rows)], g_down.at[k // RING, k % RING], sems.at[20 + k]))
+    for copy in copies:
         copy.start()
-    greet([ring_x[1], ring_x[2], ring_y[1], ring_y[2], ring_z[1], ring_z[2], sib])
-    s = Sender(send_sems, recv_sems)
-    rows, cols = up_ref.shape[0] // 2, down_ref.shape[1] // 2
-    gx = RingGather(s, 0, ring_x, lambda h: x_ref.at[h], lambda i, h: xs_ref.at[i, c, h])
-    up1 = RingGather(s, 6, ring_y, lambda h: up_ref.at[pl.ds(h * rows, rows)],
-                     lambda i, h: w1_ref.at[p.z, i, pl.ds(h * rows, rows)])
-    down1 = RingGather(s, 12, ring_z, lambda h: down_ref.at[:, pl.ds(h * cols, cols)],
-                       lambda i, h: w2_ref.at[i, p.y, :, pl.ds(h * cols, cols)])
-    up2 = RingGather(s, 18, ring_z, lambda h: w1_ref.at[p.z, pl.ds(2 * h, 2)],
-                     lambda i, h: w1_ref.at[i, pl.ds(2 * h, 2)])
-    down2 = RingGather(s, 24, ring_y, lambda h: w2_ref.at[pl.ds(2 * h, 2), p.y],
-                       lambda i, h: w2_ref.at[pl.ds(2 * h, 2), i])
-
-    def to_sibling(k, i, h, src=None):
-        s.start(30 + k, xs_ref.at[i, c, h] if src is None else src, xs_ref.at[i, c, h], sib)
-
-    up1.start()
-    down1.start()
-    gx.start()
-    for h in (0, 1):
-        to_sibling(h, p.x, h, x_ref.at[h])
-    up1.relay()
-    down1.relay()
-    up1.near()
-    down1.near()
-    up1.finish()
-    down1.finish()
-    for copy in keep:
+    for copy in copies:
         copy.wait()
-    up2.start()
-    down2.start()
-    gx.relay()
-    to_sibling(2, gx.prev, 0)
-    to_sibling(3, gx.next, 1)
-    up2.relay()
-    down2.relay()
-    gx.near()
-    to_sibling(4, gx.prev, 1)
-    to_sibling(5, gx.next, 0)
-    up2.near()
-    down2.near()
-    up2.finish()
-    down2.finish()
-    gx.finish()
-    to_sibling(6, gx.far, 0)
-    to_sibling(7, gx.far, 1)
-    for k, (i, h) in enumerate(((p.x, 0), (p.x, 1), (gx.prev, 0), (gx.next, 1), (gx.prev, 1), (gx.next, 0), (gx.far, 0), (gx.far, 1))):
-        s.arrived(30 + k, xs_ref.at[i, o, h], sib)
-    s.drain()
-
-
-def gather(x, up, down):
+
+
+def gather_back(x, up, down, u_all, pre, act):
     vmem, anywhere = pl.BlockSpec(memory_space=pltpu.VMEM), pl.BlockSpec(memory_space=pl.ANY)
+    hidden, width = x.shape[-1], up.shape[1]
+    bf16, f32, dma = jnp.bfloat16, jnp.float32, pltpu.SemaphoreType.DMA
     return pl.pallas_call(
-        gather_kernel,
-        out_shape=[jax.ShapeDtypeStruct((RING, CORES) + x.shape, x.dtype),
-                   jax.ShapeDtypeStruct((RING, RING) + up.shape, up.dtype),
-                   jax.ShapeDtypeStruct((RING, RING) + down.shape, down.dtype)],
-        in_specs=[vmem] * 3,
-        out_specs=[anywhere] * 3,
-        scratch_shapes=[pltpu.SemaphoreType.DMA((38,)), pltpu.SemaphoreType.DMA((38,)), pltpu.SemaphoreType.DMA((3,))],
-        compiler_params=pltpu.CompilerParams(collective_id=0, has_side_effects=True),
-        cost_estimate=pl.CostEstimate(flops=0, bytes_accessed=120_000_000, transcendentals=0),
-        name="gather",
-    )(x, up, down)
+        back_kernel,
+        out_shape=[jax.ShapeDtypeStruct(pre.shape, bf16),
+                   jax.ShapeDtypeStruct((RING, RING) + up.shape, bf16),
+                   jax.ShapeDtypeStruct((RING, RING, width, hidden // (RING * RING)), f32),
+                   jax.ShapeDtypeStruct((RING, RING) + down.shape, f32)],
+        in_specs=[vmem] * 3 + [anywhere] * 3,
+        out_specs=[vmem] + [anywhere] * 3,
+        scratch_shapes=[pltpu.VMEM((RING, CORES) + x.shape, bf16), pltpu.VMEM((RING, RING) + down.shape, bf16),
+                        pltpu.VMEM(pre.shape[1:], f32), pltpu.VMEM(u_all.shape, bf16), pltpu.VMEM(pre.shape, bf16),
+                        pltpu.VMEM(act.shape, bf16), pltpu.VMEM((width, hidden), f32), pltpu.VMEM((width, hidden), f32),
+                        dma((Exchange.SLOTS,)), dma((Exchange.SLOTS,)), dma((36,))],
+        compiler_params=pltpu.CompilerParams(collective_id=3, has_side_effects=True, vmem_limit_bytes=60 * 1024 * 1024),
+        cost_estimate=pl.CostEstimate(flops=0, bytes_accessed=150_000_000, transcendentals=0),
+        name="gather_back",
+    )(x, up, down, u_all, pre, act)
 
 
 def add_into(dst, *terms):
@@ -272,7 +419,7 @@
     def finish(self, up_out, down_out):
         self.up2.finish()
         self.down2.finish()
-        up_out[...] = self.u_own[self.up2.me] + self.u_arr2[0] + self.u_arr2[1]
+        up_out[...] = (self.u_own[self.up2.me] + self.u_arr2[0] + self.u_arr2[1]).T
         down_out[...] = self.d_own[self.down2.me] + self.d_arr2[0] + self.d_arr2[1]
 
     @staticmethod
@@ -384,7 +531,7 @@
     slots = 10
     extra = []
     if grads is not None:
-        up_rows, down_rows = grads[0].shape[2], grads[1].shape[2]
+        up_rows, down_rows = grads[0].shape[3], grads[1].shape[2]
         n_data = RING * CORES
         outs += [jax.ShapeDtypeStruct((n_data, up_rows // n_data, width), f32), jax.ShapeDtypeStruct((down_rows, hidden), f32)]
         slots = 10 + GradScatter.SLOTS + n_data - 1
@@ -416,7 +563,6 @@
         pad = PAD - down_rows
         width = n_local * PAD
         own = micro * rows
-        count = n_data * own
 
         up = w_up.reshape(layers, up_rows, n_local, n_data, down_rows)
         up = jnp.pad(up, ((0, 0),) * 4 + ((0, pad),))
@@ -425,9 +571,8 @@
         up = up.transpose(1, 0, 2, 3).reshape(layers, n_data * up_rows, width)
         down = jnp.pad(w_down, ((0, 0), (0, pad), (0, 0)))
 
-        def gathered(x, layer):
-            xs, w1, w2 = gather(x.reshape(micro, rows, hidden), up[layer], down[layer])
-            return xs.reshape(count, hidden), w1.reshape(hidden, width), w2.reshape(width, hidden)
+        def shaped(x):
+            return x.reshape(micro, rows, hidden)
 
         def blocks(h):
             return h.reshape(RING, CORES, own, width)
@@ -436,10 +581,9 @@
         saved = []
         for layer in range(layers):
             x_f32 = x_cur.astype(jnp.float32)
-            u_all, w1, w2 = gathered(norm_f32(x_f32).astype(jnp.bfloat16), layer)
-            pre = jnp.dot(u_all, w1, preferred_element_type=jnp.float32).astype(jnp.bfloat16)
-            act = gelu_f32(pre.astype(jnp.float32)).astype(jnp.bfloat16)
-            y, = scatter(blocks(act), w2)
+            normed = norm_f32(x_f32).astype(jnp.bfloat16)
+            u_all, pre, act, w2 = gather_up(shaped(normed), up[layer], down[layer])
+            y, = scatter(blocks(act), w2.reshape(width, hidden))
             saved.append((x_cur, u_all, pre, act))
             x_cur = (x_f32 + y).astype(jnp.bfloat16)
         x_final = x_cur
@@ -450,13 +594,8 @@
         grads_down = [None] * layers
         for layer in reversed(range(layers)):
             x_in, u_all, pre, act = saved[layer]
-            c_all, w1, w2 = gathered(d_cur, layer)
-            e = jnp.einsum("tm,fm->tf", c_all, w2, preferred_element_type=jnp.float32)
-            z = jax.vjp(gelu_f32, pre.astype(jnp.float32))[1](e)[0].astype(jnp.bfloat16)
-            d_w2 = jnp.einsum("tf,tm->fm", act, c_all, preferred_element_type=jnp.float32)
-            d_w1 = jnp.einsum("tm,tf->mf", u_all, z, preferred_element_type=jnp.float32)
-            g_up, g_down = (g.reshape((RING, RING, -1) + g.shape[1:]) for g in (d_w1, d_w2))
-            v, grads_up[layer], g_down = scatter(blocks(z), w1, (g_up, g_down))
+            z, w1, g_up, g_down = gather_back(shaped(d_cur), up[layer], down[layer], u_all, pre, act)
+            v, grads_up[layer], g_down = scatter(blocks(z), w1.reshape(hidden, width), (g_up, g_down))
             grads_down[layer] = g_down[:down_rows]
             norm_pull = jax.vjp(norm_f32, x_in.astype(jnp.float32))[1]
             d_cur = (d_cur.astype(jnp.float32) + norm_pull(v)[0]).astype(jnp.bfloat16)

time: 694 us -> 631 us (0.909)
  matrix products: 97.8 us -> 0 us
  Pallas kernels: 502 us -> 580 us
  local copies, waits for them, and re-layouts: 52 us -> 21 us
  other arithmetic: 25.1 us -> 12.6 us
    dot_general x8 -> x0, matrix products: 97.8 us -> none  [the longest x2 27.4 us: body(): e = jnp.einsum('tm,fm->tf', c_all, w2, preferred_element_type=jnp.float32)]
    pallas_call x4, Pallas kernels: 173 us -> 252 us  [the longest x2 149 us: gather_back(): pl.pallas_call(back_kernel, out_shape=[jax.ShapeDtypeStruct(pre.shape, bf...]
    dot_general x2 -> x0, local copies, waits for them, and re-layouts: 24.7 us -> none  [body(): d_w1 = jnp.einsum('tm,tf->mf', u_all, z, preferred_element_type=jnp.float32)]
    convert_element_type x4 -> x2, other arithmetic: 12 us -> 0.48 us  [body(): normed = norm_f32(x_f32).astype(jnp.bfloat16)]
    convert_element_type x2 -> x0, local copies, waits for them, and re-layouts: 9.49 us -> none  [body(): act = gelu_f32(pre.astype(jnp.float32)).astype(jnp.bfloat16)]
where the time goes in v4:
time: 631 us; the launch traced here: 628 us
  Pallas kernels  580 us (92%)
  local copies, waits for them, and re-layouts  21 us (3%)
  other arithmetic  12.6 us (2%)
  waiting for transfers between devices  6.74 us (1%)
  starting transfers between devices  6.48 us (1%)
    pallas_call x4, Pallas kernels, scatter(): pl.pallas_call(scatter_kernel, out_shape=outs, in_specs=[vmem] * 2 + [any...  328 us
    pallas_call x2, Pallas kernels, gather_back(): pl.pallas_call(back_kernel, out_shape=[jax.ShapeDtypeStruct(pre.shape, bf...  149 us
    pallas_call x2, Pallas kernels, gather_up(): pl.pallas_call(up_kernel, out_shape=[jax.ShapeDtypeStruct((RING, CORES) +...  103 us
  transfers between devices with their start and end apart: 1, of which 1 were waited for; matrix products, arithmetic and copies ran while one was open for 0% of the time, Pallas kernels for 0%

profile of v4, /device:TPU:1, one launch (start us, length us, event | category | flops | bytes accessed | tf_op | source)
XLA Modules:
  0.0 628.0 jit_solution(7972881027764828589)
XLA Ops:
  0.6 4.0 reshape.119
  4.6 0.2 copy.12
  4.8 0.0 copy-start.8
  4.9 0.2 pad_bitcast_fusion
  5.1 2.0 reshape.120
  7.1 6.5 %all-to-all-start = ((bf16[8,2,16,768]{3,2,1,0:T(8,128)(2,1)}), bf16[8,2,16,768]{3,2,1,0:T(8,128)(2,1)S(1)}, u32[]{:S(2)}, u32[]{:S(2)}) async-start(bf16[8,2,16,768]{3,2,1,0:T(8,128)(2,1)} %reshape.120), calls=%async_computation | async-start | bytes 786432 | tf_op jit(solution)/shard_map/all_to_all | solution.py:570
  13.6 0.0 copy-done.8
  13.6 0.3 fusion.9
  13.9 0.2 fusion.10.x_ref
  14.1 0.1 copy.13
  14.3 0.0 copy-start.6
  14.3 6.7 %all-to-all-done = bf16[8,2,16,768]{3,2,1,0:T(8,128)(2,1)S(1)} async-done(((bf16[8,2,16,768]{3,2,1,0:T(8,128)(2,1)}), bf16[8,2,16,768]{3,2,1,0:T(8,128)(2,1)S(1)}, u32[]{:S(2)}, u32[]{:S(2)}) %all-to-all-start) | async-done | bytes 393248 | tf_op jit(solution)/shard_map/all_to_all | solution.py:570
  21.1 0.0 copy-start.5
  21.1 0.0 copy-start.7
  21.1 53.1 %gather_up.2 = (bf16[4,2,2,128,2048]{4,3,2,1,0:T(8,128)(2,1)}, bf16[4,512,768]{2,1,0:T(8,128)(2,1)S(1)}, bf16[4,512,768]{2,1,0:T(8,128)(2,1)S(1)}, bf16[4,4,48,2048]{3,2,1,0:T(8,128)(2,1)S(1)}) custom-call(bf16[2,128,2048]{2,1,0:T(8,128)(2,1)S(1)} %fusion.10.x_ref, bf16[128,768]{1,0:T(8,128)(2,1)S(1)} %bitcast.56, ...), custom_call_target="tpu_custom_call" | custom-call | bytes 120000000 | tf_op jit(solution)/shard_map/gather_up/pallas_call | solution.py:234
  74.3 0.0 copy-start.2
  74.3 1.6 copy-done.2
  75.9 76.5 %scatter.2 = f32[256,2048]{1,0:T(8,128)S(1)} custom-call(bf16[4,2,256,768]{3,2,1,0:T(8,128)(2,1)S(1)} %bitcast.51, bf16[768,2048]{1,0:T(8,128)(2,1)S(1)} %bitcast.54), custom_call_target="tpu_custom_call" | custom-call | bytes 240000000 | tf_op jit(solution)/shard_map/scatter/pallas_call | solution.py:539
  152.4 0.4 fusion.4
  152.8 0.2 fusion.5
  153.1 50.3 %gather_up.3 = (bf16[4,2,2,128,2048]{4,3,2,1,0:T(8,128)(2,1)}, bf16[4,512,768]{2,1,0:T(8,128)(2,1)S(1)}, bf16[4,512,768]{2,1,0:T(8,128)(2,1)S(1)}, bf16[4,4,48,2048]{3,2,1,0:T(8,128)(2,1)S(1)}) custom-call(bf16[2,128,2048]{2,1,0:T(8,128)(2,1)S(1)} %bitcast.53, bf16[128,768]{1,0:T(8,128)(2,1)S(1)} %bitcast.58, bf16[48,2048]{1,0:T(8,128)(2,1)S(1)} %get-tuple-element.62.down_ref), custom_call_target="tpu_custom_call" | custom-call | bytes 120000000 | tf_op jit(solution)/shard_map/gather_up/pallas_call | solution.py:234
  203.4 1.7 copy-done.3
  205.0 76.5 %scatter.3 = f32[256,2048]{1,0:T(8,128)S(1)} custom-call(bf16[4,2,256,768]{3,2,1,0:T(8,128)(2,1)S(1)} %bitcast.52, bf16[768,2048]{1,0:T(8,128)(2,1)S(1)} %bitcast.55), custom_call_target="tpu_custom_call" | custom-call | bytes 240000000 | tf_op jit(solution)/shard_map/scatter/pallas_call | solution.py:539
  281.5 1.3 fusion.6
  282.8 73.8 %gather_back.2 = (bf16[4,512,768]{2,1,0:T(8,128)(2,1)}, bf16[4,4,128,768]{3,2,1,0:T(8,128)(2,1)}, f32[4,4,768,128]{3,2,1,0:T(8,128)}, f32[4,4,48,2048]{3,2,1,0:T(8,128)}) custom-call(bf16[2,128,2048]{2,1,0:T(8,128)(2,1)} %param.5, bf16[128,768]{1,0:T(8,128)(2,1)} %bitcast.59, bf16[48,2048]{1,0:T(8,128)(2,1)} %copy-done.6, ...), custom_call_target="tpu_custom_call" | custom-call | bytes 150000000 | tf_op jit(solution)/shard_map/gather_back/pallas_call | solution.py:307
  356.6 0.0 copy-start.11
  356.6 87.4 %scatter_grads.2 = (f32[256,2048]{1,0:T(8,128)}, f32[8,16,768]{2,1,0:T(8,128)}, f32[48,2048]{1,0:T(8,128)}) custom-call(bf16[4,2,256,768]{3,2,1,0:T(8,128)(2,1)} %bitcast.62, bf16[2048,768]{1,0:T(8,128)(2,1)} %bitcast.63, f32[4,4,768,128]{3,2,1,0:T(8,128)} %get-tuple-element.38.refs_0_, f32[4,4,48,2048]{3,2,1,0:T(8,128)} %get-tuple-element.39.refs_1_), custom_call_target="tpu_custom_call" | custom-call | bytes 240000000 | tf_op jit(solution)/shard_map/scatter_grads/pallas_call | solution.py:539
  444.0 0.0 copy-start.15
  444.0 0.0 copy-done.11
  444.0 2.0 fusion.7
  446.0 0.1 copy-done.13
  446.2 0.3 copy-done.15
  446.5 1.6 fusion.1
  448.1 1.5 stack.19
  449.6 75.0 %gather_back.3 = (bf16[4,512,768]{2,1,0:T(8,128)(2,1)}, bf16[4,4,128,768]{3,2,1,0:T(8,128)(2,1)}, f32[4,4,768,128]{3,2,1,0:T(8,128)}, f32[4,4,48,2048]{3,2,1,0:T(8,128)}) custom-call(bf16[2,128,2048]{2,1,0:T(8,128)(2,1)} %bitcast.60, bf16[128,768]{1,0:T(8,128)(2,1)} %bitcast.57, bf16[48,2048]{1,0:T(8,128)(2,1)} %copy-done.4, ...), custom_call_target="tpu_custom_call" | custom-call | bytes 150000000 | tf_op jit(solution)/shard_map/gather_back/pallas_call | solution.py:307
  524.6 0.0 copy-start.9
  524.6 87.5 %scatter_grads.3 = (f32[256,2048]{1,0:T(8,128)}, f32[8,16,768]{2,1,0:T(8,128)}, f32[48,2048]{1,0:T(8,128)}) custom-call(bf16[4,2,256,768]{3,2,1,0:T(8,128)(2,1)} %bitcast.64, bf16[2048,768]{1,0:T(8,128)(2,1)} %bitcast.65, f32[4,4,768,128]{3,2,1,0:T(8,128)} %get-tuple-element.45.refs_0_, f32[4,4,48,2048]{3,2,1,0:T(8,128)} %get-tuple-element.46.refs_1_), custom_call_target="tpu_custom_call" | custom-call | bytes 240000000 | tf_op jit(solution)/shard_map/scatter_grads/pallas_call | solution.py:539
  612.1 1.9 fusion.12
  614.1 0.1 slice_bitcast_fusion
  614.2 0.1 pad_maximum_fusion.1
  614.2 1.4 copy.15
  615.6 0.0 copy-done.17
  615.6 1.5 stack.18
  617.2 1.4 fusion.8
  618.6 2.5 copy.14
  621.1 3.6 reshape.134
  624.7 0.0 copy-done.12
  624.7 3.1 fusion.3
  (32 shorter events, 0.1 us)
Async XLA Ops:
  4.8 8.7 %copy-start.8 = (bf16[2,128,2048]{2,1,0:T(8,128)(2,1)S(1)}, bf16[2,128,2048]{2,1,0:T(8,128)(2,1)}, u32[]{:S(2)}) copy-start(bf16[2,128,2048]{2,1,0:T(8,128)(2,1)} %param.4) | copy-start | bytes 3145732
  7.1 7.1 %copy-start.20 = (bf16[2,44,2048]{2,0,1:T(2,128)(2,1)S(1)}, bf16[2,44,2048]{2,0,1:T(2,128)(2,1)}, u32[]{:S(2)}) copy-start(bf16[2,44,2048]{2,0,1:T(2,128)(2,1)} %param.7) | copy-start | bytes 1081348
  7.1 14.0 %all-to-all-start = ((bf16[8,2,16,768]{3,2,1,0:T(8,128)(2,1)}), bf16[8,2,16,768]{3,2,1,0:T(8,128)(2,1)S(1)}, u32[]{:S(2)}, u32[]{:S(2)}) async-start(bf16[8,2,16,768]{3,2,1,0:T(8,128)(2,1)} %reshape.120), calls=%async_computation | async-start | bytes 786432 | tf_op jit(solution)/shard_map/all_to_all | solution.py:570
  14.3 138.1 %copy-start.4 = (bf16[48,2048]{1,0:T(8,128)(2,1)}, bf16[48,2048]{1,0:T(8,128)(2,1)S(1)}, u32[]{:S(2)}) copy-start(bf16[48,2048]{1,0:T(8,128)(2,1)S(1)} %get-tuple-element.63.down_ref) | copy-start | bytes 589828
  14.3 138.8 %copy-start.6 = (bf16[48,2048]{1,0:T(8,128)(2,1)}, bf16[48,2048]{1,0:T(8,128)(2,1)S(1)}, u32[]{:S(2)}) copy-start(bf16[48,2048]{1,0:T(8,128)(2,1)S(1)} %get-tuple-element.62.down_ref) | copy-start | bytes 589828
  21.1 131.3 %copy-start.5 = (bf16[1,8,16,768]{3,2,0,1:T(8,128)(2,1)}, bf16[1,8,16,768]{3,2,0,1:T(8,128)(2,1)S(1)}, u32[]{:S(2)}) copy-start(bf16[1,8,16,768]{3,2,0,1:T(8,128)(2,1)S(1)} %get-tuple-element.65) | copy-start | bytes 589828
  21.1 132.0 %copy-start.7 = (bf16[1,8,16,768]{3,2,0,1:T(8,128)(2,1)}, bf16[1,8,16,768]{3,2,0,1:T(8,128)(2,1)S(1)}, u32[]{:S(2)}) copy-start(bf16[1,8,16,768]{3,2,0,1:T(8,128)(2,1)S(1)} %get-tuple-element.64) | copy-start | bytes 589828
  74.3 1.6 copy-start.2
  75.9 76.5 %copy-start = (bf16[4,512,768]{2,1,0:T(8,128)(2,1)}, bf16[4,512,768]{2,1,0:T(8,128)(2,1)S(1)}, u32[]{:S(2)}) copy-start(bf16[4,512,768]{2,1,0:T(8,128)(2,1)S(1)} %get-tuple-element.28.act_hbm) | copy-start | bytes 9437188
  152.8 128.7 %copy-start.10 = (bf16[256,2048]{1,0:T(8,128)(2,1)}, bf16[256,2048]{1,0:T(8,128)(2,1)S(1)}, u32[]{:S(2)}) copy-start(bf16[256,2048]{1,0:T(8,128)(2,1)S(1)} %get-tuple-element.61) | copy-start | bytes 3145732
  203.3 1.7 copy-start.3
  205.0 76.5 %copy-start.1 = (bf16[4,512,768]{2,1,0:T(8,128)(2,1)}, bf16[4,512,768]{2,1,0:T(8,128)(2,1)S(1)}, u32[]{:S(2)}) copy-start(bf16[4,512,768]{2,1,0:T(8,128)(2,1)S(1)} %get-tuple-element.30.act_hbm) | copy-start | bytes 9437188
  356.6 87.4 %copy-start.11 = (bf16[256,2048]{1,0:T(8,128)(2,1)S(1)}, bf16[256,2048]{1,0:T(8,128)(2,1)}, u32[]{:S(2)}) copy-start(bf16[256,2048]{1,0:T(8,128)(2,1)} %copy-done.10) | copy-start | bytes 3145732
  444.0 2.2 copy-start.13
  444.0 2.5 copy-start.15
  446.5 1.6 copy-start.19
  524.6 87.5 %copy-start.9 = (bf16[2,128,2048]{2,1,0:T(8,128)(2,1)S(1)}, bf16[2,128,2048]{2,1,0:T(8,128)(2,1)}, u32[]{:S(2)}) copy-start(bf16[2,128,2048]{2,1,0:T(8,128)(2,1)} %param.4) | copy-start | bytes 3145732
  612.1 2.0 copy-start.16
  612.1 2.0 copy-start.18
  614.1 1.6 copy-start.17
  614.1 3.0 copy-start.14
  621.1 3.6 copy-start.12

commit v5 on v4

--- a/solution.py
+++ b/solution.py
@@ -12,6 +12,9 @@
 PAD = 48
 RING = 4
 CORES = 2
+HALVES = (0, 1)
+VMEM = 62 * 2**20
+ROWS = (((1,), (1,)), ((), ()))
 MESH = pl.DeviceIdType.MESH
 
 
@@ -29,18 +32,21 @@
         self.z, self.y = local // RING, local % RING
         self.x, self.core = data // CORES, data % CORES
 
-    def dev(self, z=None, y=None, x=None, core=None):
-        z, y = self.z if z is None else z, self.y if y is None else y
-        x, core = self.x if x is None else x, self.core if core is None else core
+    def dev(self, **at):
+        z, y, x, core = (at.get(name, getattr(self, name)) for name in ("z", "y", "x", "core"))
         return (z * RING + y, x * CORES + core)
 
     def along(self, axis):
         me = getattr(self, axis)
-        right, left = lax.rem(me + 1, RING), lax.rem(me + RING - 1, RING)
+        left, right, _ = around(me)
         return me, self.dev(**{axis: right}), self.dev(**{axis: left})
 
     def sibling(self):
         return self.dev(core=1 - self.core)
+
+
+def around(me):
+    return [lax.rem(me + k, RING) for k in (3, 1, 2)]
 
 
 def greet(devices):
@@ -54,18 +60,19 @@
     def __init__(self, send_sems, recv_sems):
         self.send_sems, self.recv_sems, self.started = send_sems, recv_sems, []
 
-    def copy(self, slot, src, dst, device):
+    def copy(self, slot, src, dst, device, there=None):
+        there = slot if there is None else there
         c = pltpu.make_async_remote_copy(src_ref=src, dst_ref=dst, send_sem=self.send_sems.at[slot],
-                                         recv_sem=self.recv_sems.at[slot], device_id=device, device_id_type=MESH)
+                                         recv_sem=self.recv_sems.at[there], device_id=device, device_id_type=MESH)
         return c
 
-    def start(self, slot, src, dst, device):
-        c = self.copy(slot, src, dst, device)
+    def start(self, slot, src, dst, device, there=None):
+        c = self.copy(slot, src, dst, device, there)
         c.start()
         self.started.append(c)
 
     def arrived(self, slot, dst, device):
-        self.copy(slot, dst, dst, device).wait_recv()
+        self.copy(0, dst, dst, device, slot).wait_recv()
 
     def drain(self):
         for c in self.started:
@@ -76,11 +83,10 @@
     def __init__(self, sender, base, ring, own, block):
         self.s, self.base, self.own, self.block = sender, base, own, block
         self.me, self.right, self.left = ring
-        self.prev, self.next = lax.rem(self.me + 3, RING), lax.rem(self.me + 1, RING)
-        self.far = lax.rem(self.me + 2, RING)
-
-    def start(self):
-        for h in (0, 1):
+        self.prev, self.next, self.far = around(self.me)
+
+    def start(self, halves=HALVES):
+        for h in halves:
             self.s.start(self.base + h, self.own(h), self.block(self.me, h), self.right)
             self.s.start(self.base + 3 - h, self.own(1 - h), self.block(self.me, 1 - h), self.left)
 
@@ -110,6 +116,7 @@
             quarter = cols // 4
             sub = lambda part, h: (slice(None), pl.ds((2 * part + h) * quarter, quarter))
         block2 = (lambda i, h: dst.at[(i, slice(None)) + sub(0, h)], lambda i, h: dst.at[(slice(None), i) + sub(1, h)])
+        self.block2 = block2
         self.stage1 = (RingGather(sender, base, ring_y, lambda h: src.at[sub(0, h)], lambda i, h: dst.at[(p.z, i) + sub(0, h)]),
                        RingGather(sender, base + 6, ring_z, lambda h: src.at[sub(1, h)], lambda i, h: dst.at[(i, p.y) + sub(1, h)]))
         self.stage2 = (RingGather(sender, base + 12, ring_z, lambda h: block2[0](p.z, h), block2[0]),
@@ -120,8 +127,14 @@
             g.start()
 
     def second(self, keep=None):
+        self.early()
+        self.late(keep)
+
+    def early(self):
         for g in self.stage1:
             g.relay()
+
+    def late(self, keep=None):
         for g in self.stage1:
             g.near()
             g.finish()
@@ -165,161 +178,322 @@
     def take(self, k, i, h):
         self.s.arrived(6 + k, self.xs.at[i, 1 - self.p.core, h], self.sib)
 
-    def run(self, compute):
+    def run(self, early, compute):
         gx, me = self.gx, self.p.x
         self.first.start()
         gx.start()
-        for h in (0, 1):
+        for h in HALVES:
             self.give(h, me, h, self.x_ref.at[h])
         self.second.start()
         self.first.second()
-        self.second.second(self.keep)
+        self.second.early()
+        for h in HALVES:
+            self.take(h, me, h)
+        early(me, True)
         gx.relay()
         self.give(2, gx.prev, 0)
         self.give(3, gx.next, 1)
         self.first.relay()
+        self.second.late(self.keep)
         self.first.finish()
-        self.second.relay()
-        self.take(0, me, 0)
-        self.take(1, me, 1)
         compute(me, True)
         gx.near()
         self.give(4, gx.prev, 1)
         self.give(5, gx.next, 0)
         self.take(2, gx.prev, 0)
         self.take(4, gx.prev, 1)
+        self.second.relay()
+        early(gx.prev, False)
         compute(gx.prev, False)
         self.take(3, gx.next, 1)
         self.take(5, gx.next, 0)
         gx.finish()
         self.give(6, gx.far, 0)
         self.give(7, gx.far, 1)
+        early(gx.next, False)
         compute(gx.next, False)
         self.take(6, gx.far, 0)
         self.take(7, gx.far, 1)
+        early(gx.far, False, True)
         compute(gx.far, False)
         self.second.finish()
         self.s.drain()
 
 
-def up_kernel(x_ref, up_ref, down_ref, u_ref, pre_ref, act_ref, w2_ref, xs, w1, wide, send_sems, recv_sems, sems):
+def forward_kernel(x_ref, up_ref, down_ref, u_ref, slope_ref, act_ref, y_ref, xs, w1, wide, shards, w2, acts, passing,
+                   send_sems, recv_sems, sems):
+    p = Place()
+    me, right, left = p.along("x")
+    ring_y, ring_z = p.along("y"), p.along("z")
+    c, o, sib = p.core, 1 - p.core, p.sibling()
+    hidden, width = xs.shape[-1], w1.shape[-1]
+    rows, half_cols = down_ref.shape[0], down_ref.shape[1] // 2
+    own = acts.shape[2]
+    half = own // 2
+    mine = pl.ds(pl.multiple_of(me * rows, 16), rows)
+    w1[p.z, p.y] = up_ref[...]
+    shards[mine, :] = down_ref[...]
+    xs[me, c] = x_ref[...]
+    prev, next_, far = around(me)
+    greet([right, left, p.dev(x=prev, core=o), p.dev(x=next_, core=o), ring_y[1], ring_y[2], ring_z[1], ring_z[2], sib])
+    s = Sender(send_sems, recv_sems)
+    gx = RingGather(s, 0, (me, right, left), lambda h: x_ref.at[h], lambda i, h: xs.at[i, c, h])
+    gd = RingGather(s, 6, (me, right, left), lambda h: down_ref.at[:, pl.ds(h * half_cols, half_cols)],
+                    lambda i, h: shards.at[pl.ds(pl.multiple_of(i * rows, 16), rows), pl.ds(h * half_cols, half_cols)])
+    up = WeightGather(p, s, 12, up_ref, w1)
+    down = WeightGather(p, s, 36, shards, w2.at[c])
+    down_there = WeightGather(p, s, 36, shards, w2.at[o])
     saves = []
-    hidden, width = xs.shape[-1], w1.shape[-1]
-    ex = Exchange(x_ref, xs, up_ref, w1, down_ref, w2_ref, send_sems, recv_sems, sems.at[0])
-
-    def compute(i, _):
-        save = pltpu.make_async_copy(xs.at[i], u_ref.at[i], sems.at[1 + len(saves)])
-        save.start()
-        saves.append(save)
+
+    def give(k, i, h, src=None):
+        at = xs.at[i, c, h]
+        s.start(60 + k, at if src is None else src, at, sib)
+
+    def take(k, i, h):
+        s.arrived(60 + k, xs.at[i, o, h], sib)
+
+    def rings():
+        for part, ring in enumerate(down.stage2):
+            yield part, ring
+
+    def share(which):
+        for part, ring in rings():
+            for h in HALVES:
+                if which == "own":
+                    i, k = ring.me, 0
+                elif which == "relayed":
+                    i, k = (ring.prev, 1) if h == 0 else (ring.next, 2)
+                elif which == "near":
+                    i, k = (ring.next, 2) if h == 0 else (ring.prev, 1)
+                else:
+                    i, k = ring.far, 3
+                at = down.block2[part](i, h)
+                s.start(68 + part * 8 + k * 2 + h, at, at, sib)
+
+    def shared():
+        for part, ring in rings():
+            for k, i in enumerate((ring.me, ring.prev, ring.next, ring.far)):
+                for h in HALVES:
+                    s.arrived(68 + part * 8 + k * 2 + h, down_there.block2[part](i, h), sib)
+
+    def save(src, dst):
+        copy = pltpu.make_async_copy(src, dst, sems.at[len(saves)])
+        copy.start()
+        saves.append(copy)
+
+    def compute(i):
+        if saves:
+            saves[-1].wait()
+        save(xs.at[i], u_ref.at[i])
         wide[...] = jnp.dot(xs[i].reshape(wide.shape[0], hidden), w1[...].reshape(hidden, width),
                             preferred_element_type=jnp.float32)
 
         @pl.loop(0, wide.shape[0] // 32)
         def _(r):
             at = pl.ds(pl.multiple_of(r * 32, 32), 32)
-            pre = wide[at, :].astype(jnp.bfloat16)
-            pre_ref[i, at, :] = pre
-            act_ref[i, at, :] = gelu_f32(pre.astype(jnp.float32)).astype(jnp.bfloat16)
-
-    ex.run(compute)
-    for save in saves:
-        save.wait()
-
-
-def gather_up(x, up, down):
+            act, pull = jax.vjp(gelu_f32, wide[at, :].astype(jnp.bfloat16).astype(jnp.float32))
+            act_ref[i, at, :] = act.astype(jnp.bfloat16)
+            wide[at, :] = pull(jnp.ones_like(act))[0]
+
+        save(wide, slope_ref.at[i])
+
+    def rows_of(core, h=None):
+        if h is None:
+            return pl.ds(pl.multiple_of(core * own, own), own)
+        return pl.ds(core * own + h * half, half)
+
+    def send_act(k, i, to_right):
+        for core in HALVES:
+            s.start(k + core, act_ref.at[i, rows_of(core)], acts.at[me, c], p.dev(x=i, core=core),
+                    there=(85 if to_right else 87) + c)
+
+    gd.start()
+    up.start()
+    gd.relay()
+    gx.start()
+    for h in HALVES:
+        give(h, me, h, x_ref.at[h])
+    up.second()
+    gd.near()
+    gd.finish()
+    w2[c, p.z, p.y] = shards[...]
+    up.relay()
+    down.start()
+    gx.relay()
+    give(2, prev, 0)
+    give(3, next_, 1)
+    up.finish()
+    take(0, me, 0)
+    take(1, me, 1)
+    compute(me)
+    s.start(84, act_ref.at[me, rows_of(o)], acts.at[me, c], sib)
+    acts[me, c] = act_ref[me, rows_of(c), :]
+    down.early()
+    gx.near()
+    give(4, prev, 1)
+    give(5, next_, 0)
+    take(2, prev, 0)
+    take(4, prev, 1)
+    compute(prev)
+    send_act(85, prev, False)
+    down.late()
+    share("own")
+    take(3, next_, 1)
+    take(5, next_, 0)
+    compute(next_)
+    send_act(87, next_, True)
+    gx.finish()
+    give(6, far, 0)
+    give(7, far, 1)
+    take(6, far, 0)
+    take(7, far, 1)
+    compute(far)
+    for core in HALVES:
+        s.start(89 + core, act_ref.at[far, rows_of(core, 0)], passing.at[0, core], right)
+        s.start(91 + core, act_ref.at[far, rows_of(core, 1)], passing.at[1, core], left)
+    down.relay()
+    share("relayed")
+    for core in HALVES:
+        s.arrived(89 + core, passing.at[0, core], left)
+        s.start(93 + core, passing.at[0, core], acts.at[prev, c, pl.ds(0, half)], p.dev(x=next_, core=core), there=93 + c)
+        s.arrived(91 + core, passing.at[1, core], right)
+        s.start(95 + core, passing.at[1, core], acts.at[next_, c, pl.ds(half, half)], p.dev(x=prev, core=core), there=95 + c)
+    for ring in down.stage2:
+        ring.near()
+    share("near")
+    s.arrived(84, acts.at[me, o], sib)
+    for core in HALVES:
+        s.arrived(85 + core, acts.at[prev, core], left)
+        s.arrived(87 + core, acts.at[next_, core], right)
+        s.arrived(93 + core, acts.at[far, core, pl.ds(0, half)], left)
+        s.arrived(95 + core, acts.at[far, core, pl.ds(half, half)], right)
+    for ring in down.stage2:
+        ring.finish()
+    share("far")
+
+    def product(core, initial):
+        step = 512
+
+        @pl.loop(0, hidden // step)
+        def _(n):
+            at = pl.ds(pl.multiple_of(n * step, step), step)
+            total = None
+            for x in range(RING):
+                w = w2.at[core, :, :, pl.ds(x * rows, rows), at][...].reshape(width, step)
+                term = jnp.dot(acts[x, core], w, preferred_element_type=jnp.float32)
+                total = term if total is None else total + term
+            if initial:
+                y_ref[:, at] = total
+            else:
+                y_ref[:, at] += total
+
+    product(c, True)
+    shared()
+    product(o, False)
+    for copy in saves[::2] + saves[-1:]:
+        copy.wait()
+    s.drain()
+
+
+def forward(x, up, down):
     vmem, anywhere = pl.BlockSpec(memory_space=pltpu.VMEM), pl.BlockSpec(memory_space=pl.ANY)
     micro, rows, hidden = x.shape
-    block = CORES * micro * rows
-    bf16, dma = jnp.bfloat16, pltpu.SemaphoreType.DMA
+    own, width = micro * rows, up.shape[1]
+    block = CORES * own
+    bf16, f32, dma = jnp.bfloat16, jnp.float32, pltpu.SemaphoreType.DMA
+    shards = (RING * down.shape[0], hidden)
     return pl.pallas_call(
-        up_kernel,
-        out_shape=[jax.ShapeDtypeStruct((RING, CORES) + x.shape, bf16),
-                   jax.ShapeDtypeStruct((RING, block, up.shape[1]), bf16),
-                   jax.ShapeDtypeStruct((RING, block, up.shape[1]), bf16),
-                   jax.ShapeDtypeStruct((RING, RING) + down.shape, bf16)],
+        forward_kernel,
+        out_shape=[jax.ShapeDtypeStruct((RING, CORES) + x.shape, bf16), jax.ShapeDtypeStruct((RING, block, width), f32),
+                   jax.ShapeDtypeStruct((RING, block, width), bf16), jax.ShapeDtypeStruct((own, hidden), f32)],
         in_specs=[vmem] * 3,
-        out_specs=[anywhere, vmem, vmem, anywhere],
+        out_specs=[anywhere, anywhere, vmem, vmem],
         scratch_shapes=[pltpu.VMEM((RING, CORES) + x.shape, bf16), pltpu.VMEM((RING, RING) + up.shape, bf16),
-                        pltpu.VMEM((block, up.shape[1]), jnp.float32),
-                        dma((Exchange.SLOTS,)), dma((Exchange.SLOTS,)), dma((5,))],
-        compiler_params=pltpu.CompilerParams(collective_id=0, has_side_effects=True, vmem_limit_bytes=40 * 1024 * 1024),
-        cost_estimate=pl.CostEstimate(flops=0, bytes_accessed=120_000_000, transcendentals=0),
-        name="gather_up",
+                        pltpu.VMEM((block, width), f32), pltpu.VMEM(shards, bf16),
+                        pltpu.VMEM((CORES, RING, RING) + shards, bf16), pltpu.VMEM((RING, CORES, own, width), bf16),
+                        pltpu.VMEM((2, CORES, own // 2, width), bf16), dma((97,)), dma((97,)), dma((8,))],
+        compiler_params=pltpu.CompilerParams(collective_id=0, has_side_effects=True, vmem_limit_bytes=VMEM),
+        name="forward",
     )(x, up, down)
 
 
-def back_kernel(x_ref, up_ref, down_ref, u_hbm, pre_hbm, act_hbm, z_ref, w1_ref, g_up, g_down,
-                xs, w2, wide, us, pres, acts, acc_up, acc_down, send_sems, recv_sems, sems):
+def back_kernel(x_ref, up_ref, down_ref, u_hbm, slope_hbm, act_hbm, z_ref, w1_ref, g_up, g_down,
+                xs, w2, wide, us, slopes, acts, acc_up, acc_down, flipped, send_sems, recv_sems, sems):
     loads = [pltpu.make_async_copy(src, dst, sems.at[1 + k])
-             for k, (src, dst) in enumerate(((pre_hbm, pres), (act_hbm, acts), (u_hbm, us)))]
+             for k, (src, dst) in enumerate(((slope_hbm, slopes), (act_hbm, acts), (u_hbm, us)))]
     for load in loads:
         load.start()
     hidden, width = xs.shape[-1], z_ref.shape[-1]
     block = wide.shape[0]
     ex = Exchange(x_ref, xs, down_ref, w2, up_ref, w1_ref, send_sems, recv_sems, sems.at[0])
-    over_rows = (((0,), (0,)), ((), ()))
-
-    def compute(i, initial):
+    step = 512
+
+    def accumulate(acc, left, right, i, initial):
+        flipped[...] = left[i].T
+
+        @pl.loop(0, hidden // step)
+        def _(n):
+            at = pl.ds(pl.multiple_of(n * step, step), step)
+            term = jnp.dot(flipped[...], right.at[i, :, :, :, at][...].reshape(block, step), preferred_element_type=jnp.float32)
+            if initial:
+                acc[:, at] = term
+            else:
+                acc[:, at] += term
+
+    cols, rows = g_up.shape[3], g_down.shape[2]
+    copies = []
+
+    def store(acc_at, grad, base):
+        for k in range(RING * RING):
+            copy = pltpu.make_async_copy(acc_at(k), grad.at[k // RING, k % RING], sems.at[base + k])
+            copy.start()
+            copies.append(copy)
+
+    def early(i, initial, last=False):
         if initial:
             for load in loads:
                 load.wait()
-        wide[...] = lax.dot_general(xs[i].reshape(block, hidden), w2[...].reshape(width, hidden), (((1,), (1,)), ((), ())),
+        accumulate(acc_down, acts, xs, i, initial)
+        if last:
+            store(lambda k: acc_down.at[pl.ds(k * rows, rows)], g_down, 4)
+
+    def compute(i, initial):
+        wide[...] = lax.dot_general(xs[i].reshape(block, hidden), w2[...].reshape(width, hidden), ROWS,
                                     preferred_element_type=jnp.float32)
 
         @pl.loop(0, block // 32)
         def _(r):
             at = pl.ds(pl.multiple_of(r * 32, 32), 32)
-            pull = jax.vjp(gelu_f32, pres[i, at, :].astype(jnp.float32))[1]
-            z_ref[i, at, :] = pull(wide[at, :])[0].astype(jnp.bfloat16)
-
-        step = 512
-
-        @pl.loop(0, hidden // step)
-        def _(n):
-            at = pl.ds(pl.multiple_of(n * step, step), step)
-            d_down = lax.dot_general(acts[i], xs.at[i, :, :, :, at][...].reshape(block, step), over_rows,
-                                     preferred_element_type=jnp.float32)
-            d_up = lax.dot_general(z_ref[i], us.at[i, :, :, :, at][...].reshape(block, step), over_rows,
-                                   preferred_element_type=jnp.float32)
-            if initial:
-                acc_down[:, at] = d_down
-                acc_up[:, at] = d_up
-            else:
-                acc_down[:, at] += d_down
-                acc_up[:, at] += d_up
-
-    ex.run(compute)
-    cols, rows = g_up.shape[3], g_down.shape[2]
-    copies = []
-    for k in range(RING * RING):
-        copies.append(pltpu.make_async_copy(acc_up.at[:, pl.ds(k * cols, cols)], g_up.at[k // RING, k % RING], sems.at[4 + k]))
-        copies.append(pltpu.make_async_copy(acc_down.at[pl.ds(k * rows, rows)], g_down.at[k // RING, k % RING], sems.at[20 + k]))
-    for copy in copies:
-        copy.start()
+            z_ref[i, at, :] = (wide[at, :] * slopes[i, at, :]).astype(jnp.bfloat16)
+
+        accumulate(acc_up, z_ref, us, i, initial)
+
+    ex.run(early, compute)
+    store(lambda k: acc_up.at[:, pl.ds(k * cols, cols)], g_up, 20)
     for copy in copies:
         copy.wait()
 
 
-def gather_back(x, up, down, u_all, pre, act):
+def gather_back(x, up, down, u_all, slope, act):
     vmem, anywhere = pl.BlockSpec(memory_space=pltpu.VMEM), pl.BlockSpec(memory_space=pl.ANY)
     hidden, width = x.shape[-1], up.shape[1]
     bf16, f32, dma = jnp.bfloat16, jnp.float32, pltpu.SemaphoreType.DMA
     return pl.pallas_call(
         back_kernel,
-        out_shape=[jax.ShapeDtypeStruct(pre.shape, bf16),
+        out_shape=[jax.ShapeDtypeStruct(act.shape, bf16),
                    jax.ShapeDtypeStruct((RING, RING) + up.shape, bf16),
                    jax.ShapeDtypeStruct((RING, RING, width, hidden // (RING * RING)), f32),
                    jax.ShapeDtypeStruct((RING, RING) + down.shape, f32)],
         in_specs=[vmem] * 3 + [anywhere] * 3,
         out_specs=[vmem] + [anywhere] * 3,
         scratch_shapes=[pltpu.VMEM((RING, CORES) + x.shape, bf16), pltpu.VMEM((RING, RING) + down.shape, bf16),
-                        pltpu.VMEM(pre.shape[1:], f32), pltpu.VMEM(u_all.shape, bf16), pltpu.VMEM(pre.shape, bf16),
+                        pltpu.VMEM(slope.shape[1:], f32), pltpu.VMEM(u_all.shape, bf16), pltpu.VMEM(slope.shape, f32),
                         pltpu.VMEM(act.shape, bf16), pltpu.VMEM((width, hidden), f32), pltpu.VMEM((width, hidden), f32),
+                        pltpu.VMEM(act.shape[:0:-1], bf16),
                         dma((Exchange.SLOTS,)), dma((Exchange.SLOTS,)), dma((36,))],
-        compiler_params=pltpu.CompilerParams(collective_id=3, has_side_effects=True, vmem_limit_bytes=60 * 1024 * 1024),
-        cost_estimate=pl.CostEstimate(flops=0, bytes_accessed=150_000_000, transcendentals=0),
+        compiler_params=pltpu.CompilerParams(collective_id=3, has_side_effects=True, vmem_limit_bytes=VMEM),
         name="gather_back",
-    )(x, up, down, u_all, pre, act)
+    )(x, up, down, u_all, slope, act)
 
 
 def add_into(dst, *terms):
@@ -341,8 +515,7 @@
     def __init__(self, sender, base, ring, block, relayed, arriving):
         self.s, self.base, self.block, self.relayed, self.arriving = sender, base, block, relayed, arriving
         self.me, self.right, self.left = ring
-        self.prev, self.next = lax.rem(self.me + 3, RING), lax.rem(self.me + 1, RING)
-        self.far = lax.rem(self.me + 2, RING)
+        self.prev, self.next, self.far = around(self.me)
 
     def start(self):
         self.s.start(self.base, self.block(self.far, 0), self.relayed(0), self.right)
@@ -433,24 +606,18 @@
 
 
 def scatter_kernel(h_ref, w_ref, *refs):
-    backward = len(refs) > 8
     p = Place()
     me, right, left = p.along("x")
     sib, c, o = p.sibling(), p.core, 1 - p.core
-    if backward:
-        (g_up, g_down, y_ref, up_out, down_out, to_sib, from_sib, acc, relayed, arriving, send_sems, recv_sems,
-         up_sum, local_sems, *bufs) = refs
-        ring_y, ring_z = p.along("y"), p.along("z")
-        others = [p.dev(x=lax.rem(me + dx, RING), core=lax.rem(c + dc, CORES)) for dx in range(RING) for dc in range(CORES)][1:]
-        greet(others + [ring_y[1], ring_y[2], ring_z[1], ring_z[2]])
-        s = Sender(send_sems, recv_sems)
-        grads = GradScatter(p, s, 10, g_up, g_down, bufs, local_sems)
-        grads.start()
-        grads.load()
-    else:
-        y_ref, to_sib, from_sib, acc, relayed, arriving, send_sems, recv_sems = refs
-        greet([right, left, sib])
-        s = Sender(send_sems, recv_sems)
+    (g_up, g_down, y_ref, up_out, down_out, to_sib, from_sib, acc, relayed, arriving, send_sems, recv_sems,
+     up_sum, local_sems, *bufs) = refs
+    ring_y, ring_z = p.along("y"), p.along("z")
+    turns = [(lax.rem(me + dx, RING), lax.rem(c + dc, CORES)) for dx in range(RING) for dc in range(CORES)][1:]
+    greet([p.dev(x=x, core=core) for x, core in turns] + [ring_y[1], ring_y[2], ring_z[1], ring_z[2]])
+    s = Sender(send_sems, recv_sems)
+    grads = GradScatter(p, s, 10, g_up, g_down, bufs, local_sems)
+    grads.start()
+    grads.load()
     hidden = y_ref.shape[1]
     rows = y_ref.shape[0] // 2
     step = 512
@@ -462,11 +629,8 @@
         @pl.loop(0, hidden // step)
         def _(n):
             at = pl.ds(pl.multiple_of(n * step, step), step)
-            if backward:
-                dst[:, at] = lax.dot_general(h_ref[block, core], w_ref[at, :], (((1,), (1,)), ((), ())),
-                                             preferred_element_type=jnp.float32)
-            else:
-                dst[:, at] = jnp.dot(h_ref[block, core], w_ref[:, at], preferred_element_type=jnp.float32)
+            dst[:, at] = lax.dot_general(h_ref[block, core], w_ref[at, :], ROWS,
+                                         preferred_element_type=jnp.float32)
 
     def both(k, dx, dst):
         product(dx, o, to_sib.at[k])
@@ -489,67 +653,57 @@
     s.start(7, acc.at[2, first], arriving.at[1, first], left)
     both(3, 0, y_ref)
     joined(3, y_ref)
-    if backward:
-        grads.relay()
+    grads.relay()
     s.arrived(4, relayed.at[0], left)
     add_into(acc.at[1, first], relayed.at[0])
     s.start(8, acc.at[1, first], arriving.at[0, first], right)
     s.arrived(5, relayed.at[1], right)
     add_into(acc.at[2, second], relayed.at[1])
     s.start(9, acc.at[2, second], arriving.at[1, second], left)
-    if backward:
-        grads.second()
-        grads.finish(up_sum, down_out)
-        mine = me * CORES + c
-        piece = up_out.shape[1]
-        keep = pltpu.make_async_copy(up_sum.at[pl.ds(pl.multiple_of(mine * piece, piece), piece)], up_out.at[mine], local_sems.at[6])
-        keep.start()
-        turns = [(lax.rem(me + dx, RING), lax.rem(c + dc, CORES)) for dx in range(RING) for dc in range(CORES)][1:]
-        for k, (x, core) in enumerate(turns):
-            to = x * CORES + core
-            s.start(34 + k, up_sum.at[pl.ds(pl.multiple_of(to * piece, piece), piece)], up_out.at[mine], p.dev(x=x, core=core))
+    grads.second()
+    grads.finish(up_sum, down_out)
+    mine = me * CORES + c
+    piece = up_out.shape[1]
+    keep = pltpu.make_async_copy(up_sum.at[pl.ds(pl.multiple_of(mine * piece, piece), piece)], up_out.at[mine], local_sems.at[6])
+    keep.start()
+    for k, (x, core) in enumerate(turns):
+        to = x * CORES + core
+        s.start(34 + k, up_sum.at[pl.ds(pl.multiple_of(to * piece, piece), piece)], up_out.at[mine], p.dev(x=x, core=core))
     s.arrived(6, arriving.at[0, second], left)
     s.arrived(7, arriving.at[1, first], right)
     s.arrived(8, arriving.at[0, first], left)
     s.arrived(9, arriving.at[1, second], right)
     add_into(y_ref, arriving.at[0], arriving.at[1])
-    if backward:
-        for k in range(len(turns)):
-            dx, dc = divmod(k + 1, CORES)
-            x, core = lax.rem(me + RING - dx, RING), lax.rem(c + dc, CORES)
-            s.arrived(34 + k, up_out.at[x * CORES + core], p.dev(x=x, core=core))
-        keep.wait()
+    for k in range(len(turns)):
+        dx, dc = divmod(k + 1, CORES)
+        x, core = lax.rem(me + RING - dx, RING), lax.rem(c + dc, CORES)
+        s.arrived(34 + k, up_out.at[x * CORES + core], p.dev(x=x, core=core))
+    keep.wait()
     s.drain()
 
 
-def scatter(h, w, grads=None):
+def scatter(h, w, grads):
     rows, width = h.shape[2:]
-    hidden = w.shape[1] if grads is None else w.shape[0]
+    hidden = w.shape[0]
     vmem, anywhere = pl.BlockSpec(memory_space=pltpu.VMEM), pl.BlockSpec(memory_space=pl.ANY)
     f32 = jnp.float32
-    outs = [jax.ShapeDtypeStruct((rows, hidden), f32)]
-    slots = 10
-    extra = []
-    if grads is not None:
-        up_rows, down_rows = grads[0].shape[3], grads[1].shape[2]
-        n_data = RING * CORES
-        outs += [jax.ShapeDtypeStruct((n_data, up_rows // n_data, width), f32), jax.ShapeDtypeStruct((down_rows, hidden), f32)]
-        slots = 10 + GradScatter.SLOTS + n_data - 1
-        extra = [pltpu.VMEM((up_rows, width), f32), pltpu.SemaphoreType.DMA((7,))] + GradScatter.buffers(*grads)
+    up_rows, down_rows = grads[0].shape[3], grads[1].shape[2]
+    n_data = RING * CORES
+    slots = 10 + GradScatter.SLOTS + n_data - 1
     return pl.pallas_call(
         scatter_kernel,
-        out_shape=outs,
-        in_specs=[vmem] * 2 + [anywhere] * (0 if grads is None else 2),
-        out_specs=[vmem] * len(outs),
+        out_shape=[jax.ShapeDtypeStruct((rows, hidden), f32),
+                   jax.ShapeDtypeStruct((n_data, up_rows // n_data, width), f32), jax.ShapeDtypeStruct((down_rows, hidden), f32)],
+        in_specs=[vmem] * 2 + [anywhere] * 2,
+        out_specs=[vmem] * 3,
         scratch_shapes=[pltpu.VMEM((RING, rows, hidden), f32), pltpu.VMEM((RING, rows, hidden), f32),
                         pltpu.VMEM((3, rows, hidden), f32), pltpu.VMEM((2, rows // 2, hidden), f32),
                         pltpu.VMEM((2, rows, hidden), f32),
-                        pltpu.SemaphoreType.DMA((slots,)), pltpu.SemaphoreType.DMA((slots,))] + extra,
-        compiler_params=pltpu.CompilerParams(collective_id=1 if grads is None else 2, has_side_effects=True,
-                                             vmem_limit_bytes=(44 if grads is None else 62) * 1024 * 1024),
-        cost_estimate=pl.CostEstimate(flops=0, bytes_accessed=240_000_000, transcendentals=0),
-        name="scatter" if grads is None else "scatter_grads",
-    )(h, w, *(grads or ()))
+                        pltpu.SemaphoreType.DMA((slots,)), pltpu.SemaphoreType.DMA((slots,)),
+                        pltpu.VMEM((up_rows, width), f32), pltpu.SemaphoreType.DMA((7,))] + GradScatter.buffers(*grads),
+        compiler_params=pltpu.CompilerParams(collective_id=2, has_side_effects=True, vmem_limit_bytes=VMEM),
+        name="scatter_grads",
+    )(h, w, *grads)
 
 
 def solution(mesh):
@@ -582,9 +736,8 @@
         for layer in range(layers):
             x_f32 = x_cur.astype(jnp.float32)
             normed = norm_f32(x_f32).astype(jnp.bfloat16)
-            u_all, pre, act, w2 = gather_up(shaped(normed), up[layer], down[layer])
-            y, = scatter(blocks(act), w2.reshape(width, hidden))
-            saved.append((x_cur, u_all, pre, act))
+            u_all, slope, act, y = forward(shaped(normed), up[layer], down[layer])
+            saved.append((x_cur, u_all, slope, act))
             x_cur = (x_f32 + y).astype(jnp.bfloat16)
         x_final = x_cur
 
@@ -593,8 +746,8 @@
         grads_up = [None] * layers
         grads_down = [None] * layers
         for layer in reversed(range(layers)):
-            x_in, u_all, pre, act = saved[layer]
-            z, w1, g_up, g_down = gather_back(shaped(d_cur), up[layer], down[layer], u_all, pre, act)
+            x_in, u_all, slope, act = saved[layer]
+            z, w1, g_up, g_down = gather_back(shaped(d_cur), up[layer], down[layer], u_all, slope, act)
             v, grads_up[layer], g_down = scatter(blocks(z), w1.reshape(hidden, width), (g_up, g_down))
             grads_down[layer] = g_down[:down_rows]
             norm_pull = jax.vjp(norm_f32, x_in.astype(jnp.float32))[1]

time: 631 us -> 569 us (0.902)
  Pallas kernels: 580 us -> 515 us
    pallas_call x8 -> x6, Pallas kernels: 580 us -> 515 us  [the longest x2 216 us: forward(): pl.pallas_call(forward_kernel, out_shape=[jax.ShapeDtypeStruct((RING, COR...]
where the time goes in v5:
time: 569 us; the launch traced here: 565 us
  Pallas kernels  515 us (91%)
  local copies, waits for them, and re-layouts  19.3 us (3%)
  other arithmetic  18.3 us (3%)
  starting transfers between devices  6.48 us (1%)
    pallas_call x2, Pallas kernels, forward(): pl.pallas_call(forward_kernel, out_shape=[jax.ShapeDtypeStruct((RING, COR...  216 us
    pallas_call x2, Pallas kernels, scatter(): pl.pallas_call(scatter_kernel, out_shape=[jax.ShapeDtypeStruct((rows, hid...  174 us
    pallas_call x2, Pallas kernels, gather_back(): pl.pallas_call(back_kernel, out_shape=[jax.ShapeDtypeStruct(act.shape, bf...  125 us
  transfers between devices with their start and end apart: 1, of which 1 were waited for; matrix products, arithmetic and copies ran while one was open for 0% of the time, Pallas kernels for 0%

profile of v5, /device:TPU:1, one launch (start us, length us, event | category | flops | bytes accessed | tf_op | source)
XLA Modules:
  0.0 565.4 jit_solution(18053391544247204194)
XLA Ops:
  0.6 4.0 reshape.107
  4.6 0.2 copy.12
  4.8 0.0 copy-start
  4.9 0.2 pad_bitcast_fusion
  5.1 2.0 reshape.108
  7.1 6.5 %all-to-all-start = ((bf16[8,2,16,768]{3,2,1,0:T(8,128)(2,1)}), bf16[8,2,16,768]{3,2,1,0:T(8,128)(2,1)S(1)}, u32[]{:S(2)}, u32[]{:S(2)}) async-start(bf16[8,2,16,768]{3,2,1,0:T(8,128)(2,1)} %reshape.108), calls=%async_computation | async-start | bytes 786432 | tf_op jit(solution)/shard_map/all_to_all | solution.py:724
  13.6 0.0 copy-done
  13.6 0.3 fusion.9
  13.9 1.2 fusion.10.x_ref
  15.1 0.0 copy-done.10
  15.1 0.1 copy.13
  15.2 0.8 fusion.14
  16.0 5.1 all-to-all-done
  21.1 0.8 fusion.18
  21.8 109.3 %forward.2 = (bf16[4,2,2,128,2048]{4,3,2,1,0:T(8,128)(2,1)}, f32[4,512,768]{2,1,0:T(8,128)}, bf16[4,512,768]{2,1,0:T(8,128)(2,1)}, f32[256,2048]{1,0:T(8,128)}) custom-call(bf16[2,128,2048]{2,1,0:T(8,128)(2,1)} %fusion.10.x_ref, bf16[128,768]{1,0:T(8,128)(2,1)} %bitcast.54, bf16[48,2048]{1,0:T(8,128)(2,1)} %get-tuple-element.63.down_ref), custom_call_target="tpu_custom_call" | custom-call | tf_op jit(solution)/shard_map/forward/pallas_call | solution.py:405
  131.2 2.0 fusion.4
  133.2 1.0 copy-done.1
  134.2 1.2 fusion.5
  135.4 106.9 %forward.3 = (bf16[4,2,2,128,2048]{4,3,2,1,0:T(8,128)(2,1)}, f32[4,512,768]{2,1,0:T(8,128)}, bf16[4,512,768]{2,1,0:T(8,128)(2,1)}, f32[256,2048]{1,0:T(8,128)}) custom-call(bf16[2,128,2048]{2,1,0:T(8,128)(2,1)} %bitcast.49, bf16[128,768]{1,0:T(8,128)(2,1)} %bitcast.56, bf16[48,2048]{1,0:T(8,128)(2,1)} %get-tuple-element.62.down_ref), custom_call_target="tpu_custom_call" | custom-call | tf_op jit(solution)/shard_map/forward/pallas_call | solution.py:405
  242.3 3.1 fusion.6
  245.4 63.3 %gather_back.2 = (bf16[4,512,768]{2,1,0:T(8,128)(2,1)}, bf16[4,4,128,768]{3,2,1,0:T(8,128)(2,1)}, f32[4,4,768,128]{3,2,1,0:T(8,128)}, f32[4,4,48,2048]{3,2,1,0:T(8,128)}) custom-call(bf16[2,128,2048]{2,1,0:T(8,128)(2,1)} %param.5, bf16[128,768]{1,0:T(8,128)(2,1)} %bitcast.57, bf16[48,2048]{1,0:T(8,128)(2,1)} %get-tuple-element.62.down_ref, ...), custom_call_target="tpu_custom_call" | custom-call | tf_op jit(solution)/shard_map/gather_back/pallas_call | solution.py:481
  308.7 87.2 %scatter_grads.2 = (f32[256,2048]{1,0:T(8,128)}, f32[8,16,768]{2,1,0:T(8,128)}, f32[48,2048]{1,0:T(8,128)}) custom-call(bf16[4,2,256,768]{3,2,1,0:T(8,128)(2,1)} %bitcast.50, bf16[2048,768]{1,0:T(8,128)(2,1)} %bitcast.51, f32[4,4,768,128]{3,2,1,0:T(8,128)} %get-tuple-element.37.refs_0_, f32[4,4,48,2048]{3,2,1,0:T(8,128)} %get-tuple-element.38.refs_1_), custom_call_target="tpu_custom_call" | custom-call | tf_op jit(solution)/shard_map/scatter_grads/pallas_call | solution.py:693
  395.8 0.0 copy-start.2
  395.9 0.0 copy-start.4
  395.9 2.3 fusion.7
  398.2 0.0 copy-done.2
  398.2 0.5 copy-done.4
  398.7 2.9 fusion.1
  401.6 0.0 copy-done.9
  401.6 1.5 stack.19
  403.1 61.4 %gather_back.3 = (bf16[4,512,768]{2,1,0:T(8,128)(2,1)}, bf16[4,4,128,768]{3,2,1,0:T(8,128)(2,1)}, f32[4,4,768,128]{3,2,1,0:T(8,128)}, f32[4,4,48,2048]{3,2,1,0:T(8,128)}) custom-call(bf16[2,128,2048]{2,1,0:T(8,128)(2,1)} %bitcast.47, bf16[128,768]{1,0:T(8,128)(2,1)} %bitcast.55, bf16[48,2048]{1,0:T(8,128)(2,1)} %get-tuple-element.63.down_ref, ...), custom_call_target="tpu_custom_call" | custom-call | tf_op jit(solution)/shard_map/gather_back/pallas_call | solution.py:481
  464.5 87.1 %scatter_grads.3 = (f32[256,2048]{1,0:T(8,128)}, f32[8,16,768]{2,1,0:T(8,128)}, f32[48,2048]{1,0:T(8,128)}) custom-call(bf16[4,2,256,768]{3,2,1,0:T(8,128)(2,1)} %bitcast.52, bf16[2048,768]{1,0:T(8,128)(2,1)} %bitcast.53, f32[4,4,768,128]{3,2,1,0:T(8,128)} %get-tuple-element.45.refs_0_, f32[4,4,48,2048]{3,2,1,0:T(8,128)} %get-tuple-element.46.refs_1_), custom_call_target="tpu_custom_call" | custom-call | tf_op jit(solution)/shard_map/scatter_grads/pallas_call | solution.py:693
  551.6 0.0 copy-start.6
  551.6 0.0 copy-start.8
  551.6 1.9 fusion.12
  553.6 0.0 copy-done.6
  553.6 0.0 copy-done.8
  553.6 0.0 copy-start.7
  553.6 0.1 slice_bitcast_fusion
  553.7 0.0 copy-start.5
  553.7 0.1 pad_maximum_fusion.1
  553.8 1.4 copy.15
  555.2 0.0 copy-done.7
  555.2 0.5 stack.18
  555.7 0.2 fusion.8
  555.9 2.5 copy.14
  558.4 3.6 reshape.118
  562.0 3.1 fusion.3
  (10 shorter events, 0.1 us)
Async XLA Ops:
  4.8 8.7 %copy-start = (bf16[2,128,2048]{2,1,0:T(8,128)(2,1)S(1)}, bf16[2,128,2048]{2,1,0:T(8,128)(2,1)}, u32[]{:S(2)}) copy-start(bf16[2,128,2048]{2,1,0:T(8,128)(2,1)} %param.4) | copy-start | bytes 3145732
  7.1 8.0 %copy-start.10 = (bf16[2,44,2048]{2,0,1:T(2,128)(2,1)S(1)}, bf16[2,44,2048]{2,0,1:T(2,128)(2,1)}, u32[]{:S(2)}) copy-start(bf16[2,44,2048]{2,0,1:T(2,128)(2,1)} %param.7) | copy-start | bytes 1081348
  7.1 14.0 %all-to-all-start = ((bf16[8,2,16,768]{3,2,1,0:T(8,128)(2,1)}), bf16[8,2,16,768]{3,2,1,0:T(8,128)(2,1)S(1)}, u32[]{:S(2)}, u32[]{:S(2)}) async-start(bf16[8,2,16,768]{3,2,1,0:T(8,128)(2,1)} %reshape.108), calls=%async_computation | async-start | bytes 786432 | tf_op jit(solution)/shard_map/all_to_all | solution.py:724
  133.2 1.0 copy-start.1
  395.8 2.3 copy-start.2
  395.9 2.9 copy-start.4
  398.7 2.9 copy-start.9
  551.6 2.0 copy-start.6
  551.6 2.0 copy-start.8
  553.6 1.6 copy-start.7
  553.7 2.0 copy-start.5
  558.4 3.6 copy-start.3

commit v6 on v5

--- a/solution.py
+++ b/solution.py
@@ -1,4 +1,5 @@
 import functools
+import math
 
 import jax
 import jax.numpy as jnp
@@ -13,6 +14,13 @@
 RING = 4
 CORES = 2
 HALVES = (0, 1)
+SLAB = 2**15
+SLOTS = 101
+WIDE = 1024
+GRAD_SLOTS = 35
+NORM_ROWS = 16
+GELU_ROWS = 32
+STEP = 512
 VMEM = 62 * 2**20
 ROWS = (((1,), (1,)), ((), ()))
 MESH = pl.DeviceIdType.MESH
@@ -41,6 +49,10 @@
         left, right, _ = around(me)
         return me, self.dev(**{axis: right}), self.dev(**{axis: left})
 
+    def turns(self, sign=1):
+        return [(lax.rem(self.x + RING + sign * dx, RING), lax.rem(self.core + dc, CORES))
+                for dx in range(RING) for dc in range(CORES)][1:]
+
     def sibling(self):
         return self.dev(core=1 - self.core)
 
@@ -49,10 +61,16 @@
     return [lax.rem(me + k, RING) for k in (3, 1, 2)]
 
 
-def greet(devices):
+def slab(i, n):
+    return pl.ds(pl.multiple_of(i * n, n), n)
+
+
+def greet(devices, meanwhile=None):
     barrier = pltpu.get_barrier_semaphore()
     for device in devices:
         pl.semaphore_signal(barrier, inc=1, device_id=device, device_id_type=MESH)
+    if meanwhile is not None:
+        meanwhile()
     pl.semaphore_wait(barrier, len(devices))
 
 
@@ -106,15 +124,16 @@
 
 
 class WeightGather:
-    def __init__(self, p, sender, base, src, dst):
+    def __init__(self, p, sender, base, src, dst, cols=None):
         ring_y, ring_z = p.along("y"), p.along("z")
-        rows, cols = src.shape
-        if rows >= 64:
+        start, cols = (0, src.shape[1]) if cols is None else cols
+        rows = src.shape[0]
+        if start == 0 and cols < WIDE:
             quarter = rows // 4
             sub = lambda part, h: (pl.ds((2 * part + h) * quarter, quarter), slice(None))
         else:
             quarter = cols // 4
-            sub = lambda part, h: (slice(None), pl.ds((2 * part + h) * quarter, quarter))
+            sub = lambda part, h: (slice(None), pl.ds(start + (2 * part + h) * quarter, quarter))
         block2 = (lambda i, h: dst.at[(i, slice(None)) + sub(0, h)], lambda i, h: dst.at[(slice(None), i) + sub(1, h)])
         self.block2 = block2
         self.stage1 = (RingGather(sender, base, ring_y, lambda h: src.at[sub(0, h)], lambda i, h: dst.at[(p.z, i) + sub(0, h)]),
@@ -220,29 +239,42 @@
         self.s.drain()
 
 
-def forward_kernel(x_ref, up_ref, down_ref, u_ref, slope_ref, act_ref, y_ref, xs, w1, wide, shards, w2, acts, passing,
-                   send_sems, recv_sems, sems):
+def forward_kernel(first, tokens_ref, up_ref, down_ref, u_ref, slope_ref, act_ref, next_ref, *refs):
+    if first:
+        ups, *refs = refs
+        up_src = ups.at[0]
+    else:
+        up_src = up_ref
+    x_ref, y_ref, to_sib, from_sib, xs, w1, wide, shards, w2, acts, passing, send_sems, recv_sems, sems = refs
     p = Place()
     me, right, left = p.along("x")
     ring_y, ring_z = p.along("y"), p.along("z")
     c, o, sib = p.core, 1 - p.core, p.sibling()
     hidden, width = xs.shape[-1], w1.shape[-1]
     rows, half_cols = down_ref.shape[0], down_ref.shape[1] // 2
-    own = acts.shape[2]
+    own = y_ref.shape[0]
     half = own // 2
     mine = pl.ds(pl.multiple_of(me * rows, 16), rows)
-    w1[p.z, p.y] = up_ref[...]
-    shards[mine, :] = down_ref[...]
-    xs[me, c] = x_ref[...]
+
+    def prepare():
+        shards[mine, :] = down_ref[...]
+        for h in HALVES:
+            @pl.loop(0, half // NORM_ROWS)
+            def _(r):
+                at = slab(r, NORM_ROWS)
+                u = norm_f32(tokens_ref[h, at, :].astype(jnp.float32)).astype(jnp.bfloat16)
+                x_ref[h, at, :] = u
+                xs[me, c, h, at, :] = u
+
     prev, next_, far = around(me)
-    greet([right, left, p.dev(x=prev, core=o), p.dev(x=next_, core=o), ring_y[1], ring_y[2], ring_z[1], ring_z[2], sib])
+    over_data = [p.dev(x=x, core=core) for x, core in p.turns()] if first else [right, left, sib]
+    greet(over_data + [ring_y[1], ring_y[2], ring_z[1], ring_z[2]], prepare)
     s = Sender(send_sems, recv_sems)
     gx = RingGather(s, 0, (me, right, left), lambda h: x_ref.at[h], lambda i, h: xs.at[i, c, h])
     gd = RingGather(s, 6, (me, right, left), lambda h: down_ref.at[:, pl.ds(h * half_cols, half_cols)],
                     lambda i, h: shards.at[pl.ds(pl.multiple_of(i * rows, 16), rows), pl.ds(h * half_cols, half_cols)])
-    up = WeightGather(p, s, 12, up_ref, w1)
-    down = WeightGather(p, s, 36, shards, w2.at[c])
-    down_there = WeightGather(p, s, 36, shards, w2.at[o])
+    up = WeightGather(p, s, 12, up_src, w1)
+    downs = [WeightGather(p, s, base, shards, w2, (k * WIDE, WIDE)) for k, base in enumerate((36, 75))]
     saves = []
 
     def give(k, i, h, src=None):
@@ -251,30 +283,6 @@
 
     def take(k, i, h):
         s.arrived(60 + k, xs.at[i, o, h], sib)
-
-    def rings():
-        for part, ring in enumerate(down.stage2):
-            yield part, ring
-
-    def share(which):
-        for part, ring in rings():
-            for h in HALVES:
-                if which == "own":
-                    i, k = ring.me, 0
-                elif which == "relayed":
-                    i, k = (ring.prev, 1) if h == 0 else (ring.next, 2)
-                elif which == "near":
-                    i, k = (ring.next, 2) if h == 0 else (ring.prev, 1)
-                else:
-                    i, k = ring.far, 3
-                at = down.block2[part](i, h)
-                s.start(68 + part * 8 + k * 2 + h, at, at, sib)
-
-    def shared():
-        for part, ring in rings():
-            for k, i in enumerate((ring.me, ring.prev, ring.next, ring.far)):
-                for h in HALVES:
-                    s.arrived(68 + part * 8 + k * 2 + h, down_there.block2[part](i, h), sib)
 
     def save(src, dst):
         copy = pltpu.make_async_copy(src, dst, sems.at[len(saves)])
@@ -288,131 +296,163 @@
         wide[...] = jnp.dot(xs[i].reshape(wide.shape[0], hidden), w1[...].reshape(hidden, width),
                             preferred_element_type=jnp.float32)
 
-        @pl.loop(0, wide.shape[0] // 32)
+        @pl.loop(0, wide.shape[0] // GELU_ROWS)
         def _(r):
-            at = pl.ds(pl.multiple_of(r * 32, 32), 32)
+            at = slab(r, GELU_ROWS)
             act, pull = jax.vjp(gelu_f32, wide[at, :].astype(jnp.bfloat16).astype(jnp.float32))
             act_ref[i, at, :] = act.astype(jnp.bfloat16)
             wide[at, :] = pull(jnp.ones_like(act))[0]
 
         save(wide, slope_ref.at[i])
 
-    def rows_of(core, h=None):
-        if h is None:
-            return pl.ds(pl.multiple_of(core * own, own), own)
-        return pl.ds(core * own + h * half, half)
-
-    def send_act(k, i, to_right):
-        for core in HALVES:
-            s.start(k + core, act_ref.at[i, rows_of(core)], acts.at[me, c], p.dev(x=i, core=core),
-                    there=(85 if to_right else 87) + c)
+    def own_rows():
+        gx.start()
+        for h in HALVES:
+            give(h, me, h, x_ref.at[h])
+
+    def down_rows():
+        gd.near()
+        gd.finish()
+        w2[p.z, p.y] = shards[...]
+
+    def near_rows():
+        gx.relay()
+        give(2, prev, 0)
+        give(3, next_, 1)
 
     gd.start()
-    up.start()
-    gd.relay()
-    gx.start()
-    for h in HALVES:
-        give(h, me, h, x_ref.at[h])
-    up.second()
-    gd.near()
-    gd.finish()
-    w2[c, p.z, p.y] = shards[...]
-    up.relay()
-    down.start()
-    gx.relay()
-    give(2, prev, 0)
-    give(3, next_, 1)
+    if first:
+        rank = me * CORES + c
+        piece = up_ref.shape[2]
+        for k, (x, core) in enumerate(p.turns()):
+            s.start(SLOTS + k, up_ref.at[x * CORES + core], ups.at[:, slab(rank, piece)], p.dev(x=x, core=core))
+        ups[:, slab(rank, piece), :] = up_ref[rank]
+        gd.relay()
+        own_rows()
+        down_rows()
+        for down in downs:
+            down.start()
+        for k, (x, core) in enumerate(p.turns(-1)):
+            s.arrived(SLOTS + k, ups.at[:, slab(x * CORES + core, piece)], sib)
+        up.start()
+        w1[p.z, p.y] = up_src[...]
+        for down in downs:
+            down.early()
+        up.second()
+        near_rows()
+        up.relay()
+        downs[0].late()
+    else:
+        up.start()
+        w1[p.z, p.y] = up_src[...]
+        gd.relay()
+        own_rows()
+        up.second()
+        down_rows()
+        up.relay()
+        for down in downs:
+            down.start()
+        near_rows()
     up.finish()
     take(0, me, 0)
     take(1, me, 1)
     compute(me)
-    s.start(84, act_ref.at[me, rows_of(o)], acts.at[me, c], sib)
-    acts[me, c] = act_ref[me, rows_of(c), :]
-    down.early()
+    acts[me] = act_ref[me]
+    if not first:
+        for down in downs:
+            down.early()
     gx.near()
     give(4, prev, 1)
     give(5, next_, 0)
     take(2, prev, 0)
     take(4, prev, 1)
     compute(prev)
-    send_act(85, prev, False)
-    down.late()
-    share("own")
+    s.start(68, act_ref.at[prev], acts.at[me], left)
+    if not first:
+        downs[0].late()
     take(3, next_, 1)
     take(5, next_, 0)
     compute(next_)
-    send_act(87, next_, True)
+    s.start(69, act_ref.at[next_], acts.at[me], right)
     gx.finish()
     give(6, far, 0)
     give(7, far, 1)
     take(6, far, 0)
     take(7, far, 1)
     compute(far)
-    for core in HALVES:
-        s.start(89 + core, act_ref.at[far, rows_of(core, 0)], passing.at[0, core], right)
-        s.start(91 + core, act_ref.at[far, rows_of(core, 1)], passing.at[1, core], left)
-    down.relay()
-    share("relayed")
-    for core in HALVES:
-        s.arrived(89 + core, passing.at[0, core], left)
-        s.start(93 + core, passing.at[0, core], acts.at[prev, c, pl.ds(0, half)], p.dev(x=next_, core=core), there=93 + c)
-        s.arrived(91 + core, passing.at[1, core], right)
-        s.start(95 + core, passing.at[1, core], acts.at[next_, c, pl.ds(half, half)], p.dev(x=prev, core=core), there=95 + c)
-    for ring in down.stage2:
-        ring.near()
-    share("near")
-    s.arrived(84, acts.at[me, o], sib)
-    for core in HALVES:
-        s.arrived(85 + core, acts.at[prev, core], left)
-        s.arrived(87 + core, acts.at[next_, core], right)
-        s.arrived(93 + core, acts.at[far, core, pl.ds(0, half)], left)
-        s.arrived(95 + core, acts.at[far, core, pl.ds(half, half)], right)
-    for ring in down.stage2:
-        ring.finish()
-    share("far")
-
-    def product(core, initial):
-        step = 512
-
-        @pl.loop(0, hidden // step)
+    low, high = pl.ds(0, own), pl.ds(own, own)
+    s.start(70, act_ref.at[far, low], passing.at[0], right)
+    s.start(71, act_ref.at[far, high], passing.at[1], left)
+    downs[0].relay()
+    downs[1].late()
+    s.arrived(70, passing.at[0], left)
+    s.start(72, passing.at[0], acts.at[prev, low], right)
+    s.arrived(71, passing.at[1], right)
+    s.start(73, passing.at[1], acts.at[next_, high], left)
+    downs[1].relay()
+    s.arrived(68, acts.at[next_], right)
+    s.arrived(69, acts.at[prev], left)
+    s.arrived(72, acts.at[far, low], left)
+    s.arrived(73, acts.at[far, high], right)
+
+    def product(k, core, dst):
+        @pl.loop(0, WIDE // STEP)
         def _(n):
-            at = pl.ds(pl.multiple_of(n * step, step), step)
+            at = slab(k * (WIDE // STEP) + n, STEP)
             total = None
             for x in range(RING):
-                w = w2.at[core, :, :, pl.ds(x * rows, rows), at][...].reshape(width, step)
-                term = jnp.dot(acts[x, core], w, preferred_element_type=jnp.float32)
+                w = w2.at[:, :, pl.ds(x * rows, rows), at][...].reshape(width, STEP)
+                term = jnp.dot(acts[x, slab(core, own), :], w, preferred_element_type=jnp.float32)
                 total = term if total is None else total + term
-            if initial:
-                y_ref[:, at] = total
-            else:
-                y_ref[:, at] += total
-
-    product(c, True)
-    shared()
-    product(o, False)
+            dst[:, at] = total
+
+    for k, down in enumerate(downs):
+        down.finish()
+        product(k, o, to_sib)
+        at = pl.ds(k * WIDE, WIDE)
+        s.start(SLOTS - 1 - k, to_sib.at[:, at], from_sib.at[:, at], sib)
+        product(k, c, y_ref)
+    for k in HALVES:
+        at = pl.ds(k * WIDE, WIDE)
+        s.arrived(SLOTS - 1 - k, from_sib.at[:, at], sib)
+    for h in HALVES:
+        @pl.loop(0, half // NORM_ROWS)
+        def _(r):
+            at = slab(r, NORM_ROWS)
+            there = pl.ds(pl.multiple_of(h * half + r * NORM_ROWS, NORM_ROWS), NORM_ROWS)
+            y = y_ref[there, :] + from_sib[there, :]
+            next_ref[h, at, :] = (tokens_ref[h, at, :].astype(jnp.float32) + y).astype(jnp.bfloat16)
+
     for copy in saves[::2] + saves[-1:]:
         copy.wait()
     s.drain()
 
 
-def forward(x, up, down):
+def forward(x, up, down, first):
     vmem, anywhere = pl.BlockSpec(memory_space=pltpu.VMEM), pl.BlockSpec(memory_space=pl.ANY)
     micro, rows, hidden = x.shape
-    own, width = micro * rows, up.shape[1]
+    own, width = micro * rows, up.shape[-1]
     block = CORES * own
     bf16, f32, dma = jnp.bfloat16, jnp.float32, pltpu.SemaphoreType.DMA
     shards = (RING * down.shape[0], hidden)
+    n_data = RING * CORES
+    up_shape = (n_data * up.shape[2], width) if first else up.shape
+    outs = [jax.ShapeDtypeStruct((RING, CORES) + x.shape, bf16), jax.ShapeDtypeStruct((RING, block, width), f32),
+            jax.ShapeDtypeStruct((RING, block, width), bf16), jax.ShapeDtypeStruct(x.shape, bf16)]
+    if first:
+        outs.append(jax.ShapeDtypeStruct((up.shape[1],) + up_shape, bf16))
+    slots = SLOTS + n_data
     return pl.pallas_call(
-        forward_kernel,
-        out_shape=[jax.ShapeDtypeStruct((RING, CORES) + x.shape, bf16), jax.ShapeDtypeStruct((RING, block, width), f32),
-                   jax.ShapeDtypeStruct((RING, block, width), bf16), jax.ShapeDtypeStruct((own, hidden), f32)],
+        functools.partial(forward_kernel, first),
+        out_shape=outs,
         in_specs=[vmem] * 3,
-        out_specs=[anywhere, anywhere, vmem, vmem],
-        scratch_shapes=[pltpu.VMEM((RING, CORES) + x.shape, bf16), pltpu.VMEM((RING, RING) + up.shape, bf16),
+        out_specs=[anywhere] * 2 + [vmem] * (len(outs) - 2),
+        scratch_shapes=[pltpu.VMEM(x.shape, bf16), *[pltpu.VMEM((own, hidden), f32)] * 3,
+                        pltpu.VMEM((RING, CORES) + x.shape, bf16), pltpu.VMEM((RING, RING) + up_shape, bf16),
                         pltpu.VMEM((block, width), f32), pltpu.VMEM(shards, bf16),
-                        pltpu.VMEM((CORES, RING, RING) + shards, bf16), pltpu.VMEM((RING, CORES, own, width), bf16),
-                        pltpu.VMEM((2, CORES, own // 2, width), bf16), dma((97,)), dma((97,)), dma((8,))],
-        compiler_params=pltpu.CompilerParams(collective_id=0, has_side_effects=True, vmem_limit_bytes=VMEM),
+                        pltpu.VMEM((RING, RING) + shards, bf16), pltpu.VMEM((RING, block, width), bf16),
+                        pltpu.VMEM((2, own, width), bf16), dma((slots,)), dma((slots,)), dma((8,))],
+        compiler_params=pltpu.CompilerParams(collective_id=4 if first else 0, has_side_effects=True, vmem_limit_bytes=VMEM),
         name="forward",
     )(x, up, down)
 
@@ -426,15 +466,13 @@
     hidden, width = xs.shape[-1], z_ref.shape[-1]
     block = wide.shape[0]
     ex = Exchange(x_ref, xs, down_ref, w2, up_ref, w1_ref, send_sems, recv_sems, sems.at[0])
-    step = 512
-
     def accumulate(acc, left, right, i, initial):
         flipped[...] = left[i].T
 
-        @pl.loop(0, hidden // step)
+        @pl.loop(0, hidden // STEP)
         def _(n):
-            at = pl.ds(pl.multiple_of(n * step, step), step)
-            term = jnp.dot(flipped[...], right.at[i, :, :, :, at][...].reshape(block, step), preferred_element_type=jnp.float32)
+            at = slab(n, STEP)
+            term = jnp.dot(flipped[...], right.at[i, :, :, :, at][...].reshape(block, STEP), preferred_element_type=jnp.float32)
             if initial:
                 acc[:, at] = term
             else:
@@ -461,9 +499,9 @@
         wide[...] = lax.dot_general(xs[i].reshape(block, hidden), w2[...].reshape(width, hidden), ROWS,
                                     preferred_element_type=jnp.float32)
 
-        @pl.loop(0, block // 32)
+        @pl.loop(0, block // GELU_ROWS)
         def _(r):
-            at = pl.ds(pl.multiple_of(r * 32, 32), 32)
+            at = slab(r, GELU_ROWS)
             z_ref[i, at, :] = (wide[at, :] * slopes[i, at, :]).astype(jnp.bfloat16)
 
         accumulate(acc_up, z_ref, us, i, initial)
@@ -502,9 +540,11 @@
             add_into(dst.at[i], *(term.at[i] for term in terms))
         return
 
-    @pl.loop(0, dst.shape[0] // 8)
+    rows = math.gcd(dst.shape[0], max(8, SLAB // dst.shape[1]))
+
+    @pl.loop(0, dst.shape[0] // rows)
     def _(i):
-        at = pl.ds(pl.multiple_of(i * 8, 8), 8)
+        at = slab(i, rows)
         total = dst[at, :]
         for term in terms:
             total = total + term[at, :]
@@ -539,8 +579,6 @@
 
 
 class GradScatter:
-    SLOTS = 24
-
     def __init__(self, p, sender, base, up, down, bufs, sems):
         self.p, self.sems, self.up, self.down = p, sems, up, down
         (self.u_rel, self.u_arr, self.u_loc, self.u_own, self.u_rel2, self.u_arr2,
@@ -609,10 +647,10 @@
     p = Place()
     me, right, left = p.along("x")
     sib, c, o = p.sibling(), p.core, 1 - p.core
-    (g_up, g_down, y_ref, up_out, down_out, to_sib, from_sib, acc, relayed, arriving, send_sems, recv_sems,
+    (g_up, g_down, x_ref, c_ref, dx_ref, up_out, down_out, y_ref, to_sib, from_sib, acc, relayed, arriving, send_sems, recv_sems,
      up_sum, local_sems, *bufs) = refs
     ring_y, ring_z = p.along("y"), p.along("z")
-    turns = [(lax.rem(me + dx, RING), lax.rem(c + dc, CORES)) for dx in range(RING) for dc in range(CORES)][1:]
+    turns = p.turns()
     greet([p.dev(x=x, core=core) for x, core in turns] + [ring_y[1], ring_y[2], ring_z[1], ring_z[2]])
     s = Sender(send_sems, recv_sems)
     grads = GradScatter(p, s, 10, g_up, g_down, bufs, local_sems)
@@ -620,16 +658,15 @@
     grads.load()
     hidden = y_ref.shape[1]
     rows = y_ref.shape[0] // 2
-    step = 512
     first, second = pl.ds(0, rows), pl.ds(rows, rows)
 
-    def product(dx, core, dst):
+    def product(dx, core, dst, part=slice(None)):
         block = lax.rem(me + dx, RING)
 
-        @pl.loop(0, hidden // step)
+        @pl.loop(0, hidden // STEP)
         def _(n):
-            at = pl.ds(pl.multiple_of(n * step, step), step)
-            dst[:, at] = lax.dot_general(h_ref[block, core], w_ref[at, :], ROWS,
+            at = slab(n, STEP)
+            dst[:, at] = lax.dot_general(h_ref[block, core, part, :], w_ref[at, :], ROWS,
                                          preferred_element_type=jnp.float32)
 
     def both(k, dx, dst):
@@ -641,10 +678,15 @@
         s.arrived(k, from_sib.at[k], sib)
         add_into(dst, from_sib.at[k])
 
-    both(0, 2, acc.at[0])
-    joined(0, acc.at[0])
-    s.start(4, acc.at[0, first], relayed.at[0], right)
-    s.start(5, acc.at[0, second], relayed.at[1], left)
+    parts = ((first, right, 0), (second, left, GRAD_SLOTS - 1))
+    for h, (part, _, slot) in enumerate(parts):
+        product(2, o, to_sib.at[0, part], part)
+        s.start(slot, to_sib.at[0, part], from_sib.at[0, part], sib)
+    for h, (part, to, slot) in enumerate(parts):
+        product(2, c, acc.at[0, part], part)
+        s.arrived(slot, from_sib.at[0, part], sib)
+        add_into(acc.at[0, part], from_sib.at[0, part])
+        s.start(4 + h, acc.at[0, part], relayed.at[h], to)
     both(1, 1, acc.at[1])
     both(2, 3, acc.at[2])
     joined(1, acc.at[1])
@@ -664,46 +706,52 @@
     grads.finish(up_sum, down_out)
     mine = me * CORES + c
     piece = up_out.shape[1]
-    keep = pltpu.make_async_copy(up_sum.at[pl.ds(pl.multiple_of(mine * piece, piece), piece)], up_out.at[mine], local_sems.at[6])
+    keep = pltpu.make_async_copy(up_sum.at[slab(mine, piece)], up_out.at[mine], local_sems.at[6])
     keep.start()
     for k, (x, core) in enumerate(turns):
         to = x * CORES + core
-        s.start(34 + k, up_sum.at[pl.ds(pl.multiple_of(to * piece, piece), piece)], up_out.at[mine], p.dev(x=x, core=core))
+        s.start(GRAD_SLOTS + k, up_sum.at[slab(to, piece)], up_out.at[mine], p.dev(x=x, core=core))
     s.arrived(6, arriving.at[0, second], left)
     s.arrived(7, arriving.at[1, first], right)
     s.arrived(8, arriving.at[0, first], left)
     s.arrived(9, arriving.at[1, second], right)
-    add_into(y_ref, arriving.at[0], arriving.at[1])
-    for k in range(len(turns)):
-        dx, dc = divmod(k + 1, CORES)
-        x, core = lax.rem(me + RING - dx, RING), lax.rem(c + dc, CORES)
-        s.arrived(34 + k, up_out.at[x * CORES + core], p.dev(x=x, core=core))
+    for h in HALVES:
+        @pl.loop(0, rows // NORM_ROWS)
+        def _(r):
+            at = slab(r, NORM_ROWS)
+            there = pl.ds(pl.multiple_of(h * rows + r * NORM_ROWS, NORM_ROWS), NORM_ROWS)
+            v = y_ref[there, :] + arriving[0, there, :] + arriving[1, there, :]
+            pull = jax.vjp(norm_f32, x_ref[h, at, :].astype(jnp.float32))[1]
+            dx_ref[h, at, :] = (c_ref[h, at, :].astype(jnp.float32) + pull(v)[0]).astype(jnp.bfloat16)
+
+    for k, (x, core) in enumerate(p.turns(-1)):
+        s.arrived(GRAD_SLOTS + k, up_out.at[x * CORES + core], p.dev(x=x, core=core))
     keep.wait()
     s.drain()
 
 
-def scatter(h, w, grads):
+def scatter(h, w, grads, x, c):
     rows, width = h.shape[2:]
     hidden = w.shape[0]
     vmem, anywhere = pl.BlockSpec(memory_space=pltpu.VMEM), pl.BlockSpec(memory_space=pl.ANY)
     f32 = jnp.float32
     up_rows, down_rows = grads[0].shape[3], grads[1].shape[2]
     n_data = RING * CORES
-    slots = 10 + GradScatter.SLOTS + n_data - 1
+    slots = GRAD_SLOTS + n_data
     return pl.pallas_call(
         scatter_kernel,
-        out_shape=[jax.ShapeDtypeStruct((rows, hidden), f32),
+        out_shape=[jax.ShapeDtypeStruct(x.shape, x.dtype),
                    jax.ShapeDtypeStruct((n_data, up_rows // n_data, width), f32), jax.ShapeDtypeStruct((down_rows, hidden), f32)],
-        in_specs=[vmem] * 2 + [anywhere] * 2,
+        in_specs=[vmem] * 2 + [anywhere] * 2 + [vmem] * 2,
         out_specs=[vmem] * 3,
-        scratch_shapes=[pltpu.VMEM((RING, rows, hidden), f32), pltpu.VMEM((RING, rows, hidden), f32),
+        scratch_shapes=[pltpu.VMEM((rows, hidden), f32), pltpu.VMEM((RING, rows, hidden), f32), pltpu.VMEM((RING, rows, hidden), f32),
                         pltpu.VMEM((3, rows, hidden), f32), pltpu.VMEM((2, rows // 2, hidden), f32),
                         pltpu.VMEM((2, rows, hidden), f32),
                         pltpu.SemaphoreType.DMA((slots,)), pltpu.SemaphoreType.DMA((slots,)),
                         pltpu.VMEM((up_rows, width), f32), pltpu.SemaphoreType.DMA((7,))] + GradScatter.buffers(*grads),
         compiler_params=pltpu.CompilerParams(collective_id=2, has_side_effects=True, vmem_limit_bytes=VMEM),
         name="scatter_grads",
-    )(h, w, *grads)
+    )(h, w, *grads, x, c)
 
 
 def solution(mesh):
@@ -721,41 +769,32 @@
         up = w_up.reshape(layers, up_rows, n_local, n_data, down_rows)
         up = jnp.pad(up, ((0, 0),) * 4 + ((0, pad),))
         up = up.transpose(3, 0, 1, 2, 4).reshape(n_data, layers, up_rows, width)
-        up = lax.all_to_all(up, "data", 0, 0)
-        up = up.transpose(1, 0, 2, 3).reshape(layers, n_data * up_rows, width)
         down = jnp.pad(w_down, ((0, 0), (0, pad), (0, 0)))
-
-        def shaped(x):
-            return x.reshape(micro, rows, hidden)
 
         def blocks(h):
             return h.reshape(RING, CORES, own, width)
 
-        x_cur = tokens.reshape(own, hidden)
+        x_cur = tokens
         saved = []
         for layer in range(layers):
-            x_f32 = x_cur.astype(jnp.float32)
-            normed = norm_f32(x_f32).astype(jnp.bfloat16)
-            u_all, slope, act, y = forward(shaped(normed), up[layer], down[layer])
+            u_all, slope, act, x_next, *ups = forward(x_cur, up if layer == 0 else up[layer], down[layer], layer == 0)
+            if ups:
+                up, = ups
             saved.append((x_cur, u_all, slope, act))
-            x_cur = (x_f32 + y).astype(jnp.bfloat16)
+            x_cur = x_next
         x_final = x_cur
 
-        d_cur = cotangent.reshape(own, hidden)
-        d_cur, x_final = lax.optimization_barrier((d_cur, x_final))
+        d_cur, x_final = lax.optimization_barrier((cotangent, x_final))
         grads_up = [None] * layers
         grads_down = [None] * layers
         for layer in reversed(range(layers)):
             x_in, u_all, slope, act = saved[layer]
-            z, w1, g_up, g_down = gather_back(shaped(d_cur), up[layer], down[layer], u_all, slope, act)
-            v, grads_up[layer], g_down = scatter(blocks(z), w1.reshape(hidden, width), (g_up, g_down))
+            z, w1, g_up, g_down = gather_back(d_cur, up[layer], down[layer], u_all, slope, act)
+            d_cur, grads_up[layer], g_down = scatter(blocks(z), w1.reshape(hidden, width), (g_up, g_down), x_in, d_cur)
             grads_down[layer] = g_down[:down_rows]
-            norm_pull = jax.vjp(norm_f32, x_in.astype(jnp.float32))[1]
-            d_cur = (d_cur.astype(jnp.float32) + norm_pull(v)[0]).astype(jnp.bfloat16)
         g_up = jnp.stack(grads_up, 1).reshape(n_data, layers, up_rows, n_local, PAD)[..., :down_rows]
         g_up = g_up.transpose(1, 2, 3, 0, 4).reshape(layers, up_rows, ffn)
-        shape = (micro, rows, hidden)
-        return x_final.reshape(shape), d_cur.reshape(shape), g_up, jnp.stack(grads_down)
+        return x_final, d_cur, g_up, jnp.stack(grads_down)
 
     spec = P(None, ALL_AXES, None)
     return jax.shard_map(body, mesh=mesh, in_specs=(spec,) * 4, out_specs=(spec,) * 4, check_vma=False)

time: 569 us -> 553 us (0.972)
  other arithmetic: 18.3 us -> 0.22 us
  starting transfers between devices: 6.48 us -> 0 us
  Pallas kernels: 515 us -> 521 us
    convert_element_type x5 -> x0, other arithmetic: 11.6 us -> none  [the longest x2 6.02 us: body(): d_cur = (d_cur.astype(jnp.float32) + norm_pull(v)[0]).astype(jnp.bfloat16)]
    reduce_sum x4 -> x0, other arithmetic: 6.51 us -> none  [the longest x2 4.24 us: norm_f32(): x_f32 * lax.rsqrt(jnp.mean(x_f32 * x_f32, axis=-1, keepdims=True) + NORM_...]
    all_to_all x1 -> x0, starting transfers between devices: 6.48 us -> none  [body(): up = lax.all_to_all(up, 'data', 0, 0)]
  transfers between devices with their start and end apart: 1 -> 0, of which waited for: 1 -> 0; matrix products, arithmetic and copies ran while one was open for 0% -> 0% of each run, Pallas kernels for 0% -> 0%
where the time goes in v6:
time: 553 us; the launch traced here: 545 us
  Pallas kernels  521 us (94%)
  local copies, waits for them, and re-layouts  21.7 us (4%)
    pallas_call x2, Pallas kernels, forward(): pl.pallas_call(functools.partial(forward_kernel, first), out_shape=outs,...  222 us
    pallas_call x2, Pallas kernels, scatter(): pl.pallas_call(scatter_kernel, out_shape=[jax.ShapeDtypeStruct(x.shape, x...  173 us
    pallas_call x2, Pallas kernels, gather_back(): pl.pallas_call(back_kernel, out_shape=[jax.ShapeDtypeStruct(act.shape, bf...  126 us

profile of v6, /device:TPU:1, one launch (start us, length us, event | category | flops | bytes accessed | tf_op | source)
XLA Modules:
  0.0 544.5 jit_solution(3710731687388321790)
XLA Ops:
  0.6 1.1 copy.9
  1.7 0.8 fusion.2
  2.5 4.0 reshape.34
  6.5 0.2 copy.8
  6.7 0.2 pad_bitcast_fusion
  7.0 2.0 reshape.35.up_ref
  8.9 120.4 %forward.2 = (bf16[4,2,2,128,2048]{4,3,2,1,0:T(8,128)(2,1)}, f32[4,512,768]{2,1,0:T(8,128)}, bf16[4,512,768]{2,1,0:T(8,128)(2,1)}, bf16[2,128,2048]{2,1,0:T(8,128)(2,1)}, bf16[2,128,768]{2,1,0:T(8,128)(2,1)}) custom-call(bf16[2,128,2048]{2,1,0:T(8,128)(2,1)} %refs_2_.1, bf16[8,2,16,768]{3,2,1,0:T(8,128)(2,1)} %reshape.35.up_ref, ...), custom_call_target="tpu_custom_call" | custom-call | tf_op jit(solution)/shard_map/forward/pallas_call | solution.py:445
  129.3 1.8 slice_bitcast_fusion.2
  131.1 101.8 %forward.3 = (bf16[4,2,2,128,2048]{4,3,2,1,0:T(8,128)(2,1)}, f32[4,512,768]{2,1,0:T(8,128)}, bf16[4,512,768]{2,1,0:T(8,128)(2,1)}, bf16[2,128,2048]{2,1,0:T(8,128)(2,1)}) custom-call(bf16[2,128,2048]{2,1,0:T(8,128)(2,1)} %get-tuple-element.29.tokens_ref.refs_2_, bf16[128,768]{1,0:T(8,128)(2,1)} %get-tuple-element.59.up_ref, ...), custom_call_target="tpu_custom_call" | custom-call | tf_op jit(solution)/shard_map/forward/pallas_call | solution.py:445
  232.9 62.9 %gather_back.2 = (bf16[4,512,768]{2,1,0:T(8,128)(2,1)}, bf16[4,4,128,768]{3,2,1,0:T(8,128)(2,1)}, f32[4,4,768,128]{3,2,1,0:T(8,128)}, f32[4,4,48,2048]{3,2,1,0:T(8,128)}) custom-call(bf16[2,128,2048]{2,1,0:T(8,128)(2,1)} %refs_3_, bf16[128,768]{1,0:T(8,128)(2,1)} %get-tuple-element.59.up_ref, bf16[48,2048]{1,0:T(8,128)(2,1)} %get-tuple-element.60.down_ref, ...), custom_call_target="tpu_custom_call" | custom-call | tf_op jit(solution)/shard_map/gather_back/pallas_call | solution.py:519
  295.8 86.4 %scatter_grads.2 = (bf16[2,128,2048]{2,1,0:T(8,128)(2,1)}, f32[8,16,768]{2,1,0:T(8,128)}, f32[48,2048]{1,0:T(8,128)}) custom-call(bf16[4,2,256,768]{3,2,1,0:T(8,128)(2,1)} %bitcast.24, bf16[2048,768]{1,0:T(8,128)(2,1)} %bitcast.25, f32[4,4,768,128]{3,2,1,0:T(8,128)} %get-tuple-element.39.refs_0_, f32[4,4,48,2048]{3,2,1,0:T(8,128)} %get-tuple-element.40.refs_1_, ...), custom_call_target="tpu_custom_call" | custom-call | tf_op jit(solution)/shard_map/scatter_grads/pallas_call | solution.py:741
  382.2 1.5 stack.19
  383.8 63.4 %gather_back.3 = (bf16[4,512,768]{2,1,0:T(8,128)(2,1)}, bf16[4,4,128,768]{3,2,1,0:T(8,128)(2,1)}, f32[4,4,768,128]{3,2,1,0:T(8,128)}, f32[4,4,48,2048]{3,2,1,0:T(8,128)}) custom-call(bf16[2,128,2048]{2,1,0:T(8,128)(2,1)} %get-tuple-element.41.x_ref.refs_3_, bf16[128,768]{1,0:T(8,128)(2,1)} %get-tuple-element.58.up_ref, ...), custom_call_target="tpu_custom_call" | custom-call | tf_op jit(solution)/shard_map/gather_back/pallas_call | solution.py:519
  447.2 0.0 copy-start.1
  447.2 86.5 %scatter_grads.3 = (bf16[2,128,2048]{2,1,0:T(8,128)(2,1)}, f32[8,16,768]{2,1,0:T(8,128)}, f32[48,2048]{1,0:T(8,128)}) custom-call(bf16[4,2,256,768]{3,2,1,0:T(8,128)(2,1)} %bitcast.26, bf16[2048,768]{1,0:T(8,128)(2,1)} %bitcast.27, f32[4,4,768,128]{3,2,1,0:T(8,128)} %get-tuple-element.47.refs_0_, f32[4,4,48,2048]{3,2,1,0:T(8,128)} %get-tuple-element.48.refs_1_, ...), custom_call_target="tpu_custom_call" | custom-call | tf_op jit(solution)/shard_map/scatter_grads/pallas_call | solution.py:741
  533.7 0.0 copy-start.2
  533.7 0.0 copy-done.1
  533.7 1.1 slice_bitcast_fusion
  534.8 0.1 pad_maximum_fusion.1
  534.9 1.4 copy.11
  536.3 0.0 copy-done.2
  536.3 0.5 stack.18
  536.8 0.2 fusion
  537.0 0.0 copy-start
  537.0 1.2 copy.10
  538.2 2.6 reshape.40
  540.8 0.0 copy-done
  540.8 1.0 copy.14
  541.8 2.3 copy.15
Async XLA Ops:
  447.2 86.5 %copy-start.1 = (f32[48,2048]{1,0:T(8,128)S(1)}, f32[48,2048]{1,0:T(8,128)}, u32[]{:S(2)}) copy-start(f32[48,2048]{1,0:T(8,128)} %get-tuple-element.53) | copy-start | bytes 1179652
  533.7 2.6 copy-start.2
  537.0 3.8 copy-start

commit v7 on v6

--- a/solution.py
+++ b/solution.py
@@ -21,6 +21,7 @@
 NORM_ROWS = 16
 GELU_ROWS = 32
 STEP = 512
+TILE = 256
 VMEM = 62 * 2**20
 ROWS = (((1,), (1,)), ((), ()))
 MESH = pl.DeviceIdType.MESH
@@ -293,8 +294,12 @@
         if saves:
             saves[-1].wait()
         save(xs.at[i], u_ref.at[i])
-        wide[...] = jnp.dot(xs[i].reshape(wide.shape[0], hidden), w1[...].reshape(hidden, width),
-                            preferred_element_type=jnp.float32)
+
+        @pl.loop(0, width // TILE)
+        def _(n):
+            at = slab(n, TILE)
+            wide[:, at] = jnp.dot(xs[i].reshape(wide.shape[0], hidden), w1.at[:, :, :, at][...].reshape(hidden, TILE),
+                                  preferred_element_type=jnp.float32)
 
         @pl.loop(0, wide.shape[0] // GELU_ROWS)
         def _(r):
@@ -320,47 +325,33 @@
         give(2, prev, 0)
         give(3, next_, 1)
 
-    gd.start()
     if first:
         rank = me * CORES + c
         piece = up_ref.shape[2]
         for k, (x, core) in enumerate(p.turns()):
             s.start(SLOTS + k, up_ref.at[x * CORES + core], ups.at[:, slab(rank, piece)], p.dev(x=x, core=core))
         ups[:, slab(rank, piece), :] = up_ref[rank]
-        gd.relay()
-        own_rows()
-        down_rows()
-        for down in downs:
-            down.start()
+    gd.start()
+    if first:
         for k, (x, core) in enumerate(p.turns(-1)):
             s.arrived(SLOTS + k, ups.at[:, slab(x * CORES + core, piece)], sib)
-        up.start()
-        w1[p.z, p.y] = up_src[...]
-        for down in downs:
-            down.early()
-        up.second()
-        near_rows()
-        up.relay()
-        downs[0].late()
-    else:
-        up.start()
-        w1[p.z, p.y] = up_src[...]
-        gd.relay()
-        own_rows()
-        up.second()
-        down_rows()
-        up.relay()
-        for down in downs:
-            down.start()
-        near_rows()
+    up.start()
+    w1[p.z, p.y] = up_src[...]
+    gd.relay()
+    own_rows()
+    up.second()
+    down_rows()
+    up.relay()
+    for down in downs:
+        down.start()
+    near_rows()
     up.finish()
     take(0, me, 0)
     take(1, me, 1)
     compute(me)
     acts[me] = act_ref[me]
-    if not first:
-        for down in downs:
-            down.early()
+    for down in downs:
+        down.early()
     gx.near()
     give(4, prev, 1)
     give(5, next_, 0)
@@ -368,8 +359,7 @@
     take(4, prev, 1)
     compute(prev)
     s.start(68, act_ref.at[prev], acts.at[me], left)
-    if not first:
-        downs[0].late()
+    downs[0].late()
     take(3, next_, 1)
     take(5, next_, 0)
     compute(next_)
@@ -396,12 +386,12 @@
     s.arrived(73, acts.at[far, high], right)
 
     def product(k, core, dst):
-        @pl.loop(0, WIDE // STEP)
+        @pl.loop(0, WIDE // TILE)
         def _(n):
-            at = slab(k * (WIDE // STEP) + n, STEP)
+            at = slab(k * (WIDE // TILE) + n, TILE)
             total = None
             for x in range(RING):
-                w = w2.at[:, :, pl.ds(x * rows, rows), at][...].reshape(width, STEP)
+                w = w2.at[:, :, pl.ds(x * rows, rows), at][...].reshape(width, TILE)
                 term = jnp.dot(acts[x, slab(core, own), :], w, preferred_element_type=jnp.float32)
                 total = term if total is None else total + term
             dst[:, at] = total

time: 553 us -> 545 us (0.986)
  Pallas kernels: 521 us -> 513 us
    pallas_call x2, Pallas kernels: 222 us -> 214 us  [forward(): pl.pallas_call(functools.partial(forward_kernel, first), out_shape=outs,...]
where the time goes in v7:
time: 545 us; the launch traced here: 536 us
  Pallas kernels  513 us (94%)
  local copies, waits for them, and re-layouts  21.7 us (4%)
    pallas_call x2, Pallas kernels, forward(): pl.pallas_call(functools.partial(forward_kernel, first), out_shape=outs,...  214 us
    pallas_call x2, Pallas kernels, scatter(): pl.pallas_call(scatter_kernel, out_shape=[jax.ShapeDtypeStruct(x.shape, x...  173 us
    pallas_call x2, Pallas kernels, gather_back(): pl.pallas_call(back_kernel, out_shape=[jax.ShapeDtypeStruct(act.shape, bf...  126 us

profile of v7, /device:TPU:1, one launch (start us, length us, event | category | flops | bytes accessed | tf_op | source)
XLA Modules:
  0.0 536.2 jit_solution(7001978440147570546)
XLA Ops:
  0.6 1.1 copy.9
  1.7 0.8 fusion.2
  2.5 4.0 reshape.34
  6.5 0.2 copy.8
  6.7 0.2 pad_bitcast_fusion
  7.0 2.0 reshape.35.up_ref
  8.9 113.1 %forward.2 = (bf16[4,2,2,128,2048]{4,3,2,1,0:T(8,128)(2,1)}, f32[4,512,768]{2,1,0:T(8,128)}, bf16[4,512,768]{2,1,0:T(8,128)(2,1)}, bf16[2,128,2048]{2,1,0:T(8,128)(2,1)}, bf16[2,128,768]{2,1,0:T(8,128)(2,1)}) custom-call(bf16[2,128,2048]{2,1,0:T(8,128)(2,1)} %refs_2_.1, bf16[8,2,16,768]{3,2,1,0:T(8,128)(2,1)} %reshape.35.up_ref, ...), custom_call_target="tpu_custom_call" | custom-call | tf_op jit(solution)/shard_map/forward/pallas_call | solution.py:435
  122.1 1.8 slice_bitcast_fusion.2
  123.8 101.4 %forward.3 = (bf16[4,2,2,128,2048]{4,3,2,1,0:T(8,128)(2,1)}, f32[4,512,768]{2,1,0:T(8,128)}, bf16[4,512,768]{2,1,0:T(8,128)(2,1)}, bf16[2,128,2048]{2,1,0:T(8,128)(2,1)}) custom-call(bf16[2,128,2048]{2,1,0:T(8,128)(2,1)} %get-tuple-element.29.tokens_ref.refs_2_, bf16[128,768]{1,0:T(8,128)(2,1)} %get-tuple-element.59.up_ref, ...), custom_call_target="tpu_custom_call" | custom-call | tf_op jit(solution)/shard_map/forward/pallas_call | solution.py:435
  225.2 62.4 %gather_back.2 = (bf16[4,512,768]{2,1,0:T(8,128)(2,1)}, bf16[4,4,128,768]{3,2,1,0:T(8,128)(2,1)}, f32[4,4,768,128]{3,2,1,0:T(8,128)}, f32[4,4,48,2048]{3,2,1,0:T(8,128)}) custom-call(bf16[2,128,2048]{2,1,0:T(8,128)(2,1)} %refs_3_, bf16[128,768]{1,0:T(8,128)(2,1)} %get-tuple-element.59.up_ref, bf16[48,2048]{1,0:T(8,128)(2,1)} %get-tuple-element.60.down_ref, ...), custom_call_target="tpu_custom_call" | custom-call | tf_op jit(solution)/shard_map/gather_back/pallas_call | solution.py:509
  287.6 86.4 %scatter_grads.2 = (bf16[2,128,2048]{2,1,0:T(8,128)(2,1)}, f32[8,16,768]{2,1,0:T(8,128)}, f32[48,2048]{1,0:T(8,128)}) custom-call(bf16[4,2,256,768]{3,2,1,0:T(8,128)(2,1)} %bitcast.24, bf16[2048,768]{1,0:T(8,128)(2,1)} %bitcast.25, f32[4,4,768,128]{3,2,1,0:T(8,128)} %get-tuple-element.39.refs_0_, f32[4,4,48,2048]{3,2,1,0:T(8,128)} %get-tuple-element.40.refs_1_, ...), custom_call_target="tpu_custom_call" | custom-call | tf_op jit(solution)/shard_map/scatter_grads/pallas_call | solution.py:731
  374.1 1.5 stack.19
  375.6 63.4 %gather_back.3 = (bf16[4,512,768]{2,1,0:T(8,128)(2,1)}, bf16[4,4,128,768]{3,2,1,0:T(8,128)(2,1)}, f32[4,4,768,128]{3,2,1,0:T(8,128)}, f32[4,4,48,2048]{3,2,1,0:T(8,128)}) custom-call(bf16[2,128,2048]{2,1,0:T(8,128)(2,1)} %get-tuple-element.41.x_ref.refs_3_, bf16[128,768]{1,0:T(8,128)(2,1)} %get-tuple-element.58.up_ref, ...), custom_call_target="tpu_custom_call" | custom-call | tf_op jit(solution)/shard_map/gather_back/pallas_call | solution.py:509
  439.1 0.0 copy-start.1
  439.1 86.5 %scatter_grads.3 = (bf16[2,128,2048]{2,1,0:T(8,128)(2,1)}, f32[8,16,768]{2,1,0:T(8,128)}, f32[48,2048]{1,0:T(8,128)}) custom-call(bf16[4,2,256,768]{3,2,1,0:T(8,128)(2,1)} %bitcast.26, bf16[2048,768]{1,0:T(8,128)(2,1)} %bitcast.27, f32[4,4,768,128]{3,2,1,0:T(8,128)} %get-tuple-element.47.refs_0_, f32[4,4,48,2048]{3,2,1,0:T(8,128)} %get-tuple-element.48.refs_1_, ...), custom_call_target="tpu_custom_call" | custom-call | tf_op jit(solution)/shard_map/scatter_grads/pallas_call | solution.py:731
  525.6 0.0 copy-start.2
  525.6 0.0 copy-done.1
  525.6 1.1 slice_bitcast_fusion
  526.7 0.1 pad_maximum_fusion.1
  526.8 1.4 copy.11
  528.2 0.0 copy-done.2
  528.2 0.5 stack.18
  528.7 0.2 fusion
  528.9 0.0 copy-start
  528.9 1.2 copy.10
  530.1 2.6 reshape.40
  532.7 0.0 copy-done
  532.7 1.0 copy.14
  533.6 2.3 copy.15
Async XLA Ops:
  439.1 86.5 %copy-start.1 = (f32[48,2048]{1,0:T(8,128)S(1)}, f32[48,2048]{1,0:T(8,128)}, u32[]{:S(2)}) copy-start(f32[48,2048]{1,0:T(8,128)} %get-tuple-element.53) | copy-start | bytes 1179652
  525.6 2.6 copy-start.2
  528.9 3.8 copy-start
